TPU v7x, 512 devices: a 8x2x16 block of a 8x8x16 slice. The times are simulated.
512 devices in a mesh: groups: 2 (over y), fsdp: 16 (over z), mp: 8 (over x), sub: 2 (over core).
Axes of the slice: x: 8, y: 2, z: 16, core: 2. Of those that a mesh axis runs over, the one named last changes fastest.
The devices are a block of a 8x8x16 slice.
Arguments:
- hidden: bfloat16 [512, 36864], P(('groups', 'fsdp', 'sub'), 'mp'), parts along dimension 0, may hold values from -6 to 6
- residual: bfloat16 [512, 4608], P(('groups', 'fsdp', 'sub')), parts along dimension 0, may hold values from -6 to 6
- down_packed: int32 [4608, 4608], P('mp', 'fsdp'), may hold values from -2147483648 to 2147483646
- down_scale: bfloat16 [288, 4608], P('mp', 'fsdp'), may hold values from 0.00049972534 to 0.0019989014
- post_gain: float32 [4608], replicated, may hold values from 0.1 to 1.9
- final_gain: float32 [4608], replicated, may hold values from 0.1 to 1.9
- embed_packed: int32 [131072, 576], P(('fsdp', 'mp', 'sub')), may hold values from -2147483648 to 2147483646
- embed_scale: bfloat16 [131072, 36], P(('fsdp', 'mp', 'sub')), may hold values from 0.0059814453 to 0.029907227
- targets: int32 [512], P(('groups', 'fsdp', 'sub')), parts along dimension 0, may hold values from 0 to 131071
- loss_mask: int32 [512], P(('groups', 'fsdp', 'sub')), parts along dimension 0, may hold values 0 or 1
Outputs:
- token_loss: float32 [512], P(('groups', 'fsdp', 'sub')), parts along dimension 0
- mean_loss: float32 [2], P('groups'), parts along dimension 0
There are 2 independent parts, one for each index of `groups`. A program takes and returns all parts, laid end to end along the dimension named above; an argument that names none is the same for every part. Nothing has to cross between parts.
Inputs may be any that keep to these rules, and one draw needn't show every extreme that they name: `down_packed`: bits 4 k to 4 k + 3 of the word in row r hold the signed code of row 8 r + k of the down projection, k = 0..7. `embed_packed`: bits 4 k to 4 k + 3 of the word in column j hold the signed code of column k * 576 + j of the embedding, k = 0..7.
All inputs are finite; a program needn't handle non-finite values. No bound on the sum of `loss_mask` on one device may be relied on, other than what follows from the above.
Results may differ from a plain program's by a relative error of at most 0.00097.
Values may be sent and summed in bfloat16 or wider, within the bound.
No kernel may reach another device: no remote copies, remote signals or barrier semaphores. Data moves between devices by JAX's collectives and lax.ppermute only.
A program may use at most 64 MiB of HBM per device.

v0:
```python
import functools

import jax
import jax.numpy as jnp
from jax import lax
from jax.sharding import PartitionSpec as P

EPS = 1e-06
CAP = 30.0


def copy_for_each(value, axis):
    peers = lax.axis_size(axis)
    return lax.all_to_all(
        jnp.broadcast_to(value[None], (peers, *value.shape)), axis, 0, 0, tiled=True
    )


def over_copies(value, axis):
    everything = copy_for_each(value, axis)
    return jnp.sum(everything, axis=0)


def joined_along(pieces, dim):
    pieces = jnp.moveaxis(pieces, 0, dim)
    lengths = pieces.shape
    return pieces.reshape(*lengths[:dim], lengths[dim] * lengths[dim + 1], *lengths[dim + 2 :])


def gathered_copies(value, axis, dim):
    pieces = copy_for_each(value, axis)
    return joined_along(pieces, dim)


def by_axis(value, axes):
    return functools.reduce(lax.psum, axes, value)


def in_one(arrays, axis):
    ends = [0]
    for a in arrays:
        ends.append(ends[-1] + a.size)
    running = over_copies(jnp.concatenate([a.ravel() for a in arrays]), axis)
    return tuple((running[b:e].reshape(a.shape) for a, b, e in zip(arrays, ends, ends[1:])))


def signed_planes(words):
    shifts = (28 - 4 * jnp.arange(8, dtype=jnp.int32))[None, :, None]
    lifted = jnp.left_shift(words[:, None, :], shifts)
    return jnp.right_shift(lifted, 28)


def dequant_down(words, scales):
    cols = words.shape[1]
    codes = signed_planes(words).astype(jnp.bfloat16)
    grouped = codes.reshape(scales.shape[0], -1, cols) * scales[:, None, :]
    return grouped.reshape(-1, cols)


def dequant_embed(words, scales):
    rows = words.shape[0]
    codes = signed_planes(words).astype(jnp.bfloat16)
    grouped = codes.reshape(rows, scales.shape[1], -1) * scales[:, :, None]
    return grouped.reshape(rows, -1)


def normalize_rows(ffn, residual, post_gain, final_gain):
    ffn = over_copies(ffn, "mp")
    normed = ffn * lax.rsqrt(jnp.mean(ffn * ffn, axis=-1, keepdims=True) + EPS) * post_gain
    stream = residual.astype(jnp.float32) + normed
    return (
        stream * lax.rsqrt(jnp.mean(stream * stream, axis=-1, keepdims=True) + EPS) * final_gain
    ).astype(jnp.bfloat16)


def on_device(
    hidden,
    residual,
    down_packed,
    down_scale,
    post_gain,
    final_gain,
    embed_packed,
    embed_scale,
    targets,
    loss_mask,
):
    tok_rows = hidden.shape[0]
    local_weight = dequant_down(down_packed, down_scale)
    partial_cols = jnp.dot(
        gathered_copies(hidden, "fsdp", 0), local_weight, preferred_element_type=jnp.float32
    )
    ffn = lax.all_to_all(partial_cols, "fsdp", split_axis=0, concat_axis=1, tiled=True)
    states = normalize_rows(ffn, residual, post_gain, final_gain)
    all_states, all_targets = (
        lax.all_gather(states, ("fsdp", "sub"), axis=0, tiled=True),
        lax.all_gather(targets, ("fsdp", "sub"), axis=0, tiled=True),
    )
    embed = dequant_embed(embed_packed, embed_scale)
    logits = lax.dot_general(
        all_states, embed, (((1,), (1,)), ((), ())), preferred_element_type=jnp.float32
    )
    capped = CAP * jnp.tanh(logits / CAP)
    vocab_rows = embed.shape[0]
    first_id = lax.axis_index(("fsdp", "mp", "sub")) * vocab_rows
    ids = first_id + jnp.arange(vocab_rows, dtype=jnp.int32)
    hits = all_targets[:, None] == ids[None, :]
    exp_sums, target_logits = (
        by_axis(jnp.sum(jnp.exp(capped), axis=1), ("fsdp", "mp", "sub")),
        by_axis(jnp.sum(jnp.where(hits, capped, 0.0), axis=1), ("fsdp", "mp", "sub")),
    )
    own_start = lax.axis_index(("fsdp", "sub")) * tok_rows
    own_sums = lax.dynamic_slice_in_dim(exp_sums, own_start, tok_rows, 0)
    own_targets = lax.dynamic_slice_in_dim(target_logits, own_start, tok_rows, 0)
    weights = loss_mask.astype(jnp.float32)
    token_loss = weights * (jnp.log(own_sums) - own_targets)
    loss_sum, count = in_one((jnp.sum(token_loss), jnp.sum(weights)), ("fsdp", "sub"))
    mean_loss = (loss_sum / jnp.maximum(count, 1.0)).reshape(1)
    return (token_loss, mean_loss)


def solution(mesh):
    return jax.shard_map(
        on_device,
        mesh=mesh,
        in_specs=(
            P(("groups", "fsdp", "sub"), "mp"),
            P(("groups", "fsdp", "sub"), None),
            P("mp", "fsdp"),
            P("mp", "fsdp"),
            P(),
            P(),
            P(("fsdp", "mp", "sub"), None),
            P(("fsdp", "mp", "sub"), None),
            P(("groups", "fsdp", "sub")),
            P(("groups", "fsdp", "sub")),
        ),
        out_specs=(P(("groups", "fsdp", "sub")), P("groups")),
        check_vma=False,
    )
```

profile of v0, /device:TPU:65, one launch (start us, length us, event | category | flops | bytes accessed | tf_op | source)
XLA Modules:
  0.0 327.0 jit_solution(13066960805130694038)
XLA Ops:
  7.2 2.0 broadcast_in_dim.11
  9.2 44.2 %all-to-all-start = ((bf16[16,8,4608]{2,1,0:T(8,128)(2,1)}), bf16[16,8,4608]{2,1,0:T(8,128)(2,1)}, u32[]{:S(2)}, u32[]{:S(2)}) async-start(bf16[16,8,4608]{2,1,0:T(8,128)(2,1)} %broadcast_in_dim.11), calls=%async_computation | async-start | bytes 2359296 | tf_op jit(solution)/shard_map/all_to_all | solution.py:14
  53.4 0.1 all-gather.2.cloned.1.call-start
  53.5 0.1 shift_left.52
  53.6 1.4 copy.25
  55.0 0.0 copy-start.4
  55.0 0.5 shift_left.49
  55.5 0.3 copy-done.4
  55.8 1.3 fusion.5
  57.1 47.4 %all-to-all-done = bf16[16,8,4608]{2,1,0:T(8,128)(2,1)} async-done(((bf16[16,8,4608]{2,1,0:T(8,128)(2,1)}), bf16[16,8,4608]{2,1,0:T(8,128)(2,1)}, u32[]{:S(2)}, u32[]{:S(2)}) %all-to-all-start) | async-done | bytes 1179680 | tf_op jit(solution)/shard_map/all_to_all | solution.py:14
  104.5 3.1 fusion.10
  107.6 0.0 copy-start.1
  107.6 0.0 copy-start.2
  107.6 0.0 copy-start
  107.6 0.0 copy-start.3
  107.6 1.1 copy.27
  108.7 24.8 %all_to_all.32 = f32[16,8,288]{2,1,0:T(8,128)S(1)} all-to-all(f32[16,8,288]{2,1,0:T(8,128)S(1)} %bitcast.38), channel_id=1, replica_groups=mesh['groups'=2,'fsdp'=16,'mp'=8,'sub'=2] {'fsdp'}, dimensions={0} | all-to-all | bytes 294912 | tf_op jit(solution)/shard_map/all_to_all | solution.py:93
  133.6 0.1 broadcast_in_dim.12
  133.7 0.1 broadcast_in_dim.13
  133.8 32.8 %all_to_all.33 = f32[8,8,4608]{2,1,0:T(8,128)S(1)} all-to-all(f32[8,8,4608]{2,1,0:T(8,128)S(1)} %broadcast_in_dim.13), channel_id=1, replica_groups=mesh['groups'=2,'fsdp'=16,'mp'=8,'sub'=2] {'mp'}, dimensions={0} | all-to-all | bytes 2359296 | tf_op jit(solution)/shard_map/all_to_all | solution.py:14
  166.5 0.1 reduce_sum.72
  166.6 0.2 multiply_reduce_fusion.1
  166.8 0.0 copy-done.1
  166.8 0.0 copy-done.2
  166.8 0.2 multiply_reduce_fusion
  167.0 0.0 copy-done.5
  167.0 0.7 multiply_convert_fusion
  167.7 0.1 all-gather.2.cloned.1.call-update
  167.8 0.1 shift_left.57
  167.9 0.1 shift_left.58
  168.0 1.3 dynamic-slice
  169.9 0.0 copy-done.7
  169.9 0.2 dynamic-update-slice
  170.1 0.0 copy-done
  170.2 0.0 copy-done.3
  170.2 3.6 %fusion.4 = bf16[512,4608]{0,1:T(8,128)(2,1)} fusion(s32[4608]{0:T(1024)S(1)} %shift_left.58, s32[512,576]{0,1:T(8,128)S(1)} %copy-done, bf16[512,36]{0,1:T(8,128)(2,1)S(1)} %copy-done.3), kind=kLoop, calls=%fused_computation.6 | loop fusion | flops 16515072 | bytes 5953536 | tf_op jit(solution)/shard_map/mul | solution.py:63
  173.7 24.7 %all-reduce = s32[256]{0:T(256)S(1)} all-reduce(s32[256]{0:T(256)S(1)} %dynamic-update-slice), channel_id=1, replica_groups=mesh['groups'=2,'fsdp'=16,'mp'=8,'sub'=2] {'fsdp','sub'}, use_global_device_ids=true, to_apply=%add | all-reduce | flops 256 | bytes 2048
  198.4 43.8 %all-gather.2.cloned.1.call-done = bf16[256,4608]{1,0:T(8,128)(2,1)} async-done(((bf16[8,4608]{1,0:T(8,128)(2,1)}), bf16[256,4608]{1,0:T(8,128)(2,1)}) %all-gather.2.cloned.1.call-update) | async-done | bytes 2359312 | tf_op jit(solution)/shard_map/all_gather | solution.py:96
  242.2 4.7 %exponential_reduce_fusion = (f32[256]{0:T(256)S(1)}, f32[256]{0:T(256)S(1)}) fusion(s32[512]{0:T(512)S(1)} %iota_add_fusion, s32[256]{0:T(256)S(1)} %all-reduce, bf16[256,4608]{1,0:T(8,128)(2,1)} %all-gather.2.cloned.1.call-done, bf16[512,4608]{0,1:T(8,128)(2,1)} %fusion.4), kind=kOutput, calls=%fused_computation.15 | convolution fusion | flops 1208745472 | bytes 7083008 | tf_op jit(solution)/shard_map/dot_general | solution.py:100
  246.9 22.1 %all-reduce.1 = (f32[256]{0:T(256)S(1)}, f32[256]{0:T(256)S(1)}) all-reduce(f32[256]{0:T(256)S(1)} %get-tuple-element.3, f32[256]{0:T(256)S(1)} %get-tuple-element.2), channel_id=1, replica_groups=mesh['groups'=2,'fsdp'=16,'mp'=8,'sub'=2] {'fsdp'}, use_global_device_ids=true, to_apply=%region_8.9 | all-reduce | flops 512 | bytes 4096 | tf_op jit(solution)/shard_map/psum | solution.py:36
  269.0 13.3 %all-reduce.2 = (f32[256]{0:T(256)S(1)}, f32[256]{0:T(256)S(1)}) all-reduce(f32[256]{0:T(256)S(1)} %get-tuple-element.4, f32[256]{0:T(256)S(1)} %get-tuple-element.5), channel_id=1, replica_groups=mesh['groups'=2,'fsdp'=16,'mp'=8,'sub'=2] {'mp'}, use_global_device_ids=true, to_apply=%region_9.10 | all-reduce | flops 512 | bytes 4096 | tf_op jit(solution)/shard_map/psum | solution.py:36
  282.3 13.4 %all-reduce.3 = (f32[256]{0:T(256)S(1)}, f32[256]{0:T(256)S(1)}) all-reduce(f32[256]{0:T(256)S(1)} %get-tuple-element.6, f32[256]{0:T(256)S(1)} %get-tuple-element.7), channel_id=1, replica_groups=mesh['groups'=2,'fsdp'=16,'mp'=8,'sub'=2] {'sub'}, use_global_device_ids=true, to_apply=%region_10.11 | all-reduce | flops 512 | bytes 4096 | tf_op jit(solution)/shard_map/psum | solution.py:36
  295.8 0.0 copy-done.6
  295.8 1.3 fusion.13
  297.1 1.4 pad_maximum_fusion
  298.5 18.6 %all_to_all.34 = f32[32,1,2]{2,1,0:T(1,128)S(1)} all-to-all(f32[32,1,2]{2,1,0:T(1,128)S(1)} %broadcast_in_dim.15), channel_id=1, replica_groups=mesh['groups'=2,'fsdp'=16,'mp'=8,'sub'=2] {'fsdp','sub'}, dimensions={0} | all-to-all | bytes 512 | tf_op jit(solution)/shard_map/all_to_all | solution.py:14
  317.1 0.1 reduce_sum.79
  317.1 0.6 fusion.14
  (11 shorter events, 0.1 us)
Async XLA Ops:
  9.2 95.3 %all-to-all-start = ((bf16[16,8,4608]{2,1,0:T(8,128)(2,1)}), bf16[16,8,4608]{2,1,0:T(8,128)(2,1)}, u32[]{:S(2)}, u32[]{:S(2)}) async-start(bf16[16,8,4608]{2,1,0:T(8,128)(2,1)} %broadcast_in_dim.11), calls=%async_computation | async-start | bytes 2359296 | tf_op jit(solution)/shard_map/all_to_all | solution.py:14
  53.4 188.8 %all-gather.2.cloned.1.call-start = ((), (), s32[]{:S(2)}) async-start(), calls=%async_computation.4 | async-start | bytes 2433024 | tf_op jit(solution)/shard_map/all_gather | solution.py:96
  55.0 0.8 copy-start.4
  107.6 59.2 %copy-start.1 = (bf16[8,4608]{1,0:T(8,128)(2,1)S(1)}, bf16[8,4608]{1,0:T(8,128)(2,1)}, u32[]{:S(2)}) copy-start(bf16[8,4608]{1,0:T(8,128)(2,1)} %param.11) | copy-start | bytes 221188
  107.6 59.2 %copy-start.2 = (f32[4608]{0:T(1024)S(1)}, f32[4608]{0:T(1024)}, u32[]{:S(2)}) copy-start(f32[4608]{0:T(1024)} %param.14) | copy-start | bytes 55300
  107.6 59.4 %copy-start.5 = (f32[4608]{0:T(1024)S(1)}, f32[4608]{0:T(1024)}, u32[]{:S(2)}) copy-start(f32[4608]{0:T(1024)} %param.15) | copy-start | bytes 55300
  107.6 62.3 %copy-start.7 = (s32[8]{0:T(128)S(1)}, s32[8]{0:T(128)}, u32[]{:S(2)}) copy-start(s32[8]{0:T(128)} %param.18) | copy-start | bytes 100
  107.6 62.6 %copy-start = (s32[512,576]{0,1:T(8,128)S(1)}, s32[512,576]{0,1:T(8,128)}, u32[]{:S(2)}) copy-start(s32[512,576]{0,1:T(8,128)} %param.16) | copy-start | bytes 3538948
  107.6 62.6 %copy-start.3 = (bf16[512,36]{0,1:T(8,128)(2,1)S(1)}, bf16[512,36]{0,1:T(8,128)(2,1)}, u32[]{:S(2)}) copy-start(bf16[512,36]{0,1:T(8,128)(2,1)} %param.17) | copy-start | bytes 110596
  173.7 122.1 %copy-start.6 = (s32[8]{0:T(128)S(1)}, s32[8]{0:T(128)}, u32[]{:S(2)}) copy-start(s32[8]{0:T(128)} %param.19) | copy-start | bytes 100
Sparse Core Ops, SparseCore 0:
  167.9 74.2 all-gather.1
where the time goes:
time: 328 us; the launch traced here: 327 us
  blocking collectives  150 us (46%)
  waiting for transfers between devices  91.3 us (28%)
  starting transfers between devices  44.3 us (14%)
  between operations  17.3 us (5%)
  other arithmetic  8.79 us (3%)
  local copies, waits for them, and re-layouts  7.95 us (2%)
  matrix products  7.72 us (2%)
    all_to_all x2, blocking collectives, copy_for_each(): lax.all_to_all(jnp.broadcast_to(value[None], (peers, *value.shape)), axis...  51.3 us
    psum x3, blocking collectives, by_axis(): return functools.reduce(lax.psum, axes, value)  48.9 us
    all_to_all x1, waiting for transfers between devices, copy_for_each(): lax.all_to_all(jnp.broadcast_to(value[None], (peers, *value.shape)), axis...  47.4 us
    all_to_all x1, starting transfers between devices, copy_for_each(): lax.all_to_all(jnp.broadcast_to(value[None], (peers, *value.shape)), axis...  44.2 us
    all_gather x1, waiting for transfers between devices, on_device(): lax.all_gather(states, ('fsdp', 'sub'), axis=0, tiled=True)  43.8 us
    all_to_all x1, blocking collectives, on_device(): lax.all_to_all(partial_cols, 'fsdp', split_axis=0, concat_axis=1, tiled=T...  24.8 us
    unnamed x1, blocking collectives  24.7 us
  transfers between devices with their start and end apart: 2, of which 2 were waited for; matrix products, arithmetic and copies ran while one was open for 3% of the time, Pallas kernels for 0%

commit v1 on v0

v1 whole, which is shorter than its diff:
```python
import jax
import jax.numpy as jnp
from jax import lax
from jax.sharding import PartitionSpec as P


EPS = 1e-06
CAP = 30.0
GATHER_BYTES = 1 << 20
MXU = 256
LANES = 128


def copy_for_each(value, axis):
    peers = lax.axis_size(axis)
    return lax.all_to_all(
        jnp.broadcast_to(value[None], (peers, *value.shape)), axis, 0, 0, tiled=True
    )


def gather_cut(rows, cols, peers):
    fit = (GATHER_BYTES - 1) // (peers * rows * 2)
    return min(cols, fit // MXU * MXU)


def signed_planes(words):
    shifts = (28 - 4 * jnp.arange(8, dtype=jnp.int32))[None, :, None]
    lifted = jnp.left_shift(words[:, None, :], shifts)
    return jnp.right_shift(lifted, 28)


def dequant_down(words, scales):
    cols = words.shape[1]
    codes = signed_planes(words).astype(jnp.bfloat16)
    grouped = codes.reshape(scales.shape[0], -1, cols) * scales[:, None, :]
    return grouped.reshape(-1, cols)


def dequant_embed(words, scales):
    rows = words.shape[0]
    codes = signed_planes(words).astype(jnp.bfloat16)
    grouped = codes.reshape(rows, scales.shape[1], -1) * scales[:, :, None]
    return grouped.reshape(rows, -1)


def dot_f32(a, b, dims):
    return lax.dot_general(a, b, (dims, ((), ())), preferred_element_type=jnp.float32)


def in_digits(ids):
    return jnp.stack([ids & 255, (ids >> 8) & 255, ids >> 16], axis=-1)


def on_device(
    hidden,
    residual,
    down_packed,
    down_scale,
    post_gain,
    final_gain,
    embed_packed,
    embed_scale,
    targets,
    loss_mask,
):
    toks, width = hidden.shape
    n_z, n_x, n_s = (lax.axis_size(a) for a in ("fsdp", "mp", "sub"))
    z, x, s = (lax.axis_index(a) for a in ("fsdp", "mp", "sub"))
    cols = down_packed.shape[1]
    dim = n_z * cols
    held = n_z * toks
    per_x = held // n_x
    bf16, f32 = jnp.bfloat16, jnp.float32

    cut = gather_cut(toks, width, n_z)
    tail = copy_for_each(hidden[:, cut:], "fsdp").reshape(held, width - cut)
    head = lax.all_gather(hidden[:, :cut], "fsdp").reshape(held, cut)
    group = width // down_scale.shape[0]
    part = dot_f32(
        head, dequant_down(down_packed[: cut // 8], down_scale[: cut // group]), ((1,), (0,))
    ) + dot_f32(tail, dequant_down(down_packed[cut // 8 :], down_scale[cut // group :]), ((1,), (0,)))

    part = jnp.swapaxes(part.reshape(n_z, toks, cols), 0, 1).reshape(n_x, per_x, cols)
    ffn = jnp.sum(lax.all_to_all(part, "mp", 0, 0, tiled=True), axis=0)

    high = lax.reduce_precision(ffn, 8, 7)
    own_row = lax.dynamic_slice_in_dim(residual, x, 1, 0).reshape(n_z, cols)
    own_target = in_digits(lax.dynamic_slice_in_dim(targets, x, 1, 0)).astype(bf16)
    block = jnp.concatenate([high.astype(bf16), (ffn - high).astype(bf16), own_row], axis=0)
    extra = jnp.zeros((block.shape[0], -cols % LANES), bf16)
    extra = lax.dynamic_update_slice(extra, own_target, (2 * per_x, 0))
    block = jnp.concatenate([block, extra], axis=1)
    blocks = lax.all_gather(block, "fsdp")
    rows = (
        blocks[:, :per_x, :cols].astype(f32) + blocks[:, per_x : 2 * per_x, :cols].astype(f32)
    )
    rows = jnp.swapaxes(rows, 0, 1).reshape(per_x, dim)
    res = blocks[:, 2 * per_x :, :cols].astype(f32).reshape(per_x, dim)
    normed = rows * lax.rsqrt(jnp.mean(rows * rows, axis=-1, keepdims=True) + EPS) * post_gain
    stream = res + normed
    states = (
        stream * lax.rsqrt(jnp.mean(stream * stream, axis=-1, keepdims=True) + EPS) * final_gain
    ).astype(bf16)
    digits = jnp.pad(blocks[:, 2 * per_x, cols : cols + 3], ((0, 0), (0, LANES - 3)))

    cut = gather_cut(per_x, dim, n_x)
    tail = jnp.concatenate([states[:, cut:], digits], axis=1)
    tail = jnp.broadcast_to(tail[None], (n_x, *tail.shape))
    head, tail = lax.optimization_barrier((states[:, :cut], tail))
    tail = lax.all_to_all(tail, "mp", 0, 0, tiled=True)
    head = lax.all_gather(head, "mp")
    head = head.reshape(held, cut)
    tail = tail.reshape(held, dim - cut + LANES)
    embed = dequant_embed(embed_packed, embed_scale)
    embed_tail = jnp.pad(embed[:, cut:], ((0, 0), (0, LANES)))
    vocab_rows = embed.shape[0]
    first_id = lax.axis_index(("fsdp", "mp", "sub")) * vocab_rows
    ids = (first_id + jnp.arange(vocab_rows, dtype=jnp.int32))[:, None]
    pick = jnp.array([1.0, 256.0, 65536.0], bf16)
    pick = jnp.pad(pick, (0, LANES - 3))[None, :]

    def sums_of(head, tail):
        logits = dot_f32(embed[:, :cut], head, ((1,), (1,))) + dot_f32(
            embed_tail, tail, ((1,), (1,))
        )
        goal = dot_f32(pick, tail[:, dim - cut :], ((1,), (1,))).astype(jnp.int32)
        capped = CAP * jnp.tanh(logits / CAP)
        return (
            jnp.sum(jnp.exp(capped), axis=0),
            jnp.sum(jnp.where(ids == goal, capped, 0.0), axis=0),
        )

    swap = [(i, n_s - 1 - i) for i in range(n_s)]
    far = (lax.ppermute(head, "sub", swap), lax.ppermute(tail, "sub", swap))
    own_sums, own_goals = sums_of(head, tail)
    far_sums, far_goals = sums_of(*far)

    lane = jnp.arange(held, dtype=jnp.int32)
    spread = jnp.repeat(loss_mask.astype(f32), n_z)
    here = jnp.where((lane % n_z == z) & (x == 0), spread, 0.0)
    own = jnp.stack([own_sums, own_goals, here])
    other = jnp.stack([far_sums, far_goals, jnp.zeros_like(here)])
    packed = jnp.where(s == 0, jnp.concatenate([own, other]), jnp.concatenate([other, own]))
    packed = jnp.sum(copy_for_each(packed, ("mp", "sub")), axis=0)
    packed = jnp.sum(copy_for_each(packed, "fsdp"), axis=0)
    packed = packed.reshape(n_s, 3, held)
    losses = packed[:, 2] * (jnp.log(packed[:, 0]) - packed[:, 1])
    mean_loss = (jnp.sum(losses) / jnp.maximum(jnp.sum(packed[:, 2]), 1.0)).reshape(1)
    mine = jnp.where(s == 0, losses[0], losses[1]).reshape(toks, n_z)
    token_loss = jnp.sum(jnp.where(jnp.arange(n_z) == z, mine, 0.0), axis=1)
    return (token_loss, mean_loss)


def solution(mesh):
    return jax.shard_map(
        on_device,
        mesh=mesh,
        in_specs=(
            P(("groups", "fsdp", "sub"), "mp"),
            P(("groups", "fsdp", "sub"), None),
            P("mp", "fsdp"),
            P("mp", "fsdp"),
            P(),
            P(),
            P(("fsdp", "mp", "sub"), None),
            P(("fsdp", "mp", "sub"), None),
            P(("groups", "fsdp", "sub")),
            P(("groups", "fsdp", "sub")),
        ),
        out_specs=(P(("groups", "fsdp", "sub")), P("groups")),
        check_vma=False,
    )
```

time: 328 us -> 230 us (0.70)
  waiting for transfers between devices: 91.3 us -> 14.9 us
  blocking collectives: 150 us -> 85.6 us
  starting transfers between devices: 44.3 us -> 93.6 us
  between operations: 17.3 us -> 5.43 us
  local copies, waits for them, and re-layouts: 7.95 us -> 13.3 us
    all_gather x0 -> x3, blocking collectives: none -> 74.9 us  [the longest x1 29 us: on_device(): head = lax.all_gather(hidden[:, :cut], 'fsdp').reshape(held, cut)]
    psum x3 -> x0, blocking collectives: 48.9 us -> none  [by_axis(): return functools.reduce(lax.psum, axes, value)]
    all_gather x1 -> x0, waiting for transfers between devices: 43.8 us -> none  [on_device(): lax.all_gather(states, ('fsdp', 'sub'), axis=0, tiled=True)]
    all_to_all x2 -> x1, blocking collectives: 51.3 us -> 10.7 us  [copy_for_each(): lax.all_to_all(jnp.broadcast_to(value[None], (peers, *value.shape)), axis...]
    all_to_all x1 -> x2, waiting for transfers between devices: 47.4 us -> 11.5 us  [copy_for_each(): lax.all_to_all(jnp.broadcast_to(value[None], (peers, *value.shape)), axis...]
    ppermute x0 -> x2, starting transfers between devices: none -> 29.5 us  [on_device(): far = (lax.ppermute(head, 'sub', swap), lax.ppermute(tail, 'sub', swap))]
    all_to_all x1 -> x0, blocking collectives: 24.8 us -> none  [on_device(): lax.all_to_all(partial_cols, 'fsdp', split_axis=0, concat_axis=1, tiled=T...]
    unnamed x1 -> x0, blocking collectives: 24.7 us -> none
  transfers between devices with their start and end apart: 2 -> 6, of which waited for: 2 -> 3; matrix products, arithmetic and copies ran while one was open for 3% -> 7% of each run, Pallas kernels for 0% -> 0%
where the time goes in v1:
time: 230 us; the launch traced here: 228 us
  starting transfers between devices  93.6 us (41%)
  blocking collectives  85.6 us (37%)
  waiting for transfers between devices  14.9 us (6%)
  local copies, waits for them, and re-layouts  13.3 us (6%)
  matrix products  9.23 us (4%)
  other arithmetic  6.25 us (3%)
  between operations  5.43 us (2%)
    all_to_all x2, starting transfers between devices, copy_for_each(): lax.all_to_all(jnp.broadcast_to(value[None], (peers, *value.shape)), axis...  53.1 us
    ppermute x2, starting transfers between devices, on_device(): far = (lax.ppermute(head, 'sub', swap), lax.ppermute(tail, 'sub', swap))  29.5 us
    all_gather x1, blocking collectives, on_device(): head = lax.all_gather(hidden[:, :cut], 'fsdp').reshape(held, cut)  29 us
    all_gather x1, blocking collectives, on_device(): blocks = lax.all_gather(block, 'fsdp')  25.1 us
    all_gather x1, blocking collectives, on_device(): head = lax.all_gather(head, 'mp')  20.8 us
    all_to_all x2, waiting for transfers between devices, copy_for_each(): lax.all_to_all(jnp.broadcast_to(value[None], (peers, *value.shape)), axis...  11.5 us
    all_to_all x1, blocking collectives, copy_for_each(): lax.all_to_all(jnp.broadcast_to(value[None], (peers, *value.shape)), axis...  10.7 us
    dot_general x8, matrix products, dot_f32(): lax.dot_general(a, b, (dims, ((), ())), preferred_element_type=jnp.float32)  9.23 us
  transfers between devices with their start and end apart: 6, of which 3 were waited for; matrix products, arithmetic and copies ran while one was open for 7% of the time, Pallas kernels for 0%

profile of v1, /device:TPU:65, one launch (start us, length us, event | category | flops | bytes accessed | tf_op | source)
XLA Modules:
  0.0 228.4 jit_solution(9401649721212594716)
XLA Ops:
  0.6 0.7 slice.73
  1.4 0.7 broadcast_in_dim.24
  2.1 44.2 %all-to-all-start = ((bf16[16,8,768]{2,1,0:T(8,128)(2,1)}), bf16[16,8,768]{2,1,0:T(8,128)(2,1)S(1)}, u32[]{:S(2)}, u32[]{:S(2)}) async-start(bf16[16,8,768]{2,1,0:T(8,128)(2,1)} %broadcast_in_dim.24), calls=%async_computation | async-start | bytes 393216 | tf_op jit(solution)/shard_map/all_to_all | solution.py:16
  46.3 0.8 slice.70
  47.2 1.1 slice.68
  48.3 1.1 slice.71
  49.3 0.7 slice.72
  50.0 1.2 dynamic_slice.7
  53.3 0.3 copy.55
  53.6 29.0 %all-gather = bf16[128,3840]{1,0:T(8,128)(2,1)S(1)} all-gather(bf16[8,3840]{1,0:T(8,128)(2,1)S(1)} %slice.70), channel_id=2, replica_groups=mesh['groups'=2,'fsdp'=16,'mp'=8,'sub'=2] {'fsdp'}, dimensions={0}, use_global_device_ids=true | all-gather | bytes 1044480 | tf_op jit(solution)/shard_map/all_gather | solution.py:77
  82.6 0.1 copy.57
  82.9 0.2 fusion.33
  83.2 0.4 shift_left.83
  83.6 1.0 fusion.9
  84.6 1.0 fusion.51
  85.7 0.3 fusion.27
  86.0 0.1 copy.58
  86.2 0.7 copy.59
  86.9 7.3 %all-to-all-start.1 = ((f32[8,16,288]{2,1,0:T(8,128)}), f32[8,16,288]{2,1,0:T(8,128)S(1)}, u32[]{:S(2)}, u32[]{:S(2)}) async-start(f32[8,16,288]{2,1,0:T(8,128)} %copy.59), calls=%async_computation.1 | async-start | bytes 393216 | tf_op jit(solution)/shard_map/all_to_all | solution.py:84
  94.6 2.7 %fusion.4 = bf16[512,4608]{0,1:T(8,128)(2,1)S(1)} fusion(s32[4608]{0:T(1024)S(1)} %shift_left.80, s32[512,576]{0,1:T(8,128)} %param.17, bf16[512,36]{0,1:T(8,128)(2,1)S(1)} %copy-done.3), kind=kLoop, calls=%fused_computation.6 | loop fusion | flops 16515072 | bytes 5953536 | tf_op jit(solution)/shard_map/mul | solution.py:42
  97.3 2.1 copy-done.1
  99.7 3.1 %all-to-all-done.1 = f32[8,16,288]{2,1,0:T(8,128)S(1)} async-done(((f32[8,16,288]{2,1,0:T(8,128)}), f32[8,16,288]{2,1,0:T(8,128)S(1)}, u32[]{:S(2)}, u32[]{:S(2)}) %all-to-all-start.1) | async-done | bytes 147488 | tf_op jit(solution)/shard_map/all_to_all | solution.py:84
  102.9 25.1 %all-gather.1 = bf16[768,384]{1,0:T(8,128)(2,1)S(1)} all-gather(bf16[48,384]{1,0:T(8,128)(2,1)S(1)} %pad_maximum_fusion), channel_id=3, replica_groups=mesh['groups'=2,'fsdp'=16,'mp'=8,'sub'=2] {'fsdp'}, dimensions={0}, use_global_device_ids=true | all-gather | bytes 626688 | tf_op jit(solution)/shard_map/all_gather | solution.py:93
  128.0 0.2 multiply_reduce_fusion.1
  128.4 0.3 multiply_reduce_fusion
  128.7 0.1 copy.61
  128.8 0.2 reshape.391
  129.0 0.1 copy.62
  129.1 0.2 reshape.392
  129.3 0.1 multiply_convert_fusion
  129.7 0.7 broadcast_in_dim.26
  130.4 20.8 %all-gather.2 = bf16[128,3840]{1,0:T(8,128)(2,1)S(1)} all-gather(bf16[16,3840]{1,0:T(8,128)(2,1)S(1)} %slice.92), channel_id=4, replica_groups=mesh['groups'=2,'fsdp'=16,'mp'=8,'sub'=2] {'mp'}, dimensions={0}, use_global_device_ids=true | all-gather | bytes 1105920 | tf_op jit(solution)/shard_map/all_gather | solution.py:111
  151.2 3.7 %all-to-all-start.2 = ((bf16[8,16,896]{2,1,0:T(8,128)(2,1)}), bf16[8,16,896]{2,1,0:T(8,128)(2,1)S(1)}, u32[]{:S(2)}, u32[]{:S(2)}) async-start(bf16[8,16,896]{2,1,0:T(8,128)(2,1)} %broadcast_in_dim.26), calls=%async_computation.2 | async-start | bytes 458752 | tf_op jit(solution)/shard_map/all_to_all | solution.py:110
  154.9 22.7 %collective-permute-start = (bf16[128,3840]{1,0:T(8,128)(2,1)S(1)}, bf16[128,3840]{1,0:T(8,128)(2,1)S(1)}, u32[]{:S(2)}, u32[]{:S(2)}) collective-permute-start(bf16[128,3840]{1,0:T(8,128)(2,1)S(1)} %all-gather.2), channel_id=1, source_target_pairs={{0,1},{1,0},{2,3},{3,2},{4,5},{5,4},{6,7},{7,6},{8,9},{9,8},{10,11... | collective-permute-start | bytes 2949128 | tf_op jit(solution)/shard_map/ppermute | solution.py:134
  177.6 3.3 %fusion.7 = f32[512,128]{1,0:T(8,128)S(1)} fusion(bf16[128,3840]{1,0:T(8,128)(2,1)S(1)} %all-gather.2, bf16[512,4608]{0,1:T(8,128)(2,1)} %copy-done.1), kind=kOutput, calls=%fused_computation.9 | convolution fusion | flops 503316480 | bytes 5177344 | tf_op jit(solution)/shard_map/dot_general | solution.py:47
  181.0 6.8 %collective-permute-start.1 = (bf16[128,896]{1,0:T(8,128)(2,1)S(1)}, bf16[128,896]{1,0:T(8,128)(2,1)S(1)}, u32[]{:S(2)}, u32[]{:S(2)}) collective-permute-start(bf16[128,896]{1,0:T(8,128)(2,1)S(1)} %bitcast.83), channel_id=1, source_target_pairs={{0,1},{1,0},{2,3},{3,2},{4,5},{5,4},{6,7},{7,6},{8,9},{9,8},{10,11... | collective-permute-start | bytes 688136 | tf_op jit(solution)/shard_map/ppermute | solution.py:134
  187.8 0.4 fusion.14
  188.3 0.1 fusion.28
  188.4 0.3 collective-permute-done.1
  188.7 0.1 fusion.29
  188.9 0.5 fusion.30
  189.3 3.4 %select_reduce_fusion = (f32[128]{0:T(128)S(1)}, f32[128]{0:T(128)S(1)}, f32[128]{0:T(128)S(1)}, f32[128]{0:T(128)S(1)}) fusion(s32[128]{0:T(128)S(1)} %fusion.29, s32[512]{0:T(512)S(1)} %iota_add_fusion, f32[512,128]{1,0:T(8,128)S(1)} %fusion.14, s32[128]{0:T(128)S(1)} %fusion.28, f32[512,128]{1,0:T(8,128)S(1)} %fusion.30, ...), kind=kOutput, calls=%fused_computation.37 | convolution fusion | flops 504036864 | bytes 5444608 | tf_op jit(solution)/shard_map/dot_general | solution.py:47
  192.8 10.7 %all_to_all.25 = f32[16,6,128]{2,1,0:T(8,128)S(1)} all-to-all(f32[16,6,128]{2,1,0:T(8,128)S(1)} %broadcast_in_dim.31), channel_id=1, replica_groups=mesh['groups'=2,'fsdp'=16,'mp'=8,'sub'=2] {'mp','sub'}, dimensions={0} | all-to-all | bytes 98304 | tf_op jit(solution)/shard_map/all_to_all | solution.py:16
  203.5 0.6 broadcast_in_dim.32
  204.2 8.9 %all-to-all-start.4 = ((f32[16,6,128]{2,1,0:T(8,128)}), f32[16,6,128]{2,1,0:T(8,128)S(1)}, u32[]{:S(2)}, u32[]{:S(2)}) async-start(f32[16,6,128]{2,1,0:T(8,128)} %broadcast_in_dim.32), calls=%async_computation.4 | async-start | bytes 131072 | tf_op jit(solution)/shard_map/all_to_all | solution.py:16
  213.1 11.5 %all-to-all-done.4 = f32[16,6,128]{2,1,0:T(8,128)S(1)} async-done(((f32[16,6,128]{2,1,0:T(8,128)}), f32[16,6,128]{2,1,0:T(8,128)S(1)}, u32[]{:S(2)}, u32[]{:S(2)}) %all-to-all-start.4) | async-done | bytes 49184 | tf_op jit(solution)/shard_map/all_to_all | solution.py:16
  224.6 0.6 fusion.49
  226.6 0.6 select_reduce_fusion.2
  (59 shorter events, 1.7 us)
Async XLA Ops:
  0.6 93.5 %copy-start = (bf16[8,4608]{1,0:T(8,128)(2,1)S(1)}, bf16[8,4608]{1,0:T(8,128)(2,1)}, u32[]{:S(2)}) copy-start(bf16[8,4608]{1,0:T(8,128)(2,1)} %param.12) | copy-start | bytes 221188
  2.1 83.6 %all-to-all-start = ((bf16[16,8,768]{2,1,0:T(8,128)(2,1)}), bf16[16,8,768]{2,1,0:T(8,128)(2,1)S(1)}, u32[]{:S(2)}, u32[]{:S(2)}) async-start(bf16[16,8,768]{2,1,0:T(8,128)(2,1)} %broadcast_in_dim.24), calls=%async_computation | async-start | bytes 393216 | tf_op jit(solution)/shard_map/all_to_all | solution.py:16
  82.8 0.7 slice-start
  84.6 9.7 %copy-start.2 = (f32[4608]{0:T(1024)S(1)}, f32[4608]{0:T(1024)}, u32[]{:S(2)}) copy-start(f32[4608]{0:T(1024)} %param.15) | copy-start | bytes 55300
  84.6 9.9 %copy-start.3 = (bf16[512,36]{0,1:T(8,128)(2,1)S(1)}, bf16[512,36]{0,1:T(8,128)(2,1)}, u32[]{:S(2)}) copy-start(bf16[512,36]{0,1:T(8,128)(2,1)} %param.18) | copy-start | bytes 110596
  85.7 13.8 %copy-start.6 = (s32[8]{0:T(128)S(1)}, s32[8]{0:T(128)}, u32[]{:S(2)}) copy-start(s32[8]{0:T(128)} %param.20) | copy-start | bytes 100
  86.9 15.9 %all-to-all-start.1 = ((f32[8,16,288]{2,1,0:T(8,128)}), f32[8,16,288]{2,1,0:T(8,128)S(1)}, u32[]{:S(2)}, u32[]{:S(2)}) async-start(f32[8,16,288]{2,1,0:T(8,128)} %copy.59), calls=%async_computation.1 | async-start | bytes 393216 | tf_op jit(solution)/shard_map/all_to_all | solution.py:84
  97.3 2.1 copy-start.1
  99.4 29.9 %copy-start.4 = (f32[4608]{0:T(1024)S(1)}, f32[4608]{0:T(1024)}, u32[]{:S(2)}) copy-start(f32[4608]{0:T(1024)} %param.16) | copy-start | bytes 55300
  151.2 37.1 %copy-start.5 = (bf16[128,1]{0,1:T(2,128)(2,1)S(1)}, bf16[128,1]{0,1:T(2,128)(2,1)}, u32[]{:S(2)}) copy-start(bf16[128,1]{0,1:T(2,128)(2,1)} %constant.86) | copy-start | bytes 772
  151.2 29.8 %all-to-all-start.2 = ((bf16[8,16,896]{2,1,0:T(8,128)(2,1)}), bf16[8,16,896]{2,1,0:T(8,128)(2,1)S(1)}, u32[]{:S(2)}, u32[]{:S(2)}) async-start(bf16[8,16,896]{2,1,0:T(8,128)(2,1)} %broadcast_in_dim.26), calls=%async_computation.2 | async-start | bytes 458752 | tf_op jit(solution)/shard_map/all_to_all | solution.py:110
  154.9 34.4 %collective-permute-start = (bf16[128,3840]{1,0:T(8,128)(2,1)S(1)}, bf16[128,3840]{1,0:T(8,128)(2,1)S(1)}, u32[]{:S(2)}, u32[]{:S(2)}) collective-permute-start(bf16[128,3840]{1,0:T(8,128)(2,1)S(1)} %all-gather.2), channel_id=1, source_target_pairs={{0,1},{1,0},{2,3},{3,2},{4,5},{5,4},{6,7},{7,6},{8,9},{9,8},{10,11... | collective-permute-start | bytes 2949128 | tf_op jit(solution)/shard_map/ppermute | solution.py:134
  181.0 7.7 %collective-permute-start.1 = (bf16[128,896]{1,0:T(8,128)(2,1)S(1)}, bf16[128,896]{1,0:T(8,128)(2,1)S(1)}, u32[]{:S(2)}, u32[]{:S(2)}) collective-permute-start(bf16[128,896]{1,0:T(8,128)(2,1)S(1)} %bitcast.83), channel_id=1, source_target_pairs={{0,1},{1,0},{2,3},{3,2},{4,5},{5,4},{6,7},{7,6},{8,9},{9,8},{10,11... | collective-permute-start | bytes 688136 | tf_op jit(solution)/shard_map/ppermute | solution.py:134
  204.2 20.4 %all-to-all-start.4 = ((f32[16,6,128]{2,1,0:T(8,128)}), f32[16,6,128]{2,1,0:T(8,128)S(1)}, u32[]{:S(2)}, u32[]{:S(2)}) async-start(f32[16,6,128]{2,1,0:T(8,128)} %broadcast_in_dim.32), calls=%async_computation.4 | async-start | bytes 131072 | tf_op jit(solution)/shard_map/all_to_all | solution.py:16

commit v2 on v1

--- a/solution.py
+++ b/solution.py
@@ -1,6 +1,8 @@
 import jax
 import jax.numpy as jnp
 from jax import lax
+from jax.experimental import pallas as pl
+from jax.experimental.pallas import tpu as pltpu
 from jax.sharding import PartitionSpec as P
 
 
@@ -49,6 +51,95 @@
 
 def in_digits(ids):
     return jnp.stack([ids & 255, (ids >> 8) & 255, ids >> 16], axis=-1)
+
+
+def split_kernel(hidden_ref, head_ref, tail_ref):
+    cut = head_ref.shape[1]
+    head_ref[...] = hidden_ref[:, :cut]
+    tail_ref[...] = jnp.broadcast_to(hidden_ref[:, cut:][None], tail_ref.shape)
+
+
+def split_columns(hidden, cut, copies):
+    rows, width = hidden.shape
+    return pl.pallas_call(
+        split_kernel,
+        out_shape=(
+            jax.ShapeDtypeStruct((rows, cut), hidden.dtype),
+            jax.ShapeDtypeStruct((copies, rows, width - cut), hidden.dtype),
+        ),
+        name="split_columns",
+    )(hidden)
+
+
+def sums_kernel(n_z, pos_ref, mask_ref, head_ref, far_ref, tails_ref, embed_ref, out_ref, st_ref, acc_ref):
+    held, cut = head_ref.shape
+    blocks, per, _ = tails_ref.shape
+    n_s = st_ref.shape[0] // held
+    vocab, dim = embed_ref.shape
+    step = pl.program_id(0)
+    first, s, z, lead = (pos_ref[i] for i in range(4))
+
+    @pl.when(step == 0)
+    def _():
+        st_ref[pl.ds(pl.multiple_of(s * held, held), held), :cut] = head_ref[...]
+        st_ref[pl.ds(pl.multiple_of((n_s - 1 - s) * held, held), held), :cut] = far_ref[...]
+        for i in range(blocks):
+            row = i % n_s * held + i // n_s * per
+            st_ref[row : row + per, cut:] = tails_ref[i]
+        acc_ref[...] = jnp.zeros_like(acc_ref)
+
+    logits = dot_f32(embed_ref[...], st_ref[:, :dim], ((1,), (1,)))
+    lane = lax.broadcasted_iota(jnp.int32, (8, LANES), 1)
+    pick = jnp.where(
+        lane == 0, 1.0, jnp.where(lane == 1, 256.0, jnp.where(lane == 2, 65536.0, 0.0))
+    )
+    goal = dot_f32(pick.astype(jnp.bfloat16), st_ref[:, dim:], ((1,), (1,))).astype(jnp.int32)
+    capped = CAP * jnp.tanh(logits / CAP)
+    ids = lax.broadcasted_iota(jnp.int32, logits.shape, 0) + (first + step * vocab)
+    acc_ref[0:1] += jnp.sum(jnp.exp(capped), axis=0, keepdims=True)
+    acc_ref[1:2] += jnp.sum(jnp.where(ids == goal[0:1], capped, 0.0), axis=0, keepdims=True)
+
+    @pl.when(step == pl.num_programs(0) - 1)
+    def _():
+        place = lax.broadcasted_iota(jnp.int32, (1, n_s * held), 1)
+        row = jnp.zeros((1, n_s * held), jnp.float32)
+        for i in range(mask_ref.shape[0]):
+            row = jnp.where(
+                place == s * held + i * n_z + z, (mask_ref[i] * lead).astype(jnp.float32), row
+            )
+        acc_ref[2:3] = row
+        for r in range(3):
+            for h in range(n_s):
+                part = acc_ref[r : r + 1, h * held : (h + 1) * held]
+                out_ref[:, r * n_s + h : r * n_s + h + 1, :] = jnp.broadcast_to(
+                    part[None], (out_ref.shape[0], 1, held)
+                )
+
+
+def vocab_sums(pos, mask, head, far, tails, embed, n_z, copies):
+    held, _ = head.shape
+    vocab, dim = embed.shape
+    n_s = tails.shape[0] * tails.shape[1] // held
+    step = min(vocab, MXU)
+    smem = pl.BlockSpec(memory_space=pltpu.SMEM)
+    whole = lambda a: pl.BlockSpec(a.shape, lambda i: (0,) * a.ndim)
+    return pl.pallas_call(
+        lambda *refs: sums_kernel(n_z, *refs),
+        grid=(vocab // step,),
+        in_specs=[smem, smem, whole(head), whole(far), whole(tails), pl.BlockSpec((step, dim), lambda i: (i, 0))],
+        out_specs=pl.BlockSpec((copies, 3 * n_s, held), lambda i: (0, 0, 0)),
+        out_shape=jax.ShapeDtypeStruct((copies, 3 * n_s, held), jnp.float32),
+        scratch_shapes=[
+            pltpu.VMEM((n_s * held, dim + LANES), jnp.bfloat16),
+            pltpu.VMEM((8, n_s * held), jnp.float32),
+        ],
+        cost_estimate=pl.CostEstimate(
+            flops=2 * n_s * held * vocab * dim,
+            bytes_accessed=2 * (n_s * held + vocab) * dim,
+            transcendentals=2 * n_s * held * vocab,
+        ),
+        name="vocab_sums",
+    )(pos, mask, head, far, tails, embed)
 
 
 def on_device(
@@ -73,12 +164,16 @@
     bf16, f32 = jnp.bfloat16, jnp.float32
 
     cut = gather_cut(toks, width, n_z)
-    tail = copy_for_each(hidden[:, cut:], "fsdp").reshape(held, width - cut)
-    head = lax.all_gather(hidden[:, :cut], "fsdp").reshape(held, cut)
-    group = width // down_scale.shape[0]
-    part = dot_f32(
-        head, dequant_down(down_packed[: cut // 8], down_scale[: cut // group]), ((1,), (0,))
-    ) + dot_f32(tail, dequant_down(down_packed[cut // 8 :], down_scale[cut // group :]), ((1,), (0,)))
+    head, tail = split_columns(hidden, cut, n_z)
+    tail = lax.all_to_all(tail, "fsdp", 0, 0, tiled=True)
+    head = lax.all_gather(head, "fsdp")
+    head, residual, targets, down_packed, down_scale = lax.optimization_barrier(
+        (head, residual, targets, down_packed, down_scale)
+    )
+    weight = dequant_down(down_packed, down_scale)
+    part = dot_f32(head.reshape(held, cut), weight[:cut], ((1,), (0,))) + dot_f32(
+        tail.reshape(held, width - cut), weight[cut:], ((1,), (0,))
+    )
 
     part = jnp.swapaxes(part.reshape(n_z, toks, cols), 0, 1).reshape(n_x, per_x, cols)
     ffn = jnp.sum(lax.all_to_all(part, "mp", 0, 0, tiled=True), axis=0)
@@ -105,47 +200,22 @@
 
     cut = gather_cut(per_x, dim, n_x)
     tail = jnp.concatenate([states[:, cut:], digits], axis=1)
-    tail = jnp.broadcast_to(tail[None], (n_x, *tail.shape))
+    tail = jnp.broadcast_to(tail[None], (n_x * n_s, *tail.shape))
     head, tail = lax.optimization_barrier((states[:, :cut], tail))
-    tail = lax.all_to_all(tail, "mp", 0, 0, tiled=True)
+    tail = lax.all_to_all(tail, ("mp", "sub"), 0, 0, tiled=True)
     head = lax.all_gather(head, "mp")
     head = head.reshape(held, cut)
-    tail = tail.reshape(held, dim - cut + LANES)
+    far = lax.ppermute(head, "sub", [(i, n_s - 1 - i) for i in range(n_s)])
     embed = dequant_embed(embed_packed, embed_scale)
-    embed_tail = jnp.pad(embed[:, cut:], ((0, 0), (0, LANES)))
-    vocab_rows = embed.shape[0]
-    first_id = lax.axis_index(("fsdp", "mp", "sub")) * vocab_rows
-    ids = (first_id + jnp.arange(vocab_rows, dtype=jnp.int32))[:, None]
-    pick = jnp.array([1.0, 256.0, 65536.0], bf16)
-    pick = jnp.pad(pick, (0, LANES - 3))[None, :]
-
-    def sums_of(head, tail):
-        logits = dot_f32(embed[:, :cut], head, ((1,), (1,))) + dot_f32(
-            embed_tail, tail, ((1,), (1,))
-        )
-        goal = dot_f32(pick, tail[:, dim - cut :], ((1,), (1,))).astype(jnp.int32)
-        capped = CAP * jnp.tanh(logits / CAP)
-        return (
-            jnp.sum(jnp.exp(capped), axis=0),
-            jnp.sum(jnp.where(ids == goal, capped, 0.0), axis=0),
-        )
-
-    swap = [(i, n_s - 1 - i) for i in range(n_s)]
-    far = (lax.ppermute(head, "sub", swap), lax.ppermute(tail, "sub", swap))
-    own_sums, own_goals = sums_of(head, tail)
-    far_sums, far_goals = sums_of(*far)
-
-    lane = jnp.arange(held, dtype=jnp.int32)
-    spread = jnp.repeat(loss_mask.astype(f32), n_z)
-    here = jnp.where((lane % n_z == z) & (x == 0), spread, 0.0)
-    own = jnp.stack([own_sums, own_goals, here])
-    other = jnp.stack([far_sums, far_goals, jnp.zeros_like(here)])
-    packed = jnp.where(s == 0, jnp.concatenate([own, other]), jnp.concatenate([other, own]))
-    packed = jnp.sum(copy_for_each(packed, ("mp", "sub")), axis=0)
+    first_id = lax.axis_index(("fsdp", "mp", "sub")) * embed.shape[0]
+    pos = jnp.stack([first_id, s, z, (x == 0).astype(jnp.int32)])
+    packed = vocab_sums(pos, loss_mask, head, far, tail, embed, n_z, n_x * n_s)
+
+    packed = jnp.sum(lax.all_to_all(packed, ("mp", "sub"), 0, 0, tiled=True), axis=0)
     packed = jnp.sum(copy_for_each(packed, "fsdp"), axis=0)
-    packed = packed.reshape(n_s, 3, held)
-    losses = packed[:, 2] * (jnp.log(packed[:, 0]) - packed[:, 1])
-    mean_loss = (jnp.sum(losses) / jnp.maximum(jnp.sum(packed[:, 2]), 1.0)).reshape(1)
+    sums, goals, mask = packed.reshape(3, n_s, held)
+    losses = mask * (jnp.log(sums) - goals)
+    mean_loss = (jnp.sum(losses) / jnp.maximum(jnp.sum(mask), 1.0)).reshape(1)
     mine = jnp.where(s == 0, losses[0], losses[1]).reshape(toks, n_z)
     token_loss = jnp.sum(jnp.where(jnp.arange(n_z) == z, mine, 0.0), axis=1)
     return (token_loss, mean_loss)

time: 230 us -> 257 us (1.12)
  local copies, waits for them, and re-layouts: 13.3 us -> 32.3 us
  matrix products: 9.23 us -> 1.5 us
  other arithmetic: 6.25 us -> 13.2 us
  Pallas kernels: 0 us -> 6.57 us
  blocking collectives: 85.6 us -> 90.4 us
  starting transfers between devices: 93.6 us -> 88.8 us
  waiting for transfers between devices: 14.9 us -> 17.5 us
    all_to_all x1 -> x2, starting transfers between devices: 3.74 us -> 50.1 us  [the longest x1 44.2 us: on_device(): tail = lax.all_to_all(tail, 'fsdp', 0, 0, tiled=True)]
    all_to_all x2 -> x1, starting transfers between devices: 53.1 us -> 8.69 us  [copy_for_each(): lax.all_to_all(jnp.broadcast_to(value[None], (peers, *value.shape)), axis...]
    shift_left x6 -> x7, local copies, waits for them, and re-layouts: 0.69 us -> 15.2 us  [signed_planes(): lifted = jnp.left_shift(words[:, None, :], shifts)]
    mul x0 -> x2, local copies, waits for them, and re-layouts: none -> 9.27 us  [dequant_embed(): grouped = codes.reshape(rows, scales.shape[1], -1) * scales[:, :, None]]
    dot_general x8 -> x2, matrix products: 9.23 us -> 1.5 us  [dot_f32(): lax.dot_general(a, b, (dims, ((), ())), preferred_element_type=jnp.float32)]
    ppermute x2 -> x1, starting transfers between devices: 29.5 us -> 22.2 us  [on_device(): far = lax.ppermute(head, 'sub', [(i, n_s - 1 - i) for i in range(n_s)])]
    pallas_call x0 -> x2, Pallas kernels: none -> 6.57 us  [the longest x1 4.95 us: vocab_sums(): pl.pallas_call(lambda *refs: sums_kernel(n_z, *refs), grid=(vocab // step...]
    mul x1, other arithmetic: 2.73 us -> 9.08 us  [dequant_embed(): grouped = codes.reshape(rows, scales.shape[1], -1) * scales[:, :, None]]
  transfers between devices with their start and end apart: 6 -> 5, of which waited for: 3 -> 2; matrix products, arithmetic and copies ran while one was open for 7% -> 15% of each run, Pallas kernels for 0% -> 0%
where the time goes in v2:
time: 257 us; the launch traced here: 256 us
  blocking collectives  90.4 us (35%)
  starting transfers between devices  88.8 us (35%)
  local copies, waits for them, and re-layouts  32.3 us (13%)
  waiting for transfers between devices  17.5 us (7%)
  other arithmetic  13.2 us (5%)
  Pallas kernels  6.57 us (3%)
  between operations  5.3 us (2%)
    all_to_all x1, starting transfers between devices, on_device(): tail = lax.all_to_all(tail, 'fsdp', 0, 0, tiled=True)  44.2 us
    all_gather x1, blocking collectives, on_device(): head = lax.all_gather(head, 'fsdp')  34.9 us
    all_gather x1, blocking collectives, on_device(): blocks = lax.all_gather(block, 'fsdp')  22.8 us
    ppermute x1, starting transfers between devices, on_device(): far = lax.ppermute(head, 'sub', [(i, n_s - 1 - i) for i in range(n_s)])  22.2 us
    all_gather x1, blocking collectives, on_device(): head = lax.all_gather(head, 'mp')  22.2 us
    shift_left x7, local copies, waits for them, and re-layouts, signed_planes(): lifted = jnp.left_shift(words[:, None, :], shifts)  15.2 us
    all_to_all x1, waiting for transfers between devices, copy_for_each(): lax.all_to_all(jnp.broadcast_to(value[None], (peers, *value.shape)), axis...  11.4 us
    all_to_all x1, blocking collectives, on_device(): lax.all_to_all(packed, ('mp', 'sub'), 0, 0, tiled=True)  10.6 us
  transfers between devices with their start and end apart: 5, of which 2 were waited for; matrix products, arithmetic and copies ran while one was open for 15% of the time, Pallas kernels for 0%

profile of v2, /device:TPU:65, one launch (start us, length us, event | category | flops | bytes accessed | tf_op | source)
XLA Modules:
  0.0 255.7 jit_solution(13833724039602416389)
XLA Ops:
  0.7 1.6 split_columns.1
  2.3 44.2 %all-to-all-start = ((bf16[16,8,768]{2,1,0:T(8,128)(2,1)}), bf16[16,8,768]{2,1,0:T(8,128)(2,1)S(1)}, u32[]{:S(2)}, u32[]{:S(2)}) async-start(bf16[16,8,768]{2,1,0:T(8,128)(2,1)} %get-tuple-element.15), calls=%async_computation | async-start | bytes 393216 | tf_op jit(solution)/shard_map/all_to_all | solution.py:168
  46.5 34.9 %all-gather = bf16[128,3840]{1,0:T(8,128)(2,1)S(1)} all-gather(bf16[8,3840]{1,0:T(8,128)(2,1)} %get-tuple-element.11), channel_id=2, replica_groups=mesh['groups'=2,'fsdp'=16,'mp'=8,'sub'=2] {'fsdp'}, dimensions={0}, use_global_device_ids=true | all-gather | bytes 1044480 | tf_op jit(solution)/shard_map/all_gather | solution.py:169
  81.4 1.4 copy.60
  82.8 0.1 shift_left.44
  82.9 0.5 shift_left.41
  83.4 1.3 fusion.3
  84.7 0.5 slice.51
  85.3 1.2 fusion.5
  86.5 0.3 fusion.4
  86.8 0.1 copy.63
  86.9 0.7 copy.64
  87.6 7.8 %all-to-all-start.1 = ((f32[8,16,288]{2,1,0:T(8,128)}), f32[8,16,288]{2,1,0:T(8,128)S(1)}, u32[]{:S(2)}, u32[]{:S(2)}) async-start(f32[8,16,288]{2,1,0:T(8,128)} %copy.64), calls=%async_computation.1 | async-start | bytes 393216 | tf_op jit(solution)/shard_map/all_to_all | solution.py:179
  95.4 0.6 dynamic_slice.7
  98.0 0.1 reshape.155
  98.4 4.9 %shift_left.47 = s32[512,8,576]{0,2,1:T(8,128)} broadcast(s32[512,576]{0,1:T(8,128)S(1)} %copy-done.3), dimensions={0,2} | broadcast | bytes 10616832 | tf_op jit(solution)/shard_map/shift_left | solution.py:30
  103.2 9.6 %copy.70 = s32[512,4608]{1,0:T(8,128)} copy(s32[512,4608]{0,1:T(8,128)} %bitcast.45) | data formatting | bytes 18874368 | tf_op jit(solution)/shard_map/shift_left | solution.py:30
  112.9 2.5 mul.114
  115.4 6.8 %copy.71 = bf16[512,4608]{1,0:T(8,128)(2,1)} copy(bf16[512,4608]{0,1:T(8,128)(2,1)} %bitcast.47) | data formatting | bytes 9437184 | tf_op jit(solution)/shard_map/mul | solution.py:44
  122.3 0.1 pad_maximum_fusion
  122.4 22.8 %all-gather.1 = bf16[768,384]{1,0:T(8,128)(2,1)S(1)} all-gather(bf16[48,384]{1,0:T(8,128)(2,1)S(1)} %pad_maximum_fusion), channel_id=3, replica_groups=mesh['groups'=2,'fsdp'=16,'mp'=8,'sub'=2] {'fsdp'}, dimensions={0}, use_global_device_ids=true | all-gather | bytes 626688 | tf_op jit(solution)/shard_map/all_gather | solution.py:188
  145.2 0.2 multiply_reduce_fusion.1
  145.4 0.1 slice.58
  145.5 0.3 multiply_reduce_fusion
  145.8 0.1 copy.66
  145.9 0.2 reshape.156
  146.1 0.1 copy.67
  146.3 0.2 reshape.157
  146.5 0.1 multiply_convert_fusion
  146.6 0.1 copy.68
  146.7 0.1 copy.69
  146.8 0.8 broadcast_in_dim.11
  147.6 22.2 %all-gather.2.refs_2_ = bf16[128,3840]{1,0:T(8,128)(2,1)S(1)} all-gather(bf16[16,3840]{1,0:T(8,128)(2,1)S(1)} %slice.56), channel_id=4, replica_groups=mesh['groups'=2,'fsdp'=16,'mp'=8,'sub'=2] {'mp'}, dimensions={0}, use_global_device_ids=true | all-gather | bytes 1105920 | tf_op jit(solution)/shard_map/all_gather | solution.py:206
  169.8 22.2 %collective-permute-start = (bf16[128,3840]{1,0:T(8,128)(2,1)S(1)}, bf16[128,3840]{1,0:T(8,128)(2,1)S(1)}, u32[]{:S(2)}, u32[]{:S(2)}) collective-permute-start(bf16[128,3840]{1,0:T(8,128)(2,1)S(1)} %all-gather.2.refs_2_), channel_id=1, source_target_pairs={{0,1},{1,0},{2,3},{3,2},{4,5},{5,4},{6,7},{7,6},{8,9},{9,8},{10,11... | collective-permute-start | bytes 2949128 | tf_op jit(solution)/shard_map/ppermute | solution.py:208
  192.1 5.9 %all-to-all-start.2 = ((bf16[16,16,896]{2,1,0:T(8,128)(2,1)}), bf16[16,16,896]{2,1,0:T(8,128)(2,1)S(1)}, u32[]{:S(2)}, u32[]{:S(2)}) async-start(bf16[16,16,896]{2,1,0:T(8,128)(2,1)} %broadcast_in_dim.11), calls=%async_computation.2 | async-start | bytes 917504 | tf_op jit(solution)/shard_map/all_to_all | solution.py:205
  198.0 9.1 %fusion.2.refs_5_ = bf16[512,4608]{1,0:T(8,128)(2,1)} fusion(bf16[512,4608]{1,0:T(8,128)(2,1)} %copy.71, s32[512,4608]{1,0:T(8,128)} %copy.70, s32[4608]{0:T(1024)S(1)} %shift_left.50), kind=kLoop, calls=%fused_computation.4 | loop fusion | flops 16515072 | bytes 18892800 | tf_op jit(solution)/shard_map/mul | solution.py:44
  207.1 0.6 pad_add_fusion.refs_0_
  207.7 6.2 %all-to-all-done.2.refs_4_ = bf16[16,16,896]{2,1,0:T(8,128)(2,1)S(1)} async-done(((bf16[16,16,896]{2,1,0:T(8,128)(2,1)}), bf16[16,16,896]{2,1,0:T(8,128)(2,1)S(1)}, u32[]{:S(2)}, u32[]{:S(2)}) %all-to-all-start.2) | async-done | bytes 458784 | tf_op jit(solution)/shard_map/all_to_all | solution.py:205
  213.8 0.8 copy-done.2
  214.6 1.0 copy-done.4
  215.6 4.9 %vocab_sums.1 = f32[16,6,128]{2,1,0:T(8,128)} custom-call(s32[4]{0:T(128)} %pad_add_fusion.refs_0_, s32[8]{0:T(128)} %refs_1_.1, bf16[128,3840]{1,0:T(8,128)(2,1)} %copy-done.1, bf16[128,3840]{1,0:T(8,128)(2,1)} %copy-done.4, bf16[16,16,896]{2,1,0:T(8,128)(2,1)} %copy-done.2, bf16[512,4608]{1,0:T(8,128)(2,1)} %fusion.2.refs_5_), custom_call_target="tpu_custom_call" | custom-call | flops 1207959552 | bytes 7077888 | tf_op jit(solution)/shard_map/vocab_sums/pallas_call | solution.py:126
  220.5 10.6 %all_to_all.25 = f32[16,6,128]{2,1,0:T(8,128)S(1)} all-to-all(f32[16,6,128]{2,1,0:T(8,128)} %vocab_sums.1), channel_id=1, replica_groups=mesh['groups'=2,'fsdp'=16,'mp'=8,'sub'=2] {'mp','sub'}, dimensions={0} | all-to-all | bytes 98304 | tf_op jit(solution)/shard_map/all_to_all | solution.py:214
  231.2 0.6 broadcast_in_dim.12
  231.8 8.7 %all-to-all-start.4 = ((f32[16,6,128]{2,1,0:T(8,128)}), f32[16,6,128]{2,1,0:T(8,128)S(1)}, u32[]{:S(2)}, u32[]{:S(2)}) async-start(f32[16,6,128]{2,1,0:T(8,128)} %broadcast_in_dim.12), calls=%async_computation.4 | async-start | bytes 131072 | tf_op jit(solution)/shard_map/all_to_all | solution.py:18
  240.5 11.4 %all-to-all-done.4 = f32[16,6,128]{2,1,0:T(8,128)S(1)} async-done(((f32[16,6,128]{2,1,0:T(8,128)}), f32[16,6,128]{2,1,0:T(8,128)S(1)}, u32[]{:S(2)}, u32[]{:S(2)}) %all-to-all-start.4) | async-done | bytes 49184 | tf_op jit(solution)/shard_map/all_to_all | solution.py:18
  251.9 0.6 fusion.17
  252.5 0.1 select_n.31
  253.9 0.6 select_reduce_fusion
  (43 shorter events, 0.7 us)
Async XLA Ops:
  0.6 97.3 %copy-start = (bf16[8,4608]{1,0:T(8,128)(2,1)S(1)}, bf16[8,4608]{1,0:T(8,128)(2,1)}, u32[]{:S(2)}) copy-start(bf16[8,4608]{1,0:T(8,128)(2,1)} %param.11) | copy-start | bytes 221188
  0.6 82.7 %copy-start.7 = (bf16[36,288]{1,0:T(8,128)(2,1)S(1)}, bf16[36,288]{1,0:T(8,128)(2,1)}, u32[]{:S(2)}) copy-start(bf16[36,288]{1,0:T(8,128)(2,1)} %param.13) | copy-start | bytes 62212
  2.3 84.2 %all-to-all-start = ((bf16[16,8,768]{2,1,0:T(8,128)(2,1)}), bf16[16,8,768]{2,1,0:T(8,128)(2,1)S(1)}, u32[]{:S(2)}, u32[]{:S(2)}) async-start(bf16[16,8,768]{2,1,0:T(8,128)(2,1)} %get-tuple-element.15), calls=%async_computation | async-start | bytes 393216 | tf_op jit(solution)/shard_map/all_to_all | solution.py:168
  84.7 10.7 %copy-start.9 = (s32[8]{0:T(128)S(1)}, s32[8]{0:T(128)}, u32[]{:S(2)}) copy-start(s32[8]{0:T(128)} %param.18) | copy-start | bytes 100
  84.7 13.4 %copy-start.5 = (f32[4608]{0:T(1024)S(1)}, f32[4608]{0:T(1024)}, u32[]{:S(2)}) copy-start(f32[4608]{0:T(1024)} %param.14) | copy-start | bytes 55300
  84.7 13.7 %copy-start.3 = (s32[512,576]{0,1:T(8,128)S(1)}, s32[512,576]{0,1:T(8,128)}, u32[]{:S(2)}) copy-start(s32[512,576]{0,1:T(8,128)} %param.16) | copy-start | bytes 3538948
  87.6 34.6 %all-to-all-start.1 = ((f32[8,16,288]{2,1,0:T(8,128)}), f32[8,16,288]{2,1,0:T(8,128)S(1)}, u32[]{:S(2)}, u32[]{:S(2)}) async-start(f32[8,16,288]{2,1,0:T(8,128)} %copy.64), calls=%async_computation.1 | async-start | bytes 393216 | tf_op jit(solution)/shard_map/all_to_all | solution.py:179
  103.2 9.6 %copy-start.6 = (bf16[512,36]{0,1:T(8,128)(2,1)S(1)}, bf16[512,36]{0,1:T(8,128)(2,1)}, u32[]{:S(2)}) copy-start(bf16[512,36]{0,1:T(8,128)(2,1)} %param.17) | copy-start | bytes 110596
  115.4 31.1 %copy-start.8 = (f32[4608]{0:T(1024)S(1)}, f32[4608]{0:T(1024)}, u32[]{:S(2)}) copy-start(f32[4608]{0:T(1024)} %param.15) | copy-start | bytes 55300
  169.8 37.2 %copy-start.1 = (bf16[128,3840]{1,0:T(8,128)(2,1)}, bf16[128,3840]{1,0:T(8,128)(2,1)S(1)}, u32[]{:S(2)}) copy-start(bf16[128,3840]{1,0:T(8,128)(2,1)S(1)} %all-gather.2.refs_2_) | copy-start | bytes 2949124
  169.8 44.0 %collective-permute-start = (bf16[128,3840]{1,0:T(8,128)(2,1)S(1)}, bf16[128,3840]{1,0:T(8,128)(2,1)S(1)}, u32[]{:S(2)}, u32[]{:S(2)}) collective-permute-start(bf16[128,3840]{1,0:T(8,128)(2,1)S(1)} %all-gather.2.refs_2_), channel_id=1, source_target_pairs={{0,1},{1,0},{2,3},{3,2},{4,5},{5,4},{6,7},{7,6},{8,9},{9,8},{10,11... | collective-permute-start | bytes 2949128 | tf_op jit(solution)/shard_map/ppermute | solution.py:208
  192.1 21.8 %all-to-all-start.2 = ((bf16[16,16,896]{2,1,0:T(8,128)(2,1)}), bf16[16,16,896]{2,1,0:T(8,128)(2,1)S(1)}, u32[]{:S(2)}, u32[]{:S(2)}) async-start(bf16[16,16,896]{2,1,0:T(8,128)(2,1)} %broadcast_in_dim.11), calls=%async_computation.2 | async-start | bytes 917504 | tf_op jit(solution)/shard_map/all_to_all | solution.py:205
  213.8 0.8 copy-start.2
  214.6 1.0 copy-start.4
  231.8 20.1 %all-to-all-start.4 = ((f32[16,6,128]{2,1,0:T(8,128)}), f32[16,6,128]{2,1,0:T(8,128)S(1)}, u32[]{:S(2)}, u32[]{:S(2)}) async-start(f32[16,6,128]{2,1,0:T(8,128)} %broadcast_in_dim.12), calls=%async_computation.4 | async-start | bytes 131072 | tf_op jit(solution)/shard_map/all_to_all | solution.py:18

commit v3 on v2

--- a/solution.py
+++ b/solution.py
@@ -9,7 +9,6 @@
 EPS = 1e-06
 CAP = 30.0
 GATHER_BYTES = 1 << 20
-MXU = 256
 LANES = 128
 
 
@@ -22,7 +21,7 @@
 
 def gather_cut(rows, cols, peers):
     fit = (GATHER_BYTES - 1) // (peers * rows * 2)
-    return min(cols, fit // MXU * MXU)
+    return min(cols, fit // LANES * LANES)
 
 
 def signed_planes(words):
@@ -71,75 +70,65 @@
     )(hidden)
 
 
-def sums_kernel(n_z, pos_ref, mask_ref, head_ref, far_ref, tails_ref, embed_ref, out_ref, st_ref, acc_ref):
-    held, cut = head_ref.shape
-    blocks, per, _ = tails_ref.shape
-    n_s = st_ref.shape[0] // held
-    vocab, dim = embed_ref.shape
-    step = pl.program_id(0)
+def sums_kernel(n_z, pos_ref, mask_ref, heads, tails, embed_ref, out_ref, st_ref, acc_ref):
+    n_s, held, _ = st_ref.shape
+    cut = heads[0].shape[1]
+    dim, vocab = embed_ref.shape
     first, s, z, lead = (pos_ref[i] for i in range(4))
-
-    @pl.when(step == 0)
-    def _():
-        st_ref[pl.ds(pl.multiple_of(s * held, held), held), :cut] = head_ref[...]
-        st_ref[pl.ds(pl.multiple_of((n_s - 1 - s) * held, held), held), :cut] = far_ref[...]
-        for i in range(blocks):
-            row = i % n_s * held + i // n_s * per
-            st_ref[row : row + per, cut:] = tails_ref[i]
-        acc_ref[...] = jnp.zeros_like(acc_ref)
-
-    logits = dot_f32(embed_ref[...], st_ref[:, :dim], ((1,), (1,)))
-    lane = lax.broadcasted_iota(jnp.int32, (8, LANES), 1)
-    pick = jnp.where(
-        lane == 0, 1.0, jnp.where(lane == 1, 256.0, jnp.where(lane == 2, 65536.0, 0.0))
-    )
-    goal = dot_f32(pick.astype(jnp.bfloat16), st_ref[:, dim:], ((1,), (1,))).astype(jnp.int32)
-    capped = CAP * jnp.tanh(logits / CAP)
-    ids = lax.broadcasted_iota(jnp.int32, logits.shape, 0) + (first + step * vocab)
-    acc_ref[0:1] += jnp.sum(jnp.exp(capped), axis=0, keepdims=True)
-    acc_ref[1:2] += jnp.sum(jnp.where(ids == goal[0:1], capped, 0.0), axis=0, keepdims=True)
-
-    @pl.when(step == pl.num_programs(0) - 1)
-    def _():
-        place = lax.broadcasted_iota(jnp.int32, (1, n_s * held), 1)
-        row = jnp.zeros((1, n_s * held), jnp.float32)
-        for i in range(mask_ref.shape[0]):
-            row = jnp.where(
-                place == s * held + i * n_z + z, (mask_ref[i] * lead).astype(jnp.float32), row
+    for h in range(n_s):
+        st_ref[h, :, :cut] = heads[h][...]
+        st_ref[h, :, cut:] = tails[h][...]
+    states = st_ref.reshape(n_s * held, st_ref.shape[2])
+    acc_ref[...] = dot_f32(states[:, :dim], embed_ref[...], ((1,), (0,)))
+    digits = states[:, dim:].astype(jnp.float32)
+    goal = digits[:, 0:1] + 256.0 * digits[:, 1:2] + 65536.0 * digits[:, 2:3]
+    goal = goal.astype(jnp.int32) - first
+    sums = jnp.zeros((n_s * held, LANES), jnp.float32)
+    hits = jnp.zeros((n_s * held, LANES), jnp.float32)
+    for v in range(0, vocab, LANES):
+        capped = CAP * jnp.tanh(acc_ref[:, v : v + LANES] / CAP)
+        ids = lax.broadcasted_iota(jnp.int32, capped.shape, 1) + v
+        sums += jnp.exp(capped)
+        hits += jnp.where(ids == goal, capped, 0.0)
+    rows = [jnp.sum(r.T, axis=0, keepdims=True) for r in (sums, hits)]
+    place = lax.broadcasted_iota(jnp.int32, (1, held), 1)
+    mask = jnp.zeros((1, held), jnp.float32)
+    for i in range(mask_ref.shape[0]):
+        mask = jnp.where(place == i * n_z + z, (mask_ref[i] * lead).astype(jnp.float32), mask)
+    rows.append(jnp.concatenate([mask, jnp.zeros_like(mask)], axis=1))
+    for r, row in enumerate(rows):
+        own, far = row[:, :held], row[:, held:]
+        for h in range(n_s):
+            part = jnp.where(s == h, own, far)
+            out_ref[:, r * n_s + h : r * n_s + h + 1, :] = jnp.broadcast_to(
+                part[None], (out_ref.shape[0], 1, held)
             )
-        acc_ref[2:3] = row
-        for r in range(3):
-            for h in range(n_s):
-                part = acc_ref[r : r + 1, h * held : (h + 1) * held]
-                out_ref[:, r * n_s + h : r * n_s + h + 1, :] = jnp.broadcast_to(
-                    part[None], (out_ref.shape[0], 1, held)
-                )
-
-
-def vocab_sums(pos, mask, head, far, tails, embed, n_z, copies):
-    held, _ = head.shape
-    vocab, dim = embed.shape
-    n_s = tails.shape[0] * tails.shape[1] // held
-    step = min(vocab, MXU)
+
+
+def vocab_sums(pos, mask, heads, tails, embed, n_z, copies):
+    n_s, (held, cut) = len(heads), heads[0].shape
+    dim, vocab = embed.shape
+    def kernel(pos_ref, mask_ref, *refs):
+        sums_kernel(n_z, pos_ref, mask_ref, refs[:n_s], refs[n_s : 2 * n_s], *refs[2 * n_s :])
+
     smem = pl.BlockSpec(memory_space=pltpu.SMEM)
-    whole = lambda a: pl.BlockSpec(a.shape, lambda i: (0,) * a.ndim)
+    vmem = pl.BlockSpec(memory_space=pltpu.VMEM)
     return pl.pallas_call(
-        lambda *refs: sums_kernel(n_z, *refs),
-        grid=(vocab // step,),
-        in_specs=[smem, smem, whole(head), whole(far), whole(tails), pl.BlockSpec((step, dim), lambda i: (i, 0))],
-        out_specs=pl.BlockSpec((copies, 3 * n_s, held), lambda i: (0, 0, 0)),
+        kernel,
+        in_specs=[smem, smem] + [vmem] * (2 * n_s + 1),
         out_shape=jax.ShapeDtypeStruct((copies, 3 * n_s, held), jnp.float32),
         scratch_shapes=[
-            pltpu.VMEM((n_s * held, dim + LANES), jnp.bfloat16),
-            pltpu.VMEM((8, n_s * held), jnp.float32),
+            pltpu.VMEM((n_s, held, cut + tails[0].shape[1]), jnp.bfloat16),
+            pltpu.VMEM((n_s * held, vocab), jnp.float32),
         ],
+        compiler_params=pltpu.CompilerParams(vmem_limit_bytes=24 << 20),
         cost_estimate=pl.CostEstimate(
             flops=2 * n_s * held * vocab * dim,
             bytes_accessed=2 * (n_s * held + vocab) * dim,
             transcendentals=2 * n_s * held * vocab,
         ),
         name="vocab_sums",
-    )(pos, mask, head, far, tails, embed)
+    )(pos, mask, *heads, *tails, embed)
 
 
 def on_device(
@@ -167,9 +156,7 @@
     head, tail = split_columns(hidden, cut, n_z)
     tail = lax.all_to_all(tail, "fsdp", 0, 0, tiled=True)
     head = lax.all_gather(head, "fsdp")
-    head, residual, targets, down_packed, down_scale = lax.optimization_barrier(
-        (head, residual, targets, down_packed, down_scale)
-    )
+    head, residual, targets = lax.optimization_barrier((head, residual, targets))
     weight = dequant_down(down_packed, down_scale)
     part = dot_f32(head.reshape(held, cut), weight[:cut], ((1,), (0,))) + dot_f32(
         tail.reshape(held, width - cut), weight[cut:], ((1,), (0,))
@@ -200,16 +187,19 @@
 
     cut = gather_cut(per_x, dim, n_x)
     tail = jnp.concatenate([states[:, cut:], digits], axis=1)
-    tail = jnp.broadcast_to(tail[None], (n_x * n_s, *tail.shape))
+    tail = jnp.broadcast_to(tail[None], (n_x, *tail.shape))
     head, tail = lax.optimization_barrier((states[:, :cut], tail))
-    tail = lax.all_to_all(tail, ("mp", "sub"), 0, 0, tiled=True)
+    tail = lax.all_to_all(tail, "mp", 0, 0, tiled=True)
     head = lax.all_gather(head, "mp")
-    head = head.reshape(held, cut)
-    far = lax.ppermute(head, "sub", [(i, n_s - 1 - i) for i in range(n_s)])
+    swap = [(i, n_s - 1 - i) for i in range(n_s)]
+    heads = [head.reshape(held, cut)]
+    tails = [tail.reshape(held, dim - cut + LANES)]
+    tails.append(lax.ppermute(tails[0], "sub", swap))
+    heads.append(lax.ppermute(heads[0], "sub", swap))
     embed = dequant_embed(embed_packed, embed_scale)
     first_id = lax.axis_index(("fsdp", "mp", "sub")) * embed.shape[0]
     pos = jnp.stack([first_id, s, z, (x == 0).astype(jnp.int32)])
-    packed = vocab_sums(pos, loss_mask, head, far, tail, embed, n_z, n_x * n_s)
+    packed = vocab_sums(pos, loss_mask, heads, tails, embed.T, n_z, n_x * n_s)
 
     packed = jnp.sum(lax.all_to_all(packed, ("mp", "sub"), 0, 0, tiled=True), axis=0)
     packed = jnp.sum(copy_for_each(packed, "fsdp"), axis=0)

time: 257 us -> 225 us (0.88)
  local copies, waits for them, and re-layouts: 32.3 us -> 6.02 us
  blocking collectives: 90.4 us -> 97.4 us
  other arithmetic: 13.2 us -> 6.3 us
  Pallas kernels: 6.57 us -> 3.76 us
  starting transfers between devices: 88.8 us -> 86.1 us
    shift_left x7 -> x5, local copies, waits for them, and re-layouts: 15.2 us -> 0.69 us  [signed_planes(): lifted = jnp.left_shift(words[:, None, :], shifts)]
    all_to_all x0 -> x1, blocking collectives: none -> 13.4 us  [on_device(): tail = lax.all_to_all(tail, 'mp', 0, 0, tiled=True)]
    mul x2 -> x0, local copies, waits for them, and re-layouts: 9.27 us -> none  [dequant_embed(): grouped = codes.reshape(rows, scales.shape[1], -1) * scales[:, :, None]]
    mul x1, other arithmetic: 9.08 us -> 2.73 us  [dequant_embed(): grouped = codes.reshape(rows, scales.shape[1], -1) * scales[:, :, None]]
    all_to_all x1 -> x0, waiting for transfers between devices: 6.16 us -> none  [on_device(): tail = lax.all_to_all(tail, ('mp', 'sub'), 0, 0, tiled=True)]
    all_to_all x1 -> x0, starting transfers between devices: 5.91 us -> none  [on_device(): tail = lax.all_to_all(tail, ('mp', 'sub'), 0, 0, tiled=True)]
    all_to_all x1, waiting for transfers between devices: 0.01 us -> 5.74 us  [on_device(): ffn = jnp.sum(lax.all_to_all(part, 'mp', 0, 0, tiled=True), axis=0)]
    all_gather x1, blocking collectives: 34.9 us -> 30.1 us  [on_device(): head = lax.all_gather(head, 'fsdp')]
  transfers between devices with their start and end apart: 5 -> 5, of which waited for: 2 -> 2; matrix products, arithmetic and copies ran while one was open for 15% -> 4% of each run, Pallas kernels for 0% -> 0%
where the time goes in v3:
time: 225 us; the launch traced here: 224 us
  blocking collectives  97.4 us (43%)
  starting transfers between devices  86.1 us (38%)
  waiting for transfers between devices  17.2 us (8%)
  other arithmetic  6.3 us (3%)
  local copies, waits for them, and re-layouts  6.02 us (3%)
  between operations  5.36 us (2%)
  Pallas kernels  3.76 us (2%)
    all_to_all x1, starting transfers between devices, on_device(): tail = lax.all_to_all(tail, 'fsdp', 0, 0, tiled=True)  44.2 us
    all_gather x1, blocking collectives, on_device(): head = lax.all_gather(head, 'fsdp')  30.1 us
    all_gather x1, blocking collectives, on_device(): blocks = lax.all_gather(block, 'fsdp')  23.5 us
    ppermute x1, starting transfers between devices, on_device(): heads.append(lax.ppermute(heads[0], 'sub', swap))  23.4 us
    all_gather x1, blocking collectives, on_device(): head = lax.all_gather(head, 'mp')  20 us
    all_to_all x1, blocking collectives, on_device(): tail = lax.all_to_all(tail, 'mp', 0, 0, tiled=True)  13.4 us
    all_to_all x1, waiting for transfers between devices, copy_for_each(): lax.all_to_all(jnp.broadcast_to(value[None], (peers, *value.shape)), axis...  11.4 us
    all_to_all x1, blocking collectives, on_device(): lax.all_to_all(packed, ('mp', 'sub'), 0, 0, tiled=True)  10.3 us
  transfers between devices with their start and end apart: 5, of which 2 were waited for; matrix products, arithmetic and copies ran while one was open for 4% of the time, Pallas kernels for 0%

profile of v3, /device:TPU:65, one launch (start us, length us, event | category | flops | bytes accessed | tf_op | source)
XLA Modules:
  0.0 223.6 jit_solution(12158571317891917034)
XLA Ops:
  0.7 1.6 split_columns.1
  2.3 44.2 %all-to-all-start = ((bf16[16,8,640]{2,1,0:T(8,128)(2,1)}), bf16[16,8,640]{2,1,0:T(8,128)(2,1)S(1)}, u32[]{:S(2)}, u32[]{:S(2)}) async-start(bf16[16,8,640]{2,1,0:T(8,128)(2,1)} %get-tuple-element.11), calls=%async_computation | async-start | bytes 327680 | tf_op jit(solution)/shard_map/all_to_all | solution.py:157
  46.5 0.1 shift_left.44
  46.6 1.4 copy.49
  48.0 0.5 shift_left.41
  48.5 1.3 fusion.5
  49.8 0.5 slice.51
  50.3 0.1 slice.52
  50.4 30.1 %all-gather = bf16[128,3968]{1,0:T(8,128)(2,1)S(1)} all-gather(bf16[8,3968]{1,0:T(8,128)(2,1)S(1)} %copy-done.3), channel_id=2, replica_groups=mesh['groups'=2,'fsdp'=16,'mp'=8,'sub'=2] {'fsdp'}, dimensions={0}, use_global_device_ids=true | all-gather | bytes 1079296 | tf_op jit(solution)/shard_map/all_gather | solution.py:158
  80.5 1.2 fusion.7
  81.7 0.3 fusion.6
  82.1 0.1 copy.51
  82.2 0.7 copy.52
  82.9 7.1 %all-to-all-start.1 = ((f32[8,16,288]{2,1,0:T(8,128)}), f32[8,16,288]{2,1,0:T(8,128)S(1)}, u32[]{:S(2)}, u32[]{:S(2)}) async-start(f32[8,16,288]{2,1,0:T(8,128)} %copy.52), calls=%async_computation.1 | async-start | bytes 393216 | tf_op jit(solution)/shard_map/all_to_all | solution.py:166
  90.0 0.6 dynamic_slice.7
  92.5 0.1 dynamic-slice_reduce_fusion
  92.6 0.1 reshape.158
  92.7 0.1 mul.106
  92.8 0.1 select_maximum_fusion
  92.9 5.7 %all-to-all-done.1 = f32[8,16,288]{2,1,0:T(8,128)S(1)} async-done(((f32[8,16,288]{2,1,0:T(8,128)}), f32[8,16,288]{2,1,0:T(8,128)S(1)}, u32[]{:S(2)}, u32[]{:S(2)}) %all-to-all-start.1) | async-done | bytes 147488 | tf_op jit(solution)/shard_map/all_to_all | solution.py:166
  98.6 0.1 pad_maximum_fusion
  98.7 23.5 %all-gather.1 = bf16[768,384]{1,0:T(8,128)(2,1)S(1)} all-gather(bf16[48,384]{1,0:T(8,128)(2,1)S(1)} %pad_maximum_fusion), channel_id=3, replica_groups=mesh['groups'=2,'fsdp'=16,'mp'=8,'sub'=2] {'fsdp'}, dimensions={0}, use_global_device_ids=true | all-gather | bytes 626688 | tf_op jit(solution)/shard_map/all_gather | solution.py:175
  122.3 0.2 multiply_reduce_fusion.1
  122.5 0.1 slice.58
  122.7 0.3 multiply_reduce_fusion
  123.0 0.1 copy.54
  123.1 0.2 reshape.159
  123.3 0.1 copy.55
  123.4 0.2 reshape.160
  123.6 0.1 multiply_convert_fusion
  123.8 0.1 copy.56
  123.9 0.1 copy.57
  124.0 20.0 %all-gather.2.refs_0_ = bf16[128,3968]{1,0:T(8,128)(2,1)S(1)} all-gather(bf16[16,3968]{1,0:T(8,128)(2,1)S(1)} %slice.56), channel_id=4, replica_groups=mesh['groups'=2,'fsdp'=16,'mp'=8,'sub'=2] {'mp'}, dimensions={0}, use_global_device_ids=true | all-gather | bytes 1142784 | tf_op jit(solution)/shard_map/all_gather | solution.py:193
  144.0 23.4 %collective-permute-start = (bf16[128,3968]{1,0:T(8,128)(2,1)S(1)}, bf16[128,3968]{1,0:T(8,128)(2,1)S(1)}, u32[]{:S(2)}, u32[]{:S(2)}) collective-permute-start(bf16[128,3968]{1,0:T(8,128)(2,1)S(1)} %all-gather.2.refs_0_), channel_id=1, source_target_pairs={{0,1},{1,0},{2,3},{3,2},{4,5},{5,4},{6,7},{7,6},{8,9},{9,8},{10,11... | collective-permute-start | bytes 3047432 | tf_op jit(solution)/shard_map/ppermute | solution.py:198
  167.5 13.4 %all_to_all.25 = bf16[8,16,768]{2,1,0:T(8,128)(2,1)S(1)} all-to-all(bf16[8,16,768]{2,1,0:T(8,128)(2,1)S(1)} %broadcast_in_dim.11), channel_id=1, replica_groups=mesh['groups'=2,'fsdp'=16,'mp'=8,'sub'=2] {'mp'}, dimensions={0} | all-to-all | bytes 393216 | tf_op jit(solution)/shard_map/all_to_all | solution.py:192
  180.9 2.4 %collective-permute-start.1 = (bf16[128,768]{1,0:T(8,128)(2,1)S(1)}, bf16[128,768]{1,0:T(8,128)(2,1)S(1)}, u32[]{:S(2)}, u32[]{:S(2)}) collective-permute-start(bf16[128,768]{1,0:T(8,128)(2,1)S(1)} %bitcast.56), channel_id=1, source_target_pairs={{0,1},{1,0},{2,3},{3,2},{4,5},{5,4},{6,7},{7,6},{8,9},{9,8},{10,11... | collective-permute-start | bytes 589832 | tf_op jit(solution)/shard_map/ppermute | solution.py:197
  183.3 0.1 shift_left.49
  183.4 0.1 shift_left.50
  183.5 2.7 %fusion.4 = bf16[512,4608]{0,1:T(8,128)(2,1)S(1)} fusion(s32[4608]{0:T(1024)S(1)} %shift_left.50, s32[512,576]{0,1:T(8,128)} %param.16, bf16[512,36]{0,1:T(8,128)(2,1)S(1)} %copy-done.4), kind=kLoop, calls=%fused_computation.6 | loop fusion | flops 16515072 | bytes 5953536 | tf_op jit(solution)/shard_map/mul | solution.py:43
  186.2 0.1 pad_add_fusion.pos_ref
  186.3 2.2 vocab_sums.1
  188.4 10.3 %all_to_all.26 = f32[16,6,128]{2,1,0:T(8,128)S(1)} all-to-all(f32[16,6,128]{2,1,0:T(8,128)S(1)} %vocab_sums.1), channel_id=1, replica_groups=mesh['groups'=2,'fsdp'=16,'mp'=8,'sub'=2] {'mp','sub'}, dimensions={0} | all-to-all | bytes 98304 | tf_op jit(solution)/shard_map/all_to_all | solution.py:204
  198.8 0.6 broadcast_in_dim.12
  199.4 8.9 %all-to-all-start.4 = ((f32[16,6,128]{2,1,0:T(8,128)}), f32[16,6,128]{2,1,0:T(8,128)S(1)}, u32[]{:S(2)}, u32[]{:S(2)}) async-start(f32[16,6,128]{2,1,0:T(8,128)} %broadcast_in_dim.12), calls=%async_computation.4 | async-start | bytes 131072 | tf_op jit(solution)/shard_map/all_to_all | solution.py:17
  208.4 11.4 %all-to-all-done.4 = f32[16,6,128]{2,1,0:T(8,128)S(1)} async-done(((f32[16,6,128]{2,1,0:T(8,128)}), f32[16,6,128]{2,1,0:T(8,128)S(1)}, u32[]{:S(2)}, u32[]{:S(2)}) %all-to-all-start.4) | async-done | bytes 49184 | tf_op jit(solution)/shard_map/all_to_all | solution.py:17
  219.8 0.6 fusion.19
  220.4 0.1 select_n.31
  221.8 0.6 select_reduce_fusion
  (36 shorter events, 0.3 us)
Async XLA Ops:
  0.6 91.9 %copy-start = (bf16[8,4608]{1,0:T(8,128)(2,1)S(1)}, bf16[8,4608]{1,0:T(8,128)(2,1)}, u32[]{:S(2)}) copy-start(bf16[8,4608]{1,0:T(8,128)(2,1)} %param.11) | copy-start | bytes 221188
  0.6 47.9 %copy-start.5 = (bf16[36,288]{1,0:T(8,128)(2,1)S(1)}, bf16[36,288]{1,0:T(8,128)(2,1)}, u32[]{:S(2)}) copy-start(bf16[36,288]{1,0:T(8,128)(2,1)} %param.13) | copy-start | bytes 62212
  2.3 79.5 %all-to-all-start = ((bf16[16,8,640]{2,1,0:T(8,128)(2,1)}), bf16[16,8,640]{2,1,0:T(8,128)(2,1)S(1)}, u32[]{:S(2)}, u32[]{:S(2)}) async-start(bf16[16,8,640]{2,1,0:T(8,128)(2,1)} %get-tuple-element.11), calls=%async_computation | async-start | bytes 327680 | tf_op jit(solution)/shard_map/all_to_all | solution.py:157
  48.5 1.9 copy-start.3
  49.8 40.2 %copy-start.7 = (s32[8]{0:T(128)S(1)}, s32[8]{0:T(128)}, u32[]{:S(2)}) copy-start(s32[8]{0:T(128)} %param.18) | copy-start | bytes 100
  49.8 42.9 %copy-start.2 = (f32[4608]{0:T(1024)S(1)}, f32[4608]{0:T(1024)}, u32[]{:S(2)}) copy-start(f32[4608]{0:T(1024)} %param.14) | copy-start | bytes 55300
  50.4 73.2 %copy-start.6 = (f32[4608]{0:T(1024)S(1)}, f32[4608]{0:T(1024)}, u32[]{:S(2)}) copy-start(f32[4608]{0:T(1024)} %param.15) | copy-start | bytes 55300
  80.5 102.9 %copy-start.4 = (bf16[512,36]{0,1:T(8,128)(2,1)S(1)}, bf16[512,36]{0,1:T(8,128)(2,1)}, u32[]{:S(2)}) copy-start(bf16[512,36]{0,1:T(8,128)(2,1)} %param.17) | copy-start | bytes 110596
  82.9 15.7 %all-to-all-start.1 = ((f32[8,16,288]{2,1,0:T(8,128)}), f32[8,16,288]{2,1,0:T(8,128)S(1)}, u32[]{:S(2)}, u32[]{:S(2)}) async-start(f32[8,16,288]{2,1,0:T(8,128)} %copy.52), calls=%async_computation.1 | async-start | bytes 393216 | tf_op jit(solution)/shard_map/all_to_all | solution.py:166
  122.3 64.0 %copy-start.1 = (s32[8]{0:T(128)S(1)}, s32[8]{0:T(128)}, u32[]{:S(2)}) copy-start(s32[8]{0:T(128)} %mask_ref.1) | copy-start | bytes 100
  144.0 42.2 %collective-permute-start = (bf16[128,3968]{1,0:T(8,128)(2,1)S(1)}, bf16[128,3968]{1,0:T(8,128)(2,1)S(1)}, u32[]{:S(2)}, u32[]{:S(2)}) collective-permute-start(bf16[128,3968]{1,0:T(8,128)(2,1)S(1)} %all-gather.2.refs_0_), channel_id=1, source_target_pairs={{0,1},{1,0},{2,3},{3,2},{4,5},{5,4},{6,7},{7,6},{8,9},{9,8},{10,11... | collective-permute-start | bytes 3047432 | tf_op jit(solution)/shard_map/ppermute | solution.py:198
  180.9 5.4 %collective-permute-start.1 = (bf16[128,768]{1,0:T(8,128)(2,1)S(1)}, bf16[128,768]{1,0:T(8,128)(2,1)S(1)}, u32[]{:S(2)}, u32[]{:S(2)}) collective-permute-start(bf16[128,768]{1,0:T(8,128)(2,1)S(1)} %bitcast.56), channel_id=1, source_target_pairs={{0,1},{1,0},{2,3},{3,2},{4,5},{5,4},{6,7},{7,6},{8,9},{9,8},{10,11... | collective-permute-start | bytes 589832 | tf_op jit(solution)/shard_map/ppermute | solution.py:197
  199.4 20.4 %all-to-all-start.4 = ((f32[16,6,128]{2,1,0:T(8,128)}), f32[16,6,128]{2,1,0:T(8,128)S(1)}, u32[]{:S(2)}, u32[]{:S(2)}) async-start(f32[16,6,128]{2,1,0:T(8,128)} %broadcast_in_dim.12), calls=%async_computation.4 | async-start | bytes 131072 | tf_op jit(solution)/shard_map/all_to_all | solution.py:17

commit v4 on v3

v4 whole, which is shorter than its diff:
```python
import functools

import jax
import jax.numpy as jnp
from jax import lax
from jax.experimental import pallas as pl
from jax.experimental.pallas import tpu as pltpu
from jax.sharding import PartitionSpec as P


EPS = 1e-06
CAP = 30.0
GATHER_BYTES = 1 << 20
LANES = 128
VMEM = pl.BlockSpec(memory_space=pltpu.VMEM)
SMEM = pl.BlockSpec(memory_space=pltpu.SMEM)


def copy_for_each(value, axis):
    peers = lax.axis_size(axis)
    return lax.all_to_all(
        jnp.broadcast_to(value[None], (peers, *value.shape)), axis, 0, 0, tiled=True
    )


def rings(axis):
    n, n_s = lax.axis_size(axis), lax.axis_size("sub")
    return [[i * n_s + (i + r) % n_s for i in range(n)] for r in range(n_s)]


def gather_ring(value, axis):
    return lax.all_gather(value, (axis, "sub"), axis_index_groups=rings(axis))


def exchange_ring(copies, axis):
    return lax.all_to_all(
        copies, (axis, "sub"), 0, 0, tiled=True, axis_index_groups=rings(axis)
    )


def gather_cut(rows, cols, peers):
    fit = (GATHER_BYTES - 1) // (peers * rows * 2)
    return min(cols, fit // LANES * LANES)


def signed_planes(words):
    shifts = (28 - 4 * jnp.arange(8, dtype=jnp.int32))[None, :, None]
    lifted = jnp.left_shift(words[:, None, :], shifts)
    return jnp.right_shift(lifted, 28)


def dequant_down(words, scales):
    cols = words.shape[1]
    codes = signed_planes(words).astype(jnp.bfloat16)
    grouped = codes.reshape(scales.shape[0], -1, cols) * scales[:, None, :]
    return grouped.reshape(-1, cols)


def dequant_embed(words, scales):
    rows = words.shape[0]
    codes = signed_planes(words).astype(jnp.bfloat16)
    grouped = codes.reshape(rows, scales.shape[1], -1) * scales[:, :, None]
    return grouped.reshape(rows, -1)


def dot_f32(a, b, dims):
    return lax.dot_general(a, b, (dims, ((), ())), preferred_element_type=jnp.float32)


def split_kernel(hidden_ref, head_ref, tail_ref):
    cut = head_ref.shape[1]
    head_ref[...] = hidden_ref[:, :cut]
    tail_ref[...] = jnp.broadcast_to(hidden_ref[:, cut:][None], tail_ref.shape)


def split_columns(hidden, cut, copies):
    rows, width = hidden.shape
    return pl.pallas_call(
        split_kernel,
        out_shape=(
            jax.ShapeDtypeStruct((rows, cut), hidden.dtype),
            jax.ShapeDtypeStruct((copies, rows, width - cut), hidden.dtype),
        ),
        in_specs=[VMEM],
        compiler_params=pltpu.CompilerParams(vmem_limit_bytes=4 << 20),
        name="split_columns",
    )(hidden)


def pack_kernel(targets_ref, parts_ref, residual_ref, out_ref):
    per, cols = parts_ref.shape[1:]
    width = out_ref.shape[1]
    ffn = jnp.sum(parts_ref[...], axis=0)
    high = ffn.astype(jnp.bfloat16)
    out_ref[...] = jnp.zeros_like(out_ref)
    out_ref[:per, :cols] = high
    out_ref[per : 2 * per, :cols] = (ffn - high.astype(jnp.float32)).astype(jnp.bfloat16)
    x = lax.axis_index("mp")
    res = residual_ref[...].astype(jnp.float32)
    token = lax.broadcasted_iota(jnp.int32, res.shape, 0)
    res = jnp.sum(jnp.where(token == x, res, 0.0), axis=0, keepdims=True)
    rows = [res[:, c : c + width] for c in range(0, res.shape[1], width)]
    goal = targets_ref[x]
    lane = lax.broadcasted_iota(jnp.int32, (1, width), 1)
    digit = jnp.where(
        lane == 0, goal & 255, jnp.where(lane == 1, (goal >> 8) & 255, jnp.where(lane == 2, goal >> 16, 0))
    )
    rows.append(digit.astype(jnp.float32))
    rows.append(jnp.zeros((out_ref.shape[0] - 2 * per - len(rows), width), jnp.float32))
    out_ref[2 * per :] = jnp.concatenate(rows, axis=0).astype(jnp.bfloat16)


def pack_rows(targets, parts, residual):
    per, cols = parts.shape[1:]
    width = cols + -cols % LANES
    count = 2 * per + residual.shape[1] // width + 1
    return pl.pallas_call(
        pack_kernel,
        in_specs=[SMEM, VMEM, VMEM],
        out_shape=jax.ShapeDtypeStruct((count + -count % 16, width), jnp.bfloat16),
        compiler_params=pltpu.CompilerParams(vmem_limit_bytes=4 << 20),
        name="pack_rows",
    )(targets, parts, residual)


def norm_kernel(blocks_ref, post_ref, final_ref, head_ref, tail_ref, turn_ref):
    n_z = blocks_ref.shape[0]
    per, cut = head_ref.shape
    dim = post_ref.shape[1]
    cols = dim // n_z
    rest, width = turn_ref.shape[1] // n_z, blocks_ref.shape[2]
    f32 = jnp.float32
    ffn = jnp.concatenate(
        [
            blocks_ref[i, :per, :cols].astype(f32) + blocks_ref[i, per : 2 * per, :cols].astype(f32)
            for i in range(n_z)
        ],
        axis=1,
    )
    for i in range(n_z):
        for c in range(width // LANES):
            turn_ref[c, i * rest : (i + 1) * rest] = blocks_ref[
                i, 2 * per :, c * LANES : (c + 1) * LANES
            ].astype(f32)

    def turned(r, c):
        return turn_ref[c, pl.ds(r, n_z, stride=rest), :]

    res = jnp.concatenate(
        [turned(r, c) for r in range(dim // width) for c in range(width // LANES)], axis=1
    )
    scale = lax.rsqrt(jnp.sum(ffn * ffn, axis=1, keepdims=True) / dim + EPS)
    stream = res + ffn * scale * post_ref[...]
    scale = lax.rsqrt(jnp.sum(stream * stream, axis=1, keepdims=True) / dim + EPS)
    states = (stream * scale * final_ref[...]).astype(jnp.bfloat16)
    head_ref[...] = states[:, :cut]
    tail = jnp.concatenate([states[:, cut:], turned(dim // width, 0).astype(jnp.bfloat16)], axis=1)
    tail_ref[...] = jnp.broadcast_to(tail[None], tail_ref.shape)


def norm_rows(blocks, post_gain, final_gain, per, cut, copies):
    n_z, rows, width = blocks.shape
    dim = post_gain.shape[0]
    return pl.pallas_call(
        norm_kernel,
        in_specs=[VMEM] * 3,
        out_shape=(
            jax.ShapeDtypeStruct((per, cut), blocks.dtype),
            jax.ShapeDtypeStruct((copies, per, dim - cut + LANES), blocks.dtype),
        ),
        scratch_shapes=[pltpu.VMEM((width // LANES, n_z * (rows - 2 * per), LANES), jnp.float32)],
        compiler_params=pltpu.CompilerParams(vmem_limit_bytes=8 << 20),
        name="norm_rows",
    )(blocks, post_gain[None], final_gain[None])


def sums_kernel(n_z, mask_ref, heads, tails, embed_ref, out_ref, st_ref, acc_ref):
    n_s, held, _ = st_ref.shape
    cut = heads[0].shape[1]
    dim, vocab = embed_ref.shape
    z, x, s = (lax.axis_index(a) for a in ("fsdp", "mp", "sub"))
    first = ((z * lax.axis_size("mp") + x) * n_s + s) * vocab
    lead = jnp.where(x == 0, 1, 0)
    for h in range(n_s):
        st_ref[h, :, :cut] = heads[h][...]
        st_ref[h, :, cut:] = tails[h][...]
    states = st_ref.reshape(n_s * held, st_ref.shape[2])
    acc_ref[...] = dot_f32(states[:, :dim], embed_ref[...], ((1,), (0,)))
    digits = states[:, dim:].astype(jnp.float32)
    goal = digits[:, 0:1] + 256.0 * digits[:, 1:2] + 65536.0 * digits[:, 2:3]
    goal = goal.astype(jnp.int32) - first
    sums = jnp.zeros((n_s * held, LANES), jnp.float32)
    hits = jnp.zeros((n_s * held, LANES), jnp.float32)
    for v in range(0, vocab, LANES):
        capped = CAP * jnp.tanh(acc_ref[:, v : v + LANES] / CAP)
        ids = lax.broadcasted_iota(jnp.int32, capped.shape, 1) + v
        sums += jnp.exp(capped)
        hits += jnp.where(ids == goal, capped, 0.0)
    rows = [jnp.sum(r.T, axis=0, keepdims=True) for r in (sums, hits)]
    place = lax.broadcasted_iota(jnp.int32, (1, held), 1)
    core = (place + place // n_z + z + x + s) % n_s
    mask = jnp.zeros((1, held), jnp.float32)
    for i in range(mask_ref.shape[0]):
        mask = jnp.where(place == i * n_z + z, (mask_ref[i] * lead).astype(jnp.float32), mask)
    parts = [
        jnp.where(core == h, row[:, :held], row[:, held:]) for row in rows for h in range(n_s)
    ] + [jnp.where(s == h, mask, 0.0) for h in range(n_s)]
    for r, part in enumerate(parts):
        out_ref[:, r : r + 1, :] = jnp.broadcast_to(part[None], (out_ref.shape[0], 1, held))


def vocab_sums(mask, heads, tails, embed, n_z, copies):
    n_s, (held, cut) = len(heads), heads[0].shape
    dim, vocab = embed.shape

    def kernel(mask_ref, *refs):
        sums_kernel(n_z, mask_ref, refs[:n_s], refs[n_s : 2 * n_s], *refs[2 * n_s :])

    return pl.pallas_call(
        kernel,
        in_specs=[SMEM] + [VMEM] * (2 * n_s + 1),
        out_shape=jax.ShapeDtypeStruct((copies, 3 * n_s, held), jnp.float32),
        scratch_shapes=[
            pltpu.VMEM((n_s, held, cut + tails[0].shape[1]), jnp.bfloat16),
            pltpu.VMEM((n_s * held, vocab), jnp.float32),
        ],
        compiler_params=pltpu.CompilerParams(vmem_limit_bytes=24 << 20),
        cost_estimate=pl.CostEstimate(
            flops=2 * n_s * held * vocab * dim,
            bytes_accessed=2 * (n_s * held + vocab) * dim,
            transcendentals=2 * n_s * held * vocab,
        ),
        name="vocab_sums",
    )(mask, *heads, *tails, embed)


def loss_kernel(n_z, packed_ref, token_ref, mean_ref):
    toks = token_ref.shape[0]
    n_s, held = packed_ref.shape[1] // 3, packed_ref.shape[2]
    z, s = lax.axis_index("fsdp"), lax.axis_index("sub")
    packed = jnp.sum(packed_ref[...], axis=0)
    sums, goals, mask = (packed[r * n_s : (r + 1) * n_s] for r in range(3))
    losses = mask * (jnp.log(sums) - goals)
    total, count = jnp.sum(losses), jnp.sum(mask)
    whole = jnp.full((1, held), total) / jnp.maximum(jnp.full((1, held), count), 1.0)
    mean_ref[...] = whole[0, :1]
    core = lax.broadcasted_iota(jnp.int32, losses.shape, 0)
    mine = jnp.sum(jnp.where(core == s, losses, 0.0), axis=0, keepdims=True)
    row = lax.broadcasted_iota(jnp.int32, (held, held), 0)
    lane = lax.broadcasted_iota(jnp.int32, (held, held), 1)
    spread = jnp.where((lane == row * n_z + z) & (row < toks), mine, 0.0)
    token_ref[...] = jnp.sum(spread.T, axis=0)[:toks]


def losses_of(packed, n_z, toks):
    return pl.pallas_call(
        functools.partial(loss_kernel, n_z),
        in_specs=[VMEM],
        out_shape=(
            jax.ShapeDtypeStruct((toks,), jnp.float32),
            jax.ShapeDtypeStruct((1,), jnp.float32),
        ),
        compiler_params=pltpu.CompilerParams(vmem_limit_bytes=4 << 20),
        name="losses_of",
    )(packed)


def on_device(
    hidden,
    residual,
    down_packed,
    down_scale,
    post_gain,
    final_gain,
    embed_packed,
    embed_scale,
    targets,
    loss_mask,
):
    toks, width = hidden.shape
    n_z, n_x, n_s = (lax.axis_size(a) for a in ("fsdp", "mp", "sub"))
    cols = down_packed.shape[1]
    dim = n_z * cols
    held = n_z * toks
    per_x = held // n_x

    cut = gather_cut(toks, width, n_z)
    head, tail = split_columns(hidden, cut, n_z)
    tail = exchange_ring(tail, "fsdp")
    head = gather_ring(head, "fsdp")
    weight = dequant_down(down_packed, down_scale)
    part = dot_f32(head.reshape(held, cut), weight[:cut], ((1,), (0,))) + dot_f32(
        tail.reshape(held, width - cut), weight[cut:], ((1,), (0,))
    )

    part = jnp.swapaxes(part.reshape(n_z, toks, cols), 0, 1).reshape(n_x, per_x, cols)
    parts = lax.all_to_all(part, "mp", 0, 0, tiled=True)
    parts, residual, targets = lax.optimization_barrier((parts, residual, targets))

    block = pack_rows(targets, parts, residual)
    blocks = gather_ring(block, "fsdp")
    blocks, post_gain, final_gain = lax.optimization_barrier((blocks, post_gain, final_gain))

    cut = gather_cut(per_x, dim, n_x)
    head, tail = norm_rows(blocks, post_gain, final_gain, per_x, cut, n_x)
    tail = exchange_ring(tail, "mp")
    head = gather_ring(head, "mp")
    swap = [(i, n_s - 1 - i) for i in range(n_s)]
    heads = [head.reshape(held, cut)]
    tails = [tail.reshape(held, dim - cut + LANES)]
    tails.append(lax.ppermute(tails[0], "sub", swap))
    heads.append(lax.ppermute(heads[0], "sub", swap))
    embed = dequant_embed(embed_packed, embed_scale)
    packed = vocab_sums(loss_mask, heads, tails, embed.T, n_z, n_x * n_s)

    packed = jnp.sum(lax.all_to_all(packed, ("mp", "sub"), 0, 0, tiled=True), axis=0)
    return losses_of(copy_for_each(packed, "fsdp"), n_z, toks)


def solution(mesh):
    return jax.shard_map(
        on_device,
        mesh=mesh,
        in_specs=(
            P(("groups", "fsdp", "sub"), "mp"),
            P(("groups", "fsdp", "sub"), None),
            P("mp", "fsdp"),
            P("mp", "fsdp"),
            P(),
            P(),
            P(("fsdp", "mp", "sub"), None),
            P(("fsdp", "mp", "sub"), None),
            P(("groups", "fsdp", "sub")),
            P(("groups", "fsdp", "sub")),
        ),
        out_specs=(P(("groups", "fsdp", "sub")), P("groups")),
        check_vma=False,
    )
```

time: 225 us -> 213 us (0.947)
  blocking collectives: 97.4 us -> 147 us
  starting transfers between devices: 86.1 us -> 50.1 us
  waiting for transfers between devices: 17.2 us -> 0.01 us
  between operations: 5.36 us -> 0.87 us
  other arithmetic: 6.3 us -> 4.03 us
    all_to_all x1 -> x3, blocking collectives: 13.4 us -> 50.9 us  [the longest x1 20.7 us: copy_for_each(): lax.all_to_all(jnp.broadcast_to(value[None], (peers, *value.shape)), axis...]
    ppermute x1, starting transfers between devices: 23.4 us -> 2.15 us  [on_device(): heads.append(lax.ppermute(heads[0], 'sub', swap))]
    all_to_all x3 -> x1, waiting for transfers between devices: 17.2 us -> 0.01 us  [exchange_ring(): lax.all_to_all(copies, (axis, 'sub'), 0, 0, tiled=True, axis_index_groups...]
    all_to_all x3 -> x1, starting transfers between devices: 60.2 us -> 44.7 us  [exchange_ring(): lax.all_to_all(copies, (axis, 'sub'), 0, 0, tiled=True, axis_index_groups...]
    all_gather x3, blocking collectives: 73.7 us -> 86.3 us  [gather_ring(): return lax.all_gather(value, (axis, 'sub'), axis_index_groups=rings(axis))]
  transfers between devices with their start and end apart: 5 -> 3, of which waited for: 2 -> 0; matrix products, arithmetic and copies ran while one was open for 4% -> 4% of each run, Pallas kernels for 0% -> 0%
where the time goes in v4:
time: 213 us; the launch traced here: 212 us
  blocking collectives  147 us (69%)
  starting transfers between devices  50.1 us (24%)
  Pallas kernels  4.52 us (2%)
  other arithmetic  4.03 us (2%)
  local copies, waits for them, and re-layouts  3.78 us (2%)
    all_gather x3, blocking collectives, gather_ring(): return lax.all_gather(value, (axis, 'sub'), axis_index_groups=rings(axis))  86.3 us
    all_to_all x1, starting transfers between devices, exchange_ring(): lax.all_to_all(copies, (axis, 'sub'), 0, 0, tiled=True, axis_index_groups...  44.7 us
    all_to_all x1, blocking collectives, copy_for_each(): lax.all_to_all(jnp.broadcast_to(value[None], (peers, *value.shape)), axis...  20.7 us
    all_to_all x1, blocking collectives, on_device(): parts = lax.all_to_all(part, 'mp', 0, 0, tiled=True)  16.7 us
    all_to_all x1, blocking collectives, exchange_ring(): lax.all_to_all(copies, (axis, 'sub'), 0, 0, tiled=True, axis_index_groups...  13.6 us
    all_to_all x1, blocking collectives, on_device(): lax.all_to_all(packed, ('mp', 'sub'), 0, 0, tiled=True)  10.3 us
  transfers between devices with their start and end apart: 3, of which 0 were waited for; matrix products, arithmetic and copies ran while one was open for 4% of the time, Pallas kernels for 0%

profile of v4, /device:TPU:65, one launch (start us, length us, event | category | flops | bytes accessed | tf_op | source)
XLA Modules:
  0.0 212.2 jit_solution(1335807063923560541)
XLA Ops:
  0.6 0.0 copy-start
  0.6 0.9 copy-done
  1.5 0.0 copy-start.5
  1.5 0.7 split_columns.1
  2.2 44.7 %all-to-all-start = ((bf16[16,8,640]{2,1,0:T(8,128)(2,1)}), bf16[16,8,640]{2,1,0:T(8,128)(2,1)S(1)}, u32[]{:S(2)}, u32[]{:S(2)}) async-start(bf16[16,8,640]{2,1,0:T(8,128)(2,1)} %get-tuple-element.13), calls=%async_computation | async-start | bytes 327680 | tf_op jit(solution)/shard_map/all_to_all | solution.py:36
  46.9 0.1 shift_left.44
  47.0 1.4 copy.19
  48.5 0.5 shift_left.41
  48.9 0.0 copy-done.5
  48.9 1.3 fusion.5
  50.2 0.0 copy-start.1
  50.2 0.0 copy-start.2
  50.2 0.0 copy-start.6
  50.3 0.0 copy-start.7
  50.3 0.5 slice.16
  50.8 0.0 copy-start.4
  50.8 0.1 slice.17
  50.8 34.7 %all-gather = bf16[128,3968]{1,0:T(8,128)(2,1)S(1)} all-gather(bf16[8,3968]{1,0:T(8,128)(2,1)S(1)} %get-tuple-element.12), channel_id=2, replica_groups={{0,17,32,49,64,81,96,113,128,145,160,177,192,209,224,241},{1,16,33,48,6..., dimensions={0}, use_global_device_ids=true | all-gather | bytes 1079296 | tf_op jit(solution)/shard_map/all_gather | solution.py:32
  85.5 0.0 copy-start.3
  85.5 1.1 fusion.8
  86.6 0.0 all-to-all-done
  86.6 0.3 fusion.6
  86.9 0.1 copy.21
  87.1 16.7 %all_to_all.25.parts_ref = f32[8,16,288]{2,1,0:T(8,128)S(1)} all-to-all(f32[8,16,288]{2,1,0:T(8,128)S(1)} %bitcast.43), channel_id=1, replica_groups=mesh['groups'=2,'fsdp'=16,'mp'=8,'sub'=2] {'mp'}, dimensions={0} | all-to-all | bytes 294912 | tf_op jit(solution)/shard_map/all_to_all | solution.py:297
  103.8 0.0 copy-done.1
  103.8 0.0 copy-done.2
  103.8 0.6 pack_rows.1
  104.4 28.1 %all-gather.1 = bf16[768,384]{1,0:T(8,128)(2,1)S(1)} all-gather(bf16[48,384]{1,0:T(8,128)(2,1)S(1)} %pack_rows.1), channel_id=3, replica_groups={{0,17,32,49,64,81,96,113,128,145,160,177,192,209,224,241},{1,16,33,48,6..., dimensions={0}, use_global_device_ids=true | all-gather | bytes 626688 | tf_op jit(solution)/shard_map/all_gather | solution.py:32
  132.5 0.0 copy-done.6
  132.5 0.0 copy-done.7
  132.5 0.4 norm_rows.1
  132.9 23.5 %all-gather.2.refs_0_ = bf16[128,3968]{1,0:T(8,128)(2,1)S(1)} all-gather(bf16[16,3968]{1,0:T(8,128)(2,1)S(1)} %get-tuple-element.20), channel_id=4, replica_groups={{0,3,4,7,8,11,12,15},{1,2,5,6,9,10,13,14},{16,19,20,23,24,27,28,31},{17..., dimensions={0}, use_global_device_ids=true | all-gather | bytes 1142784 | tf_op jit(solution)/shard_map/all_gather | solution.py:32
  156.4 2.1 %collective-permute-start = (bf16[128,3968]{1,0:T(8,128)(2,1)S(1)}, bf16[128,3968]{1,0:T(8,128)(2,1)S(1)}, u32[]{:S(2)}, u32[]{:S(2)}) collective-permute-start(bf16[128,3968]{1,0:T(8,128)(2,1)S(1)} %all-gather.2.refs_0_), channel_id=1, source_target_pairs={{0,1},{1,0},{2,3},{3,2},{4,5},{5,4},{6,7},{7,6},{8,9},{9,8},{10,11... | collective-permute-start | bytes 3047432 | tf_op jit(solution)/shard_map/ppermute | solution.py:312
  158.6 13.6 %all_to_all.26 = bf16[8,16,768]{2,1,0:T(8,128)(2,1)S(1)} all-to-all(bf16[8,16,768]{2,1,0:T(8,128)(2,1)S(1)} %get-tuple-element.21), channel_id=1, replica_groups={{0,3,4,7,8,11,12,15},{1,2,5,6,9,10,13,14},{16,19,20,23,24,27,28,31},{17..., dimensions={0} | all-to-all | bytes 393216 | tf_op jit(solution)/shard_map/all_to_all | solution.py:36
  172.2 3.3 %collective-permute-start.1 = (bf16[128,768]{1,0:T(8,128)(2,1)S(1)}, bf16[128,768]{1,0:T(8,128)(2,1)S(1)}, u32[]{:S(2)}, u32[]{:S(2)}) collective-permute-start(bf16[128,768]{1,0:T(8,128)(2,1)S(1)} %bitcast.38), channel_id=1, source_target_pairs={{0,1},{1,0},{2,3},{3,2},{4,5},{5,4},{6,7},{7,6},{8,9},{9,8},{10,11... | collective-permute-start | bytes 589832 | tf_op jit(solution)/shard_map/ppermute | solution.py:311
  175.4 0.1 shift_left.49
  175.5 0.1 shift_left.50
  175.6 0.0 copy-done.4
  175.6 2.7 %fusion.4 = bf16[512,4608]{0,1:T(8,128)(2,1)S(1)} fusion(s32[4608]{0:T(1024)S(1)} %shift_left.50, s32[512,576]{0,1:T(8,128)} %param.16, bf16[512,36]{0,1:T(8,128)(2,1)S(1)} %copy-done.4), kind=kLoop, calls=%fused_computation.6 | loop fusion | flops 16515072 | bytes 5953536 | tf_op jit(solution)/shard_map/mul | solution.py:62
  178.3 0.0 collective-permute-done.1.refs_3_
  178.3 0.0 collective-permute-done.refs_1_
  178.4 0.0 copy-done.3
  178.4 2.2 %vocab_sums.1 = f32[16,6,128]{2,1,0:T(8,128)S(1)} custom-call(s32[8]{0:T(128)S(1)} %copy-done.3, bf16[128,3968]{1,0:T(8,128)(2,1)S(1)} %all-gather.2.refs_0_, bf16[128,3968]{1,0:T(8,128)(2,1)S(1)} %collective-permute-done.refs_1_, bf16[128,768]{1,0:T(8,128)(2,1)S(1)} %bitcast.39, bf16[128,768]{1,0:T(8,128)(2,1)S(1)} %collective-permute-done.1.refs_3_, ...), custom_call_target="tpu_custom_call" | custom-call | flops 1207959552 | bytes 7077888 | tf_op jit(solution)/shard_map/vocab_sums/pallas_call | solution.py:219
  180.5 10.3 %all_to_all.27 = f32[16,6,128]{2,1,0:T(8,128)S(1)} all-to-all(f32[16,6,128]{2,1,0:T(8,128)S(1)} %vocab_sums.1), channel_id=1, replica_groups=mesh['groups'=2,'fsdp'=16,'mp'=8,'sub'=2] {'mp','sub'}, dimensions={0} | all-to-all | bytes 98304 | tf_op jit(solution)/shard_map/all_to_all | solution.py:316
  190.9 20.7 %all_to_all.28.packed_ref = f32[16,6,128]{2,1,0:T(8,128)S(1)} all-to-all(f32[16,6,128]{2,1,0:T(8,128)S(1)} %broadcast_in_dim.8), channel_id=1, replica_groups=mesh['groups'=2,'fsdp'=16,'mp'=8,'sub'=2] {'fsdp'}, dimensions={0} | all-to-all | bytes 98304 | tf_op jit(solution)/shard_map/all_to_all | solution.py:21
  211.5 0.7 losses_of.1
  (7 shorter events, 0.1 us)
Async XLA Ops:
  0.6 0.9 copy-start
  1.5 47.4 %copy-start.5 = (bf16[36,288]{1,0:T(8,128)(2,1)S(1)}, bf16[36,288]{1,0:T(8,128)(2,1)}, u32[]{:S(2)}) copy-start(bf16[36,288]{1,0:T(8,128)(2,1)} %param.13) | copy-start | bytes 62212
  2.2 84.4 %all-to-all-start = ((bf16[16,8,640]{2,1,0:T(8,128)(2,1)}), bf16[16,8,640]{2,1,0:T(8,128)(2,1)S(1)}, u32[]{:S(2)}, u32[]{:S(2)}) async-start(bf16[16,8,640]{2,1,0:T(8,128)(2,1)} %get-tuple-element.13), calls=%async_computation | async-start | bytes 327680 | tf_op jit(solution)/shard_map/all_to_all | solution.py:36
  50.2 53.6 %copy-start.1 = (bf16[8,4608]{1,0:T(8,128)(2,1)S(1)}, bf16[8,4608]{1,0:T(8,128)(2,1)}, u32[]{:S(2)}) copy-start(bf16[8,4608]{1,0:T(8,128)(2,1)} %residual_ref) | copy-start | bytes 221188
  50.2 53.5 %copy-start.2 = (s32[8]{0:T(128)S(1)}, s32[8]{0:T(128)}, u32[]{:S(2)}) copy-start(s32[8]{0:T(128)} %targets_ref) | copy-start | bytes 100
  50.2 82.2 %copy-start.6 = (f32[4608]{0:T(1024)S(1)}, f32[4608]{0:T(1024)}, u32[]{:S(2)}) copy-start(f32[4608]{0:T(1024)} %param.14) | copy-start | bytes 55300
  50.3 82.2 %copy-start.7 = (f32[4608]{0:T(1024)S(1)}, f32[4608]{0:T(1024)}, u32[]{:S(2)}) copy-start(f32[4608]{0:T(1024)} %param.15) | copy-start | bytes 55300
  50.8 124.8 %copy-start.4 = (bf16[512,36]{0,1:T(8,128)(2,1)S(1)}, bf16[512,36]{0,1:T(8,128)(2,1)}, u32[]{:S(2)}) copy-start(bf16[512,36]{0,1:T(8,128)(2,1)} %param.17) | copy-start | bytes 110596
  85.5 92.8 %copy-start.3 = (s32[8]{0:T(128)S(1)}, s32[8]{0:T(128)}, u32[]{:S(2)}) copy-start(s32[8]{0:T(128)} %mask_ref.1) | copy-start | bytes 100
  156.4 21.9 %collective-permute-start = (bf16[128,3968]{1,0:T(8,128)(2,1)S(1)}, bf16[128,3968]{1,0:T(8,128)(2,1)S(1)}, u32[]{:S(2)}, u32[]{:S(2)}) collective-permute-start(bf16[128,3968]{1,0:T(8,128)(2,1)S(1)} %all-gather.2.refs_0_), channel_id=1, source_target_pairs={{0,1},{1,0},{2,3},{3,2},{4,5},{5,4},{6,7},{7,6},{8,9},{9,8},{10,11... | collective-permute-start | bytes 3047432 | tf_op jit(solution)/shard_map/ppermute | solution.py:312
  172.2 6.2 %collective-permute-start.1 = (bf16[128,768]{1,0:T(8,128)(2,1)S(1)}, bf16[128,768]{1,0:T(8,128)(2,1)S(1)}, u32[]{:S(2)}, u32[]{:S(2)}) collective-permute-start(bf16[128,768]{1,0:T(8,128)(2,1)S(1)} %bitcast.38), channel_id=1, source_target_pairs={{0,1},{1,0},{2,3},{3,2},{4,5},{5,4},{6,7},{7,6},{8,9},{9,8},{10,11... | collective-permute-start | bytes 589832 | tf_op jit(solution)/shard_map/ppermute | solution.py:311

commit v5 on v4

--- a/solution.py
+++ b/solution.py
@@ -67,27 +67,43 @@
     return lax.dot_general(a, b, (dims, ((), ())), preferred_element_type=jnp.float32)
 
 
-def split_kernel(hidden_ref, head_ref, tail_ref):
+def split_kernel(hidden_hbm, words_hbm, head_ref, tail_ref, turned_ref, hidden_ref, words_ref, sem):
     cut = head_ref.shape[1]
+    loads = [
+        pltpu.make_async_copy(hidden_hbm, hidden_ref, sem.at[0]),
+        pltpu.make_async_copy(words_hbm, words_ref, sem.at[1]),
+    ]
+    for load in loads:
+        load.start()
+    loads[0].wait()
     head_ref[...] = hidden_ref[:, :cut]
     tail_ref[...] = jnp.broadcast_to(hidden_ref[:, cut:][None], tail_ref.shape)
-
-
-def split_columns(hidden, cut, copies):
+    loads[1].wait()
+    turned_ref[...] = words_ref[...].T
+
+
+def split_columns(hidden, words, cut, copies):
     rows, width = hidden.shape
     return pl.pallas_call(
         split_kernel,
+        in_specs=[pl.BlockSpec(memory_space=pl.ANY)] * 2,
+        out_specs=[VMEM] * 3,
         out_shape=(
             jax.ShapeDtypeStruct((rows, cut), hidden.dtype),
             jax.ShapeDtypeStruct((copies, rows, width - cut), hidden.dtype),
-        ),
-        in_specs=[VMEM],
-        compiler_params=pltpu.CompilerParams(vmem_limit_bytes=4 << 20),
+            jax.ShapeDtypeStruct(words.shape[::-1], words.dtype),
+        ),
+        scratch_shapes=[
+            pltpu.VMEM(hidden.shape, hidden.dtype),
+            pltpu.VMEM(words.shape, words.dtype),
+            pltpu.SemaphoreType.DMA((2,)),
+        ],
+        compiler_params=pltpu.CompilerParams(vmem_limit_bytes=8 << 20),
         name="split_columns",
-    )(hidden)
-
-
-def pack_kernel(targets_ref, parts_ref, residual_ref, out_ref):
+    )(hidden, words)
+
+
+def pack_kernel(targets_ref, loss_mask_ref, parts_ref, residual_ref, out_ref):
     per, cols = parts_ref.shape[1:]
     width = out_ref.shape[1]
     ffn = jnp.sum(parts_ref[...], axis=0)
@@ -101,26 +117,27 @@
     res = jnp.sum(jnp.where(token == x, res, 0.0), axis=0, keepdims=True)
     rows = [res[:, c : c + width] for c in range(0, res.shape[1], width)]
     goal = targets_ref[x]
+    values = (goal & 255, (goal >> 8) & 255, goal >> 16, loss_mask_ref[x])
     lane = lax.broadcasted_iota(jnp.int32, (1, width), 1)
-    digit = jnp.where(
-        lane == 0, goal & 255, jnp.where(lane == 1, (goal >> 8) & 255, jnp.where(lane == 2, goal >> 16, 0))
-    )
+    digit = jnp.zeros((1, width), jnp.int32)
+    for i, value in enumerate(values):
+        digit = jnp.where(lane == i, value, digit)
     rows.append(digit.astype(jnp.float32))
     rows.append(jnp.zeros((out_ref.shape[0] - 2 * per - len(rows), width), jnp.float32))
     out_ref[2 * per :] = jnp.concatenate(rows, axis=0).astype(jnp.bfloat16)
 
 
-def pack_rows(targets, parts, residual):
+def pack_rows(targets, loss_mask, parts, residual):
     per, cols = parts.shape[1:]
     width = cols + -cols % LANES
     count = 2 * per + residual.shape[1] // width + 1
     return pl.pallas_call(
         pack_kernel,
-        in_specs=[SMEM, VMEM, VMEM],
+        in_specs=[SMEM, SMEM, VMEM, VMEM],
         out_shape=jax.ShapeDtypeStruct((count + -count % 16, width), jnp.bfloat16),
         compiler_params=pltpu.CompilerParams(vmem_limit_bytes=4 << 20),
         name="pack_rows",
-    )(targets, parts, residual)
+    )(targets, loss_mask, parts, residual)
 
 
 def norm_kernel(blocks_ref, post_ref, final_ref, head_ref, tail_ref, turn_ref):
@@ -174,16 +191,13 @@
     )(blocks, post_gain[None], final_gain[None])
 
 
-def sums_kernel(n_z, mask_ref, heads, tails, embed_ref, out_ref, st_ref, acc_ref):
+def sums_kernel(n_z, halves, embed_ref, out_ref, mask_ref, st_ref, acc_ref):
     n_s, held, _ = st_ref.shape
-    cut = heads[0].shape[1]
     dim, vocab = embed_ref.shape
     z, x, s = (lax.axis_index(a) for a in ("fsdp", "mp", "sub"))
     first = ((z * lax.axis_size("mp") + x) * n_s + s) * vocab
-    lead = jnp.where(x == 0, 1, 0)
     for h in range(n_s):
-        st_ref[h, :, :cut] = heads[h][...]
-        st_ref[h, :, cut:] = tails[h][...]
+        st_ref[h] = halves[h][...]
     states = st_ref.reshape(n_s * held, st_ref.shape[2])
     acc_ref[...] = dot_f32(states[:, :dim], embed_ref[...], ((1,), (0,)))
     digits = states[:, dim:].astype(jnp.float32)
@@ -197,31 +211,33 @@
         sums += jnp.exp(capped)
         hits += jnp.where(ids == goal, capped, 0.0)
     rows = [jnp.sum(r.T, axis=0, keepdims=True) for r in (sums, hits)]
+    rows.append(digits.T[3:4])
     place = lax.broadcasted_iota(jnp.int32, (1, held), 1)
     core = (place + place // n_z + z + x + s) % n_s
-    mask = jnp.zeros((1, held), jnp.float32)
-    for i in range(mask_ref.shape[0]):
-        mask = jnp.where(place == i * n_z + z, (mask_ref[i] * lead).astype(jnp.float32), mask)
     parts = [
         jnp.where(core == h, row[:, :held], row[:, held:]) for row in rows for h in range(n_s)
-    ] + [jnp.where(s == h, mask, 0.0) for h in range(n_s)]
-    for r, part in enumerate(parts):
-        out_ref[:, r : r + 1, :] = jnp.broadcast_to(part[None], (out_ref.shape[0], 1, held))
-
-
-def vocab_sums(mask, heads, tails, embed, n_z, copies):
-    n_s, (held, cut) = len(heads), heads[0].shape
+    ]
+    mask_ref[...] = jnp.concatenate(parts[2 * n_s :], axis=0)
+    part = jnp.concatenate(parts[: 2 * n_s], axis=0)
+    out_ref[...] = jnp.broadcast_to(part[None], out_ref.shape)
+
+
+def vocab_sums(halves, embed, n_z, copies):
+    n_s, (held, width) = len(halves), halves[0].shape
     dim, vocab = embed.shape
 
-    def kernel(mask_ref, *refs):
-        sums_kernel(n_z, mask_ref, refs[:n_s], refs[n_s : 2 * n_s], *refs[2 * n_s :])
+    def kernel(*refs):
+        sums_kernel(n_z, refs[:n_s], *refs[n_s:])
 
     return pl.pallas_call(
         kernel,
-        in_specs=[SMEM] + [VMEM] * (2 * n_s + 1),
-        out_shape=jax.ShapeDtypeStruct((copies, 3 * n_s, held), jnp.float32),
+        in_specs=[VMEM] * (n_s + 1),
+        out_shape=(
+            jax.ShapeDtypeStruct((copies, 2 * n_s, held), jnp.float32),
+            jax.ShapeDtypeStruct((n_s, held), jnp.float32),
+        ),
         scratch_shapes=[
-            pltpu.VMEM((n_s, held, cut + tails[0].shape[1]), jnp.bfloat16),
+            pltpu.VMEM((n_s, held, width), jnp.bfloat16),
             pltpu.VMEM((n_s * held, vocab), jnp.float32),
         ],
         compiler_params=pltpu.CompilerParams(vmem_limit_bytes=24 << 20),
@@ -231,15 +247,15 @@
             transcendentals=2 * n_s * held * vocab,
         ),
         name="vocab_sums",
-    )(mask, *heads, *tails, embed)
-
-
-def loss_kernel(n_z, packed_ref, token_ref, mean_ref):
+    )(*halves, embed)
+
+
+def loss_kernel(n_z, packed_ref, mask_ref, token_ref, mean_ref):
     toks = token_ref.shape[0]
-    n_s, held = packed_ref.shape[1] // 3, packed_ref.shape[2]
+    n_s, held = mask_ref.shape
     z, s = lax.axis_index("fsdp"), lax.axis_index("sub")
     packed = jnp.sum(packed_ref[...], axis=0)
-    sums, goals, mask = (packed[r * n_s : (r + 1) * n_s] for r in range(3))
+    sums, goals, mask = packed[:n_s], packed[n_s:], mask_ref[...]
     losses = mask * (jnp.log(sums) - goals)
     total, count = jnp.sum(losses), jnp.sum(mask)
     whole = jnp.full((1, held), total) / jnp.maximum(jnp.full((1, held), count), 1.0)
@@ -252,17 +268,17 @@
     token_ref[...] = jnp.sum(spread.T, axis=0)[:toks]
 
 
-def losses_of(packed, n_z, toks):
+def losses_of(packed, mask, n_z, toks):
     return pl.pallas_call(
         functools.partial(loss_kernel, n_z),
-        in_specs=[VMEM],
+        in_specs=[VMEM, VMEM],
         out_shape=(
             jax.ShapeDtypeStruct((toks,), jnp.float32),
             jax.ShapeDtypeStruct((1,), jnp.float32),
         ),
         compiler_params=pltpu.CompilerParams(vmem_limit_bytes=4 << 20),
         name="losses_of",
-    )(packed)
+    )(packed, mask)
 
 
 def on_device(
@@ -285,7 +301,7 @@
     per_x = held // n_x
 
     cut = gather_cut(toks, width, n_z)
-    head, tail = split_columns(hidden, cut, n_z)
+    head, tail, down_packed = split_columns(hidden, down_packed.T, cut, n_z)
     tail = exchange_ring(tail, "fsdp")
     head = gather_ring(head, "fsdp")
     weight = dequant_down(down_packed, down_scale)
@@ -297,7 +313,7 @@
     parts = lax.all_to_all(part, "mp", 0, 0, tiled=True)
     parts, residual, targets = lax.optimization_barrier((parts, residual, targets))
 
-    block = pack_rows(targets, parts, residual)
+    block = pack_rows(targets, loss_mask, parts, residual)
     blocks = gather_ring(block, "fsdp")
     blocks, post_gain, final_gain = lax.optimization_barrier((blocks, post_gain, final_gain))
 
@@ -305,16 +321,13 @@
     head, tail = norm_rows(blocks, post_gain, final_gain, per_x, cut, n_x)
     tail = exchange_ring(tail, "mp")
     head = gather_ring(head, "mp")
-    swap = [(i, n_s - 1 - i) for i in range(n_s)]
-    heads = [head.reshape(held, cut)]
-    tails = [tail.reshape(held, dim - cut + LANES)]
-    tails.append(lax.ppermute(tails[0], "sub", swap))
-    heads.append(lax.ppermute(heads[0], "sub", swap))
+    own = jnp.concatenate([head.reshape(held, cut), tail.reshape(held, dim - cut + LANES)], axis=1)
+    far = lax.ppermute(own, "sub", [(i, n_s - 1 - i) for i in range(n_s)])
     embed = dequant_embed(embed_packed, embed_scale)
-    packed = vocab_sums(loss_mask, heads, tails, embed.T, n_z, n_x * n_s)
+    packed, mask = vocab_sums((own, far), embed.T, n_z, n_x * n_s)
 
     packed = jnp.sum(lax.all_to_all(packed, ("mp", "sub"), 0, 0, tiled=True), axis=0)
-    return losses_of(copy_for_each(packed, "fsdp"), n_z, toks)
+    return losses_of(copy_for_each(packed, "fsdp"), mask, n_z, toks)
 
 
 def solution(mesh):

time: 213 us -> 207 us (0.972)
  blocking collectives: 147 us -> 141 us
    all_to_all x1 -> x0, blocking collectives: 13.6 us -> none  [exchange_ring(): lax.all_to_all(copies, (axis, 'sub'), 0, 0, tiled=True, axis_index_groups...]
    all_gather x3, blocking collectives: 86.3 us -> 91.6 us  [gather_ring(): return lax.all_gather(value, (axis, 'sub'), axis_index_groups=rings(axis))]
    all_to_all x1 -> x2, starting transfers between devices: 44.7 us -> 48.3 us  [exchange_ring(): lax.all_to_all(copies, (axis, 'sub'), 0, 0, tiled=True, axis_index_groups...]
    ppermute x2 -> x1, starting transfers between devices: 5.42 us -> 2.28 us  [on_device(): far = lax.ppermute(own, 'sub', [(i, n_s - 1 - i) for i in range(n_s)])]
    all_to_all x1, blocking collectives: 10.3 us -> 13.1 us  [on_device(): lax.all_to_all(packed, ('mp', 'sub'), 0, 0, tiled=True)]
  transfers between devices with their start and end apart: 3 -> 3, of which waited for: 0 -> 0; matrix products, arithmetic and copies ran while one was open for 4% -> 3% of each run, Pallas kernels for 0% -> 0%
where the time goes in v5:
time: 207 us
  blocking collectives  141 us (68%)
  starting transfers between devices  50.6 us (24%)
  Pallas kernels  5.04 us (2%)
  other arithmetic  4.13 us (2%)
  local copies, waits for them, and re-layouts  3.47 us (2%)
    all_gather x3, blocking collectives, gather_ring(): return lax.all_gather(value, (axis, 'sub'), axis_index_groups=rings(axis))  91.6 us
    all_to_all x2, starting transfers between devices, exchange_ring(): lax.all_to_all(copies, (axis, 'sub'), 0, 0, tiled=True, axis_index_groups...  48.3 us
    all_to_all x1, blocking collectives, copy_for_each(): lax.all_to_all(jnp.broadcast_to(value[None], (peers, *value.shape)), axis...  20 us
    all_to_all x1, blocking collectives, on_device(): parts = lax.all_to_all(part, 'mp', 0, 0, tiled=True)  16.1 us
    all_to_all x1, blocking collectives, on_device(): lax.all_to_all(packed, ('mp', 'sub'), 0, 0, tiled=True)  13.1 us
  transfers between devices with their start and end apart: 3, of which 0 were waited for; matrix products, arithmetic and copies ran while one was open for 3% of the time, Pallas kernels for 0%

profile of v5, /device:TPU:65, one launch (start us, length us, event | category | flops | bytes accessed | tf_op | source)
XLA Modules:
  0.0 206.5 jit_solution(9544301381033872640)
XLA Ops:
  0.6 0.0 copy-start
  0.6 1.1 copy-done
  1.7 0.0 copy-start.1
  1.7 0.9 copy-done.1
  2.6 0.0 copy-start.6
  2.6 1.1 split_columns.1
  3.7 44.7 %all-to-all-start = ((bf16[16,8,640]{2,1,0:T(8,128)(2,1)}), bf16[16,8,640]{2,1,0:T(8,128)(2,1)S(1)}, u32[]{:S(2)}, u32[]{:S(2)}) async-start(bf16[16,8,640]{2,1,0:T(8,128)(2,1)} %get-tuple-element.17), calls=%async_computation | async-start | bytes 327680 | tf_op jit(solution)/shard_map/all_to_all | solution.py:36
  48.5 0.1 shift_left.44
  48.6 0.5 shift_left.41
  49.0 0.0 copy-done.6
  49.0 1.3 fusion.5
  50.3 0.5 slice.16
  50.8 0.0 copy-start.2
  50.8 0.0 copy-start.3
  50.9 0.0 copy-start.4
  50.9 0.0 copy-start.7
  50.9 0.0 copy-start.8
  50.9 0.1 slice.17
  50.9 35.5 %all-gather = bf16[128,3968]{1,0:T(8,128)(2,1)S(1)} all-gather(bf16[8,3968]{1,0:T(8,128)(2,1)S(1)} %get-tuple-element.15), channel_id=2, replica_groups={{0,17,32,49,64,81,96,113,128,145,160,177,192,209,224,241},{1,16,33,48,6..., dimensions={0}, use_global_device_ids=true | all-gather | bytes 1079296 | tf_op jit(solution)/shard_map/all_gather | solution.py:32
  86.5 1.2 fusion.7
  87.7 0.0 copy-start.5
  87.7 0.0 all-to-all-done
  87.7 0.3 convolution_add_fusion
  88.0 0.1 copy.17
  88.2 16.1 %all_to_all.25.parts_ref = f32[8,16,288]{2,1,0:T(8,128)S(1)} all-to-all(f32[8,16,288]{2,1,0:T(8,128)S(1)} %bitcast.42), channel_id=1, replica_groups=mesh['groups'=2,'fsdp'=16,'mp'=8,'sub'=2] {'mp'}, dimensions={0} | all-to-all | bytes 294912 | tf_op jit(solution)/shard_map/all_to_all | solution.py:313
  104.4 0.0 copy-done.2
  104.4 0.0 copy-done.3
  104.4 0.0 copy-done.4
  104.4 0.6 pack_rows.1
  105.0 29.2 %all-gather.1 = bf16[768,384]{1,0:T(8,128)(2,1)S(1)} all-gather(bf16[48,384]{1,0:T(8,128)(2,1)S(1)} %pack_rows.1), channel_id=3, replica_groups={{0,17,32,49,64,81,96,113,128,145,160,177,192,209,224,241},{1,16,33,48,6..., dimensions={0}, use_global_device_ids=true | all-gather | bytes 626688 | tf_op jit(solution)/shard_map/all_gather | solution.py:32
  134.2 0.0 copy-done.7
  134.2 0.0 copy-done.8
  134.3 1.1 norm_rows.1
  135.4 3.6 %all-to-all-start.2 = ((bf16[8,16,768]{2,1,0:T(8,128)(2,1)}), bf16[8,16,768]{2,1,0:T(8,128)(2,1)S(1)}, u32[]{:S(2)}, u32[]{:S(2)}) async-start(bf16[8,16,768]{2,1,0:T(8,128)(2,1)} %get-tuple-element.25), calls=%async_computation.2 | async-start | bytes 393216 | tf_op jit(solution)/shard_map/all_to_all | solution.py:36
  139.0 26.9 %all-gather.2 = bf16[128,3968]{1,0:T(8,128)(2,1)S(1)} all-gather(bf16[16,3968]{1,0:T(8,128)(2,1)S(1)} %get-tuple-element.24), channel_id=4, replica_groups={{0,3,4,7,8,11,12,15},{1,2,5,6,9,10,13,14},{16,19,20,23,24,27,28,31},{17..., dimensions={0}, use_global_device_ids=true | all-gather | bytes 1142784 | tf_op jit(solution)/shard_map/all_gather | solution.py:32
  165.8 0.0 all-to-all-done.2
  165.8 0.1 pad_maximum_fusion.refs_0_
  165.9 2.3 %collective-permute-start = (bf16[128,4736]{1,0:T(8,128)(2,1)S(1)}, bf16[128,4736]{1,0:T(8,128)(2,1)S(1)}, u32[]{:S(2)}, u32[]{:S(2)}) collective-permute-start(bf16[128,4736]{1,0:T(8,128)(2,1)S(1)} %pad_maximum_fusion.refs_0_), channel_id=1, source_target_pairs={{0,1},{1,0},{2,3},{3,2},{4,5},{5,4},{6,7},{7,6},{8,9},{9,8},{10,11... | collective-permute-start | bytes 3637256 | tf_op jit(solution)/shard_map/ppermute | solution.py:325
  168.2 0.1 shift_left.49
  168.3 0.1 shift_left.50
  168.4 0.0 copy-done.5
  168.4 2.7 %fusion.4 = bf16[512,4608]{0,1:T(8,128)(2,1)S(1)} fusion(s32[4608]{0:T(1024)S(1)} %shift_left.50, s32[512,576]{0,1:T(8,128)} %param.16, bf16[512,36]{0,1:T(8,128)(2,1)S(1)} %copy-done.5), kind=kLoop, calls=%fused_computation.6 | loop fusion | flops 16515072 | bytes 5953536 | tf_op jit(solution)/shard_map/mul | solution.py:62
  171.1 0.0 collective-permute-done.refs_1_
  171.1 1.6 vocab_sums.1
  172.7 13.1 %all_to_all.26 = f32[16,4,128]{2,1,0:T(4,128)S(1)} all-to-all(f32[16,4,128]{2,1,0:T(4,128)S(1)} %get-tuple-element.26), channel_id=1, replica_groups=mesh['groups'=2,'fsdp'=16,'mp'=8,'sub'=2] {'mp','sub'}, dimensions={0} | all-to-all | bytes 65536 | tf_op jit(solution)/shard_map/all_to_all | solution.py:329
  185.9 20.0 %all_to_all.27.packed_ref = f32[16,4,128]{2,1,0:T(4,128)S(1)} all-to-all(f32[16,4,128]{2,1,0:T(4,128)S(1)} %broadcast_in_dim.8), channel_id=1, replica_groups=mesh['groups'=2,'fsdp'=16,'mp'=8,'sub'=2] {'fsdp'}, dimensions={0} | all-to-all | bytes 65536 | tf_op jit(solution)/shard_map/all_to_all | solution.py:21
  205.9 0.7 losses_of.1
  (7 shorter events, 0.1 us)
Async XLA Ops:
  0.6 1.1 copy-start
  1.7 0.9 copy-start.1
  2.6 46.4 %copy-start.6 = (bf16[36,288]{1,0:T(8,128)(2,1)S(1)}, bf16[36,288]{1,0:T(8,128)(2,1)}, u32[]{:S(2)}) copy-start(bf16[36,288]{1,0:T(8,128)(2,1)} %param.13) | copy-start | bytes 62212
  3.7 84.0 %all-to-all-start = ((bf16[16,8,640]{2,1,0:T(8,128)(2,1)}), bf16[16,8,640]{2,1,0:T(8,128)(2,1)S(1)}, u32[]{:S(2)}, u32[]{:S(2)}) async-start(bf16[16,8,640]{2,1,0:T(8,128)(2,1)} %get-tuple-element.17), calls=%async_computation | async-start | bytes 327680 | tf_op jit(solution)/shard_map/all_to_all | solution.py:36
  50.8 53.5 %copy-start.2 = (bf16[8,4608]{1,0:T(8,128)(2,1)S(1)}, bf16[8,4608]{1,0:T(8,128)(2,1)}, u32[]{:S(2)}) copy-start(bf16[8,4608]{1,0:T(8,128)(2,1)} %residual_ref) | copy-start | bytes 221188
  50.8 53.5 %copy-start.3 = (s32[8]{0:T(128)S(1)}, s32[8]{0:T(128)}, u32[]{:S(2)}) copy-start(s32[8]{0:T(128)} %targets_ref) | copy-start | bytes 100
  50.9 53.5 %copy-start.4 = (s32[8]{0:T(128)S(1)}, s32[8]{0:T(128)}, u32[]{:S(2)}) copy-start(s32[8]{0:T(128)} %loss_mask_ref.1) | copy-start | bytes 100
  50.9 83.4 %copy-start.7 = (f32[4608]{0:T(1024)S(1)}, f32[4608]{0:T(1024)}, u32[]{:S(2)}) copy-start(f32[4608]{0:T(1024)} %param.14) | copy-start | bytes 55300
  50.9 83.4 %copy-start.8 = (f32[4608]{0:T(1024)S(1)}, f32[4608]{0:T(1024)}, u32[]{:S(2)}) copy-start(f32[4608]{0:T(1024)} %param.15) | copy-start | bytes 55300
  87.7 80.7 %copy-start.5 = (bf16[512,36]{0,1:T(8,128)(2,1)S(1)}, bf16[512,36]{0,1:T(8,128)(2,1)}, u32[]{:S(2)}) copy-start(bf16[512,36]{0,1:T(8,128)(2,1)} %param.17) | copy-start | bytes 110596
  135.4 30.5 %all-to-all-start.2 = ((bf16[8,16,768]{2,1,0:T(8,128)(2,1)}), bf16[8,16,768]{2,1,0:T(8,128)(2,1)S(1)}, u32[]{:S(2)}, u32[]{:S(2)}) async-start(bf16[8,16,768]{2,1,0:T(8,128)(2,1)} %get-tuple-element.25), calls=%async_computation.2 | async-start | bytes 393216 | tf_op jit(solution)/shard_map/all_to_all | solution.py:36
  165.9 5.2 %collective-permute-start = (bf16[128,4736]{1,0:T(8,128)(2,1)S(1)}, bf16[128,4736]{1,0:T(8,128)(2,1)S(1)}, u32[]{:S(2)}, u32[]{:S(2)}) collective-permute-start(bf16[128,4736]{1,0:T(8,128)(2,1)S(1)} %pad_maximum_fusion.refs_0_), channel_id=1, source_target_pairs={{0,1},{1,0},{2,3},{3,2},{4,5},{5,4},{6,7},{7,6},{8,9},{9,8},{10,11... | collective-permute-start | bytes 3637256 | tf_op jit(solution)/shard_map/ppermute | solution.py:325

commit v6 on v5

--- a/solution.py
+++ b/solution.py
@@ -67,50 +67,32 @@
     return lax.dot_general(a, b, (dims, ((), ())), preferred_element_type=jnp.float32)
 
 
-def split_kernel(hidden_hbm, words_hbm, head_ref, tail_ref, turned_ref, hidden_ref, words_ref, sem):
+def split_kernel(hidden_ref, head_ref, tail_ref):
     cut = head_ref.shape[1]
-    loads = [
-        pltpu.make_async_copy(hidden_hbm, hidden_ref, sem.at[0]),
-        pltpu.make_async_copy(words_hbm, words_ref, sem.at[1]),
-    ]
-    for load in loads:
-        load.start()
-    loads[0].wait()
     head_ref[...] = hidden_ref[:, :cut]
     tail_ref[...] = jnp.broadcast_to(hidden_ref[:, cut:][None], tail_ref.shape)
-    loads[1].wait()
-    turned_ref[...] = words_ref[...].T
-
-
-def split_columns(hidden, words, cut, copies):
+
+
+def split_columns(hidden, cut, copies):
     rows, width = hidden.shape
     return pl.pallas_call(
         split_kernel,
-        in_specs=[pl.BlockSpec(memory_space=pl.ANY)] * 2,
-        out_specs=[VMEM] * 3,
+        in_specs=[VMEM],
         out_shape=(
             jax.ShapeDtypeStruct((rows, cut), hidden.dtype),
             jax.ShapeDtypeStruct((copies, rows, width - cut), hidden.dtype),
-            jax.ShapeDtypeStruct(words.shape[::-1], words.dtype),
-        ),
-        scratch_shapes=[
-            pltpu.VMEM(hidden.shape, hidden.dtype),
-            pltpu.VMEM(words.shape, words.dtype),
-            pltpu.SemaphoreType.DMA((2,)),
-        ],
-        compiler_params=pltpu.CompilerParams(vmem_limit_bytes=8 << 20),
+        ),
+        compiler_params=pltpu.CompilerParams(vmem_limit_bytes=4 << 20),
         name="split_columns",
-    )(hidden, words)
+    )(hidden)
 
 
 def pack_kernel(targets_ref, loss_mask_ref, parts_ref, residual_ref, out_ref):
     per, cols = parts_ref.shape[1:]
     width = out_ref.shape[1]
     ffn = jnp.sum(parts_ref[...], axis=0)
-    high = ffn.astype(jnp.bfloat16)
-    out_ref[...] = jnp.zeros_like(out_ref)
-    out_ref[:per, :cols] = high
-    out_ref[per : 2 * per, :cols] = (ffn - high.astype(jnp.float32)).astype(jnp.bfloat16)
+    out_ref[:per] = jnp.zeros((per, width), jnp.bfloat16)
+    out_ref[:per, :cols] = ffn.astype(jnp.bfloat16)
     x = lax.axis_index("mp")
     res = residual_ref[...].astype(jnp.float32)
     token = lax.broadcasted_iota(jnp.int32, res.shape, 0)
@@ -123,14 +105,14 @@
     for i, value in enumerate(values):
         digit = jnp.where(lane == i, value, digit)
     rows.append(digit.astype(jnp.float32))
-    rows.append(jnp.zeros((out_ref.shape[0] - 2 * per - len(rows), width), jnp.float32))
-    out_ref[2 * per :] = jnp.concatenate(rows, axis=0).astype(jnp.bfloat16)
+    rows.append(jnp.zeros((out_ref.shape[0] - per - len(rows), width), jnp.float32))
+    out_ref[per:] = jnp.concatenate(rows, axis=0).astype(jnp.bfloat16)
 
 
 def pack_rows(targets, loss_mask, parts, residual):
     per, cols = parts.shape[1:]
     width = cols + -cols % LANES
-    count = 2 * per + residual.shape[1] // width + 1
+    count = per + residual.shape[1] // width + 1
     return pl.pallas_call(
         pack_kernel,
         in_specs=[SMEM, SMEM, VMEM, VMEM],
@@ -148,16 +130,12 @@
     rest, width = turn_ref.shape[1] // n_z, blocks_ref.shape[2]
     f32 = jnp.float32
     ffn = jnp.concatenate(
-        [
-            blocks_ref[i, :per, :cols].astype(f32) + blocks_ref[i, per : 2 * per, :cols].astype(f32)
-            for i in range(n_z)
-        ],
-        axis=1,
+        [blocks_ref[i, :per, :cols].astype(f32) for i in range(n_z)], axis=1
     )
     for i in range(n_z):
         for c in range(width // LANES):
             turn_ref[c, i * rest : (i + 1) * rest] = blocks_ref[
-                i, 2 * per :, c * LANES : (c + 1) * LANES
+                i, per:, c * LANES : (c + 1) * LANES
             ].astype(f32)
 
     def turned(r, c):
@@ -185,7 +163,7 @@
             jax.ShapeDtypeStruct((per, cut), blocks.dtype),
             jax.ShapeDtypeStruct((copies, per, dim - cut + LANES), blocks.dtype),
         ),
-        scratch_shapes=[pltpu.VMEM((width // LANES, n_z * (rows - 2 * per), LANES), jnp.float32)],
+        scratch_shapes=[pltpu.VMEM((width // LANES, n_z * (rows - per), LANES), jnp.float32)],
         compiler_params=pltpu.CompilerParams(vmem_limit_bytes=8 << 20),
         name="norm_rows",
     )(blocks, post_gain[None], final_gain[None])
@@ -301,7 +279,7 @@
     per_x = held // n_x
 
     cut = gather_cut(toks, width, n_z)
-    head, tail, down_packed = split_columns(hidden, down_packed.T, cut, n_z)
+    head, tail = split_columns(hidden, cut, n_z)
     tail = exchange_ring(tail, "fsdp")
     head = gather_ring(head, "fsdp")
     weight = dequant_down(down_packed, down_scale)

time: 207 us -> 204 us (0.986)
  blocking collectives: 141 us -> 138 us
    all_gather x3, blocking collectives: 91.6 us -> 88.5 us  [gather_ring(): return lax.all_gather(value, (axis, 'sub'), axis_index_groups=rings(axis))]
  transfers between devices with their start and end apart: 3 -> 3, of which waited for: 0 -> 0; matrix products, arithmetic and copies ran while one was open for 3% -> 4% of each run, Pallas kernels for 0% -> 0%
where the time goes in v6:
time: 204 us; the launch traced here: 203 us
  blocking collectives  138 us (68%)
  starting transfers between devices  50.4 us (25%)
  Pallas kernels  4.6 us (2%)
  other arithmetic  4.12 us (2%)
  local copies, waits for them, and re-layouts  3.79 us (2%)
    all_gather x3, blocking collectives, gather_ring(): return lax.all_gather(value, (axis, 'sub'), axis_index_groups=rings(axis))  88.5 us
    all_to_all x2, starting transfers between devices, exchange_ring(): lax.all_to_all(copies, (axis, 'sub'), 0, 0, tiled=True, axis_index_groups...  48.3 us
    all_to_all x1, blocking collectives, copy_for_each(): lax.all_to_all(jnp.broadcast_to(value[None], (peers, *value.shape)), axis...  19.9 us
    all_to_all x1, blocking collectives, on_device(): parts = lax.all_to_all(part, 'mp', 0, 0, tiled=True)  16.6 us
    all_to_all x1, blocking collectives, on_device(): lax.all_to_all(packed, ('mp', 'sub'), 0, 0, tiled=True)  13.2 us
  transfers between devices with their start and end apart: 3, of which 0 were waited for; matrix products, arithmetic and copies ran while one was open for 4% of the time, Pallas kernels for 0%

profile of v6, /device:TPU:65, one launch (start us, length us, event | category | flops | bytes accessed | tf_op | source)
XLA Modules:
  0.0 203.4 jit_solution(11899352810318252488)
XLA Ops:
  0.6 0.0 copy-start
  0.6 0.9 copy-done
  1.5 0.7 split_columns.1
  2.2 44.7 %all-to-all-start = ((bf16[16,8,640]{2,1,0:T(8,128)(2,1)}), bf16[16,8,640]{2,1,0:T(8,128)(2,1)S(1)}, u32[]{:S(2)}, u32[]{:S(2)}) async-start(bf16[16,8,640]{2,1,0:T(8,128)(2,1)} %get-tuple-element.15), calls=%async_computation | async-start | bytes 327680 | tf_op jit(solution)/shard_map/all_to_all | solution.py:36
  46.9 0.1 shift_left.44
  47.0 0.0 copy-start.5
  47.0 1.4 copy.19
  48.5 0.5 shift_left.41
  48.9 0.0 copy-done.5
  49.0 1.3 fusion.5
  50.2 0.5 slice.16
  50.7 0.0 copy-start.1
  50.7 0.0 copy-start.2
  50.8 0.0 copy-start.3
  50.8 0.0 copy-start.6
  50.8 0.0 copy-start.7
  50.8 0.1 slice.17
  50.9 34.7 %all-gather = bf16[128,3968]{1,0:T(8,128)(2,1)S(1)} all-gather(bf16[8,3968]{1,0:T(8,128)(2,1)S(1)} %get-tuple-element.14), channel_id=2, replica_groups={{0,17,32,49,64,81,96,113,128,145,160,177,192,209,224,241},{1,16,33,48,6..., dimensions={0}, use_global_device_ids=true | all-gather | bytes 1079296 | tf_op jit(solution)/shard_map/all_gather | solution.py:32
  85.6 1.1 fusion.8
  86.7 0.0 copy-start.4
  86.7 0.0 all-to-all-done
  86.7 0.3 fusion.6
  87.0 0.1 copy.21
  87.2 16.6 %all_to_all.25.parts_ref = f32[8,16,288]{2,1,0:T(8,128)S(1)} all-to-all(f32[8,16,288]{2,1,0:T(8,128)S(1)} %bitcast.42), channel_id=1, replica_groups=mesh['groups'=2,'fsdp'=16,'mp'=8,'sub'=2] {'mp'}, dimensions={0} | all-to-all | bytes 294912 | tf_op jit(solution)/shard_map/all_to_all | solution.py:291
  103.8 0.0 copy-done.1
  103.8 0.0 copy-done.2
  103.8 0.0 copy-done.3
  103.8 0.6 pack_rows.1
  104.4 27.0 %all-gather.1 = bf16[512,384]{1,0:T(8,128)(2,1)S(1)} all-gather(bf16[32,384]{1,0:T(8,128)(2,1)S(1)} %pack_rows.1), channel_id=3, replica_groups={{0,17,32,49,64,81,96,113,128,145,160,177,192,209,224,241},{1,16,33,48,6..., dimensions={0}, use_global_device_ids=true | all-gather | bytes 417792 | tf_op jit(solution)/shard_map/all_gather | solution.py:32
  131.4 0.0 copy-done.6
  131.4 0.0 copy-done.7
  131.5 1.1 norm_rows.1
  132.5 3.6 %all-to-all-start.2 = ((bf16[8,16,768]{2,1,0:T(8,128)(2,1)}), bf16[8,16,768]{2,1,0:T(8,128)(2,1)S(1)}, u32[]{:S(2)}, u32[]{:S(2)}) async-start(bf16[8,16,768]{2,1,0:T(8,128)(2,1)} %get-tuple-element.23), calls=%async_computation.2 | async-start | bytes 393216 | tf_op jit(solution)/shard_map/all_to_all | solution.py:36
  136.1 26.8 %all-gather.2 = bf16[128,3968]{1,0:T(8,128)(2,1)S(1)} all-gather(bf16[16,3968]{1,0:T(8,128)(2,1)S(1)} %get-tuple-element.22), channel_id=4, replica_groups={{0,3,4,7,8,11,12,15},{1,2,5,6,9,10,13,14},{16,19,20,23,24,27,28,31},{17..., dimensions={0}, use_global_device_ids=true | all-gather | bytes 1142784 | tf_op jit(solution)/shard_map/all_gather | solution.py:32
  162.9 0.0 all-to-all-done.2
  162.9 0.1 pad_maximum_fusion.refs_0_
  163.0 2.1 %collective-permute-start = (bf16[128,4736]{1,0:T(8,128)(2,1)S(1)}, bf16[128,4736]{1,0:T(8,128)(2,1)S(1)}, u32[]{:S(2)}, u32[]{:S(2)}) collective-permute-start(bf16[128,4736]{1,0:T(8,128)(2,1)S(1)} %pad_maximum_fusion.refs_0_), channel_id=1, source_target_pairs={{0,1},{1,0},{2,3},{3,2},{4,5},{5,4},{6,7},{7,6},{8,9},{9,8},{10,11... | collective-permute-start | bytes 3637256 | tf_op jit(solution)/shard_map/ppermute | solution.py:303
  165.1 0.1 shift_left.49
  165.2 0.1 shift_left.50
  165.3 0.0 copy-done.4
  165.3 2.7 %fusion.4 = bf16[512,4608]{0,1:T(8,128)(2,1)S(1)} fusion(s32[4608]{0:T(1024)S(1)} %shift_left.50, s32[512,576]{0,1:T(8,128)} %param.16, bf16[512,36]{0,1:T(8,128)(2,1)S(1)} %copy-done.4), kind=kLoop, calls=%fused_computation.6 | loop fusion | flops 16515072 | bytes 5953536 | tf_op jit(solution)/shard_map/mul | solution.py:62
  168.0 0.0 collective-permute-done.refs_1_
  168.0 1.6 vocab_sums.1
  169.6 13.2 %all_to_all.26 = f32[16,4,128]{2,1,0:T(4,128)S(1)} all-to-all(f32[16,4,128]{2,1,0:T(4,128)S(1)} %get-tuple-element.24), channel_id=1, replica_groups=mesh['groups'=2,'fsdp'=16,'mp'=8,'sub'=2] {'mp','sub'}, dimensions={0} | all-to-all | bytes 65536 | tf_op jit(solution)/shard_map/all_to_all | solution.py:307
  182.9 19.9 %all_to_all.27.packed_ref = f32[16,4,128]{2,1,0:T(4,128)S(1)} all-to-all(f32[16,4,128]{2,1,0:T(4,128)S(1)} %broadcast_in_dim.8), channel_id=1, replica_groups=mesh['groups'=2,'fsdp'=16,'mp'=8,'sub'=2] {'fsdp'}, dimensions={0} | all-to-all | bytes 65536 | tf_op jit(solution)/shard_map/all_to_all | solution.py:21
  202.7 0.7 losses_of.1
  (7 shorter events, 0.1 us)
Async XLA Ops:
  0.6 0.9 copy-start
  2.2 84.5 %all-to-all-start = ((bf16[16,8,640]{2,1,0:T(8,128)(2,1)}), bf16[16,8,640]{2,1,0:T(8,128)(2,1)S(1)}, u32[]{:S(2)}, u32[]{:S(2)}) async-start(bf16[16,8,640]{2,1,0:T(8,128)(2,1)} %get-tuple-element.15), calls=%async_computation | async-start | bytes 327680 | tf_op jit(solution)/shard_map/all_to_all | solution.py:36
  47.0 1.9 copy-start.5
  50.7 53.1 %copy-start.1 = (bf16[8,4608]{1,0:T(8,128)(2,1)S(1)}, bf16[8,4608]{1,0:T(8,128)(2,1)}, u32[]{:S(2)}) copy-start(bf16[8,4608]{1,0:T(8,128)(2,1)} %residual_ref) | copy-start | bytes 221188
  50.7 53.1 %copy-start.2 = (s32[8]{0:T(128)S(1)}, s32[8]{0:T(128)}, u32[]{:S(2)}) copy-start(s32[8]{0:T(128)} %targets_ref) | copy-start | bytes 100
  50.8 53.0 %copy-start.3 = (s32[8]{0:T(128)S(1)}, s32[8]{0:T(128)}, u32[]{:S(2)}) copy-start(s32[8]{0:T(128)} %loss_mask_ref.1) | copy-start | bytes 100
  50.8 80.7 %copy-start.6 = (f32[4608]{0:T(1024)S(1)}, f32[4608]{0:T(1024)}, u32[]{:S(2)}) copy-start(f32[4608]{0:T(1024)} %param.14) | copy-start | bytes 55300
  50.8 80.7 %copy-start.7 = (f32[4608]{0:T(1024)S(1)}, f32[4608]{0:T(1024)}, u32[]{:S(2)}) copy-start(f32[4608]{0:T(1024)} %param.15) | copy-start | bytes 55300
  86.7 78.6 %copy-start.4 = (bf16[512,36]{0,1:T(8,128)(2,1)S(1)}, bf16[512,36]{0,1:T(8,128)(2,1)}, u32[]{:S(2)}) copy-start(bf16[512,36]{0,1:T(8,128)(2,1)} %param.17) | copy-start | bytes 110596
  132.5 30.4 %all-to-all-start.2 = ((bf16[8,16,768]{2,1,0:T(8,128)(2,1)}), bf16[8,16,768]{2,1,0:T(8,128)(2,1)S(1)}, u32[]{:S(2)}, u32[]{:S(2)}) async-start(bf16[8,16,768]{2,1,0:T(8,128)(2,1)} %get-tuple-element.23), calls=%async_computation.2 | async-start | bytes 393216 | tf_op jit(solution)/shard_map/all_to_all | solution.py:36
  163.0 5.0 %collective-permute-start = (bf16[128,4736]{1,0:T(8,128)(2,1)S(1)}, bf16[128,4736]{1,0:T(8,128)(2,1)S(1)}, u32[]{:S(2)}, u32[]{:S(2)}) collective-permute-start(bf16[128,4736]{1,0:T(8,128)(2,1)S(1)} %pad_maximum_fusion.refs_0_), channel_id=1, source_target_pairs={{0,1},{1,0},{2,3},{3,2},{4,5},{5,4},{6,7},{7,6},{8,9},{9,8},{10,11... | collective-permute-start | bytes 3637256 | tf_op jit(solution)/shard_map/ppermute | solution.py:303

commit v7 on v6

--- a/solution.py
+++ b/solution.py
@@ -91,8 +91,10 @@
     per, cols = parts_ref.shape[1:]
     width = out_ref.shape[1]
     ffn = jnp.sum(parts_ref[...], axis=0)
-    out_ref[:per] = jnp.zeros((per, width), jnp.bfloat16)
-    out_ref[:per, :cols] = ffn.astype(jnp.bfloat16)
+    high = ffn.astype(jnp.bfloat16)
+    low = (ffn - high.astype(jnp.float32)).astype(jnp.bfloat16)
+    out_ref[:per, :cols] = high
+    out_ref[:per, cols:] = low[:, : width - cols]
     x = lax.axis_index("mp")
     res = residual_ref[...].astype(jnp.float32)
     token = lax.broadcasted_iota(jnp.int32, res.shape, 0)
@@ -129,9 +131,12 @@
     cols = dim // n_z
     rest, width = turn_ref.shape[1] // n_z, blocks_ref.shape[2]
     f32 = jnp.float32
-    ffn = jnp.concatenate(
-        [blocks_ref[i, :per, :cols].astype(f32) for i in range(n_z)], axis=1
-    )
+    pieces = []
+    for i in range(n_z):
+        high = blocks_ref[i, :per, :cols].astype(f32)
+        low = blocks_ref[i, :per, cols:].astype(f32)
+        pieces += [high[:, : width - cols] + low, high[:, width - cols :]]
+    ffn = jnp.concatenate(pieces, axis=1)
     for i in range(n_z):
         for c in range(width // LANES):
             turn_ref[c, i * rest : (i + 1) * rest] = blocks_ref[

time: 204 us -> 204 us (level)
  no operation moved by 1% of the time
where the time goes in v7:
time: 204 us; the launch traced here: 203 us
  blocking collectives  138 us (68%)
  starting transfers between devices  50.4 us (25%)
  Pallas kernels  4.68 us (2%)
  other arithmetic  4.12 us (2%)
  local copies, waits for them, and re-layouts  3.79 us (2%)
    all_gather x3, blocking collectives, gather_ring(): return lax.all_gather(value, (axis, 'sub'), axis_index_groups=rings(axis))  88.5 us
    all_to_all x2, starting transfers between devices, exchange_ring(): lax.all_to_all(copies, (axis, 'sub'), 0, 0, tiled=True, axis_index_groups...  48.3 us
    all_to_all x1, blocking collectives, copy_for_each(): lax.all_to_all(jnp.broadcast_to(value[None], (peers, *value.shape)), axis...  19.9 us
    all_to_all x1, blocking collectives, on_device(): parts = lax.all_to_all(part, 'mp', 0, 0, tiled=True)  16.6 us
    all_to_all x1, blocking collectives, on_device(): lax.all_to_all(packed, ('mp', 'sub'), 0, 0, tiled=True)  13.2 us
  transfers between devices with their start and end apart: 3, of which 0 were waited for; matrix products, arithmetic and copies ran while one was open for 4% of the time, Pallas kernels for 0%

profile of v7, /device:TPU:65, one launch (start us, length us, event | category | flops | bytes accessed | tf_op | source)
XLA Modules:
  0.0 203.4 jit_solution(17096783435806620185)
XLA Ops:
  0.6 0.0 copy-start
  0.6 0.9 copy-done
  1.5 0.7 split_columns.1
  2.2 44.7 %all-to-all-start = ((bf16[16,8,640]{2,1,0:T(8,128)(2,1)}), bf16[16,8,640]{2,1,0:T(8,128)(2,1)S(1)}, u32[]{:S(2)}, u32[]{:S(2)}) async-start(bf16[16,8,640]{2,1,0:T(8,128)(2,1)} %get-tuple-element.15), calls=%async_computation | async-start | bytes 327680 | tf_op jit(solution)/shard_map/all_to_all | solution.py:36
  46.9 0.1 shift_left.44
  47.0 0.0 copy-start.5
  47.0 1.4 copy.19
  48.5 0.5 shift_left.41
  48.9 0.0 copy-done.5
  49.0 1.3 fusion.5
  50.2 0.5 slice.16
  50.7 0.0 copy-start.1
  50.7 0.0 copy-start.2
  50.8 0.0 copy-start.3
  50.8 0.0 copy-start.6
  50.8 0.0 copy-start.7
  50.8 0.1 slice.17
  50.9 34.7 %all-gather = bf16[128,3968]{1,0:T(8,128)(2,1)S(1)} all-gather(bf16[8,3968]{1,0:T(8,128)(2,1)S(1)} %get-tuple-element.14), channel_id=2, replica_groups={{0,17,32,49,64,81,96,113,128,145,160,177,192,209,224,241},{1,16,33,48,6..., dimensions={0}, use_global_device_ids=true | all-gather | bytes 1079296 | tf_op jit(solution)/shard_map/all_gather | solution.py:32
  85.6 1.1 fusion.8
  86.7 0.0 copy-start.4
  86.7 0.0 all-to-all-done
  86.7 0.3 fusion.6
  87.0 0.1 copy.21
  87.2 16.6 %all_to_all.25.parts_ref = f32[8,16,288]{2,1,0:T(8,128)S(1)} all-to-all(f32[8,16,288]{2,1,0:T(8,128)S(1)} %bitcast.42), channel_id=1, replica_groups=mesh['groups'=2,'fsdp'=16,'mp'=8,'sub'=2] {'mp'}, dimensions={0} | all-to-all | bytes 294912 | tf_op jit(solution)/shard_map/all_to_all | solution.py:296
  103.8 0.0 copy-done.1
  103.8 0.0 copy-done.2
  103.8 0.0 copy-done.3
  103.8 0.6 pack_rows.1
  104.4 27.0 %all-gather.1 = bf16[512,384]{1,0:T(8,128)(2,1)S(1)} all-gather(bf16[32,384]{1,0:T(8,128)(2,1)S(1)} %pack_rows.1), channel_id=3, replica_groups={{0,17,32,49,64,81,96,113,128,145,160,177,192,209,224,241},{1,16,33,48,6..., dimensions={0}, use_global_device_ids=true | all-gather | bytes 417792 | tf_op jit(solution)/shard_map/all_gather | solution.py:32
  131.4 0.0 copy-done.6
  131.4 0.0 copy-done.7
  131.5 1.1 norm_rows.1
  132.6 3.6 %all-to-all-start.2 = ((bf16[8,16,768]{2,1,0:T(8,128)(2,1)}), bf16[8,16,768]{2,1,0:T(8,128)(2,1)S(1)}, u32[]{:S(2)}, u32[]{:S(2)}) async-start(bf16[8,16,768]{2,1,0:T(8,128)(2,1)} %get-tuple-element.23), calls=%async_computation.2 | async-start | bytes 393216 | tf_op jit(solution)/shard_map/all_to_all | solution.py:36
  136.2 26.8 %all-gather.2 = bf16[128,3968]{1,0:T(8,128)(2,1)S(1)} all-gather(bf16[16,3968]{1,0:T(8,128)(2,1)S(1)} %get-tuple-element.22), channel_id=4, replica_groups={{0,3,4,7,8,11,12,15},{1,2,5,6,9,10,13,14},{16,19,20,23,24,27,28,31},{17..., dimensions={0}, use_global_device_ids=true | all-gather | bytes 1142784 | tf_op jit(solution)/shard_map/all_gather | solution.py:32
  163.0 0.0 all-to-all-done.2
  163.0 0.1 pad_maximum_fusion.refs_0_
  163.1 2.1 %collective-permute-start = (bf16[128,4736]{1,0:T(8,128)(2,1)S(1)}, bf16[128,4736]{1,0:T(8,128)(2,1)S(1)}, u32[]{:S(2)}, u32[]{:S(2)}) collective-permute-start(bf16[128,4736]{1,0:T(8,128)(2,1)S(1)} %pad_maximum_fusion.refs_0_), channel_id=1, source_target_pairs={{0,1},{1,0},{2,3},{3,2},{4,5},{5,4},{6,7},{7,6},{8,9},{9,8},{10,11... | collective-permute-start | bytes 3637256 | tf_op jit(solution)/shard_map/ppermute | solution.py:308
  165.2 0.1 shift_left.49
  165.2 0.1 shift_left.50
  165.3 0.0 copy-done.4
  165.3 2.7 %fusion.4 = bf16[512,4608]{0,1:T(8,128)(2,1)S(1)} fusion(s32[4608]{0:T(1024)S(1)} %shift_left.50, s32[512,576]{0,1:T(8,128)} %param.16, bf16[512,36]{0,1:T(8,128)(2,1)S(1)} %copy-done.4), kind=kLoop, calls=%fused_computation.6 | loop fusion | flops 16515072 | bytes 5953536 | tf_op jit(solution)/shard_map/mul | solution.py:62
  168.0 0.0 collective-permute-done.refs_1_
  168.1 1.6 vocab_sums.1
  169.7 13.2 %all_to_all.26 = f32[16,4,128]{2,1,0:T(4,128)S(1)} all-to-all(f32[16,4,128]{2,1,0:T(4,128)S(1)} %get-tuple-element.24), channel_id=1, replica_groups=mesh['groups'=2,'fsdp'=16,'mp'=8,'sub'=2] {'mp','sub'}, dimensions={0} | all-to-all | bytes 65536 | tf_op jit(solution)/shard_map/all_to_all | solution.py:312
  182.9 19.9 %all_to_all.27.packed_ref = f32[16,4,128]{2,1,0:T(4,128)S(1)} all-to-all(f32[16,4,128]{2,1,0:T(4,128)S(1)} %broadcast_in_dim.8), channel_id=1, replica_groups=mesh['groups'=2,'fsdp'=16,'mp'=8,'sub'=2] {'fsdp'}, dimensions={0} | all-to-all | bytes 65536 | tf_op jit(solution)/shard_map/all_to_all | solution.py:21
  202.8 0.7 losses_of.1
  (7 shorter events, 0.1 us)
Async XLA Ops:
  0.6 0.9 copy-start
  2.2 84.5 %all-to-all-start = ((bf16[16,8,640]{2,1,0:T(8,128)(2,1)}), bf16[16,8,640]{2,1,0:T(8,128)(2,1)S(1)}, u32[]{:S(2)}, u32[]{:S(2)}) async-start(bf16[16,8,640]{2,1,0:T(8,128)(2,1)} %get-tuple-element.15), calls=%async_computation | async-start | bytes 327680 | tf_op jit(solution)/shard_map/all_to_all | solution.py:36
  47.0 1.9 copy-start.5
  50.7 53.1 %copy-start.1 = (bf16[8,4608]{1,0:T(8,128)(2,1)S(1)}, bf16[8,4608]{1,0:T(8,128)(2,1)}, u32[]{:S(2)}) copy-start(bf16[8,4608]{1,0:T(8,128)(2,1)} %residual_ref) | copy-start | bytes 221188
  50.7 53.1 %copy-start.2 = (s32[8]{0:T(128)S(1)}, s32[8]{0:T(128)}, u32[]{:S(2)}) copy-start(s32[8]{0:T(128)} %targets_ref) | copy-start | bytes 100
  50.8 53.0 %copy-start.3 = (s32[8]{0:T(128)S(1)}, s32[8]{0:T(128)}, u32[]{:S(2)}) copy-start(s32[8]{0:T(128)} %loss_mask_ref.1) | copy-start | bytes 100
  50.8 80.7 %copy-start.6 = (f32[4608]{0:T(1024)S(1)}, f32[4608]{0:T(1024)}, u32[]{:S(2)}) copy-start(f32[4608]{0:T(1024)} %param.14) | copy-start | bytes 55300
  50.8 80.7 %copy-start.7 = (f32[4608]{0:T(1024)S(1)}, f32[4608]{0:T(1024)}, u32[]{:S(2)}) copy-start(f32[4608]{0:T(1024)} %param.15) | copy-start | bytes 55300
  86.7 78.7 %copy-start.4 = (bf16[512,36]{0,1:T(8,128)(2,1)S(1)}, bf16[512,36]{0,1:T(8,128)(2,1)}, u32[]{:S(2)}) copy-start(bf16[512,36]{0,1:T(8,128)(2,1)} %param.17) | copy-start | bytes 110596
  132.6 30.4 %all-to-all-start.2 = ((bf16[8,16,768]{2,1,0:T(8,128)(2,1)}), bf16[8,16,768]{2,1,0:T(8,128)(2,1)S(1)}, u32[]{:S(2)}, u32[]{:S(2)}) async-start(bf16[8,16,768]{2,1,0:T(8,128)(2,1)} %get-tuple-element.23), calls=%async_computation.2 | async-start | bytes 393216 | tf_op jit(solution)/shard_map/all_to_all | solution.py:36
  163.1 5.0 %collective-permute-start = (bf16[128,4736]{1,0:T(8,128)(2,1)S(1)}, bf16[128,4736]{1,0:T(8,128)(2,1)S(1)}, u32[]{:S(2)}, u32[]{:S(2)}) collective-permute-start(bf16[128,4736]{1,0:T(8,128)(2,1)S(1)} %pad_maximum_fusion.refs_0_), channel_id=1, source_target_pairs={{0,1},{1,0},{2,3},{3,2},{4,5},{5,4},{6,7},{7,6},{8,9},{9,8},{10,11... | collective-permute-start | bytes 3637256 | tf_op jit(solution)/shard_map/ppermute | solution.py:308

commit v8 on v7

--- a/solution.py
+++ b/solution.py
@@ -12,6 +12,7 @@
 CAP = 30.0
 GATHER_BYTES = 1 << 20
 LANES = 128
+DIGITS = 4
 VMEM = pl.BlockSpec(memory_space=pltpu.VMEM)
 SMEM = pl.BlockSpec(memory_space=pltpu.SMEM)
 
@@ -100,12 +101,13 @@
     token = lax.broadcasted_iota(jnp.int32, res.shape, 0)
     res = jnp.sum(jnp.where(token == x, res, 0.0), axis=0, keepdims=True)
     rows = [res[:, c : c + width] for c in range(0, res.shape[1], width)]
-    goal = targets_ref[x]
-    values = (goal & 255, (goal >> 8) & 255, goal >> 16, loss_mask_ref[x])
     lane = lax.broadcasted_iota(jnp.int32, (1, width), 1)
     digit = jnp.zeros((1, width), jnp.int32)
-    for i, value in enumerate(values):
-        digit = jnp.where(lane == i, value, digit)
+    for i in range(targets_ref.shape[0]):
+        goal = targets_ref[i]
+        values = (goal & 255, (goal >> 8) & 255, goal >> 16, loss_mask_ref[i])
+        for v, value in enumerate(values):
+            digit = jnp.where(lane == DIGITS * i + v, value, digit)
     rows.append(digit.astype(jnp.float32))
     rows.append(jnp.zeros((out_ref.shape[0] - per - len(rows), width), jnp.float32))
     out_ref[per:] = jnp.concatenate(rows, axis=0).astype(jnp.bfloat16)
@@ -124,7 +126,7 @@
     )(targets, loss_mask, parts, residual)
 
 
-def norm_kernel(blocks_ref, post_ref, final_ref, head_ref, tail_ref, turn_ref):
+def norm_kernel(blocks_ref, post_ref, final_ref, head_ref, tail_ref, digit_ref, turn_ref):
     n_z = blocks_ref.shape[0]
     per, cut = head_ref.shape
     dim = post_ref.shape[1]
@@ -154,11 +156,15 @@
     scale = lax.rsqrt(jnp.sum(stream * stream, axis=1, keepdims=True) / dim + EPS)
     states = (stream * scale * final_ref[...]).astype(jnp.bfloat16)
     head_ref[...] = states[:, :cut]
-    tail = jnp.concatenate([states[:, cut:], turned(dim // width, 0).astype(jnp.bfloat16)], axis=1)
-    tail_ref[...] = jnp.broadcast_to(tail[None], tail_ref.shape)
-
-
-def norm_rows(blocks, post_gain, final_gain, per, cut, copies):
+    tail_ref[...] = jnp.broadcast_to(states[:, cut:][None], tail_ref.shape)
+    digits = turned(dim // width, 0)
+    rows = [digits] + [
+        pltpu.roll(digits, LANES - DIGITS * i, axis=1) for i in range(1, digit_ref.shape[0] // n_z)
+    ]
+    digit_ref[...] = jnp.concatenate(rows, axis=0).astype(jnp.bfloat16)
+
+
+def norm_rows(blocks, post_gain, final_gain, per, cut, copies, toks):
     n_z, rows, width = blocks.shape
     dim = post_gain.shape[0]
     return pl.pallas_call(
@@ -166,7 +172,8 @@
         in_specs=[VMEM] * 3,
         out_shape=(
             jax.ShapeDtypeStruct((per, cut), blocks.dtype),
-            jax.ShapeDtypeStruct((copies, per, dim - cut + LANES), blocks.dtype),
+            jax.ShapeDtypeStruct((copies, per, dim - cut), blocks.dtype),
+            jax.ShapeDtypeStruct((toks * n_z, LANES), blocks.dtype),
         ),
         scratch_shapes=[pltpu.VMEM((width // LANES, n_z * (rows - per), LANES), jnp.float32)],
         compiler_params=pltpu.CompilerParams(vmem_limit_bytes=8 << 20),
@@ -183,7 +190,15 @@
         st_ref[h] = halves[h][...]
     states = st_ref.reshape(n_s * held, st_ref.shape[2])
     acc_ref[...] = dot_f32(states[:, :dim], embed_ref[...], ((1,), (0,)))
-    digits = states[:, dim:].astype(jnp.float32)
+    rings_of = [half[:, dim:].astype(jnp.float32) for half in halves]
+    token = lax.broadcasted_iota(jnp.int32, rings_of[0].shape, 0) // n_z
+    digits = jnp.concatenate(
+        [
+            jnp.where((token + x) % n_s == 0, rings_of[h], rings_of[n_s - 1 - h])
+            for h in range(n_s)
+        ],
+        axis=0,
+    )
     goal = digits[:, 0:1] + 256.0 * digits[:, 1:2] + 65536.0 * digits[:, 2:3]
     goal = goal.astype(jnp.int32) - first
     sums = jnp.zeros((n_s * held, LANES), jnp.float32)
@@ -301,10 +316,11 @@
     blocks, post_gain, final_gain = lax.optimization_barrier((blocks, post_gain, final_gain))
 
     cut = gather_cut(per_x, dim, n_x)
-    head, tail = norm_rows(blocks, post_gain, final_gain, per_x, cut, n_x)
+    head, tail, digits = norm_rows(blocks, post_gain, final_gain, per_x, cut, n_x, toks)
     tail = exchange_ring(tail, "mp")
     head = gather_ring(head, "mp")
-    own = jnp.concatenate([head.reshape(held, cut), tail.reshape(held, dim - cut + LANES)], axis=1)
+    own = [head.reshape(held, cut), tail.reshape(held, dim - cut), digits]
+    own = jnp.concatenate(own, axis=1)
     far = lax.ppermute(own, "sub", [(i, n_s - 1 - i) for i in range(n_s)])
     embed = dequant_embed(embed_packed, embed_scale)
     packed, mask = vocab_sums((own, far), embed.T, n_z, n_x * n_s)

time: 204 us -> 204 us (level)
  no operation moved by 1% of the time
where the time goes in v8:
time: 204 us; the launch traced here: 203 us
  blocking collectives  137 us (67%)
  starting transfers between devices  50.6 us (25%)
  Pallas kernels  4.67 us (2%)
  other arithmetic  4.12 us (2%)
  local copies, waits for them, and re-layouts  3.79 us (2%)
    all_gather x3, blocking collectives, gather_ring(): return lax.all_gather(value, (axis, 'sub'), axis_index_groups=rings(axis))  88.5 us
    all_to_all x2, starting transfers between devices, exchange_ring(): lax.all_to_all(copies, (axis, 'sub'), 0, 0, tiled=True, axis_index_groups...  48.3 us
    all_to_all x1, blocking collectives, copy_for_each(): lax.all_to_all(jnp.broadcast_to(value[None], (peers, *value.shape)), axis...  20.3 us
    all_to_all x1, blocking collectives, on_device(): parts = lax.all_to_all(part, 'mp', 0, 0, tiled=True)  16.6 us
    all_to_all x1, blocking collectives, on_device(): lax.all_to_all(packed, ('mp', 'sub'), 0, 0, tiled=True)  12 us
  transfers between devices with their start and end apart: 3, of which 0 were waited for; matrix products, arithmetic and copies ran while one was open for 4% of the time, Pallas kernels for 0%

profile of v8, /device:TPU:65, one launch (start us, length us, event | category | flops | bytes accessed | tf_op | source)
XLA Modules:
  0.0 202.9 jit_solution(6032796718932731624)
XLA Ops:
  0.6 0.0 copy-start
  0.6 0.9 copy-done
  1.5 0.7 split_columns.1
  2.2 44.7 %all-to-all-start = ((bf16[16,8,640]{2,1,0:T(8,128)(2,1)}), bf16[16,8,640]{2,1,0:T(8,128)(2,1)S(1)}, u32[]{:S(2)}, u32[]{:S(2)}) async-start(bf16[16,8,640]{2,1,0:T(8,128)(2,1)} %get-tuple-element.16), calls=%async_computation | async-start | bytes 327680 | tf_op jit(solution)/shard_map/all_to_all | solution.py:37
  46.9 0.1 shift_left.44
  47.0 0.0 copy-start.5
  47.0 1.4 copy.19
  48.5 0.5 shift_left.41
  48.9 0.0 copy-done.5
  49.0 1.3 fusion.5
  50.2 0.5 slice.16
  50.7 0.0 copy-start.1
  50.7 0.0 copy-start.2
  50.8 0.0 copy-start.3
  50.8 0.0 copy-start.6
  50.8 0.0 copy-start.7
  50.8 0.1 slice.17
  50.9 34.7 %all-gather = bf16[128,3968]{1,0:T(8,128)(2,1)S(1)} all-gather(bf16[8,3968]{1,0:T(8,128)(2,1)S(1)} %get-tuple-element.15), channel_id=2, replica_groups={{0,17,32,49,64,81,96,113,128,145,160,177,192,209,224,241},{1,16,33,48,6..., dimensions={0}, use_global_device_ids=true | all-gather | bytes 1079296 | tf_op jit(solution)/shard_map/all_gather | solution.py:33
  85.6 0.0 copy-start.4
  85.6 1.1 fusion.8
  86.7 0.0 all-to-all-done
  86.7 0.3 fusion.6
  87.0 0.1 copy.21
  87.2 16.6 %all_to_all.25.parts_ref = f32[8,16,288]{2,1,0:T(8,128)S(1)} all-to-all(f32[8,16,288]{2,1,0:T(8,128)S(1)} %bitcast.41), channel_id=1, replica_groups=mesh['groups'=2,'fsdp'=16,'mp'=8,'sub'=2] {'mp'}, dimensions={0} | all-to-all | bytes 294912 | tf_op jit(solution)/shard_map/all_to_all | solution.py:311
  103.8 0.0 copy-done.1
  103.8 0.0 copy-done.2
  103.8 0.0 copy-done.3
  103.8 0.6 pack_rows.1
  104.4 27.0 %all-gather.1 = bf16[512,384]{1,0:T(8,128)(2,1)S(1)} all-gather(bf16[32,384]{1,0:T(8,128)(2,1)S(1)} %pack_rows.1), channel_id=3, replica_groups={{0,17,32,49,64,81,96,113,128,145,160,177,192,209,224,241},{1,16,33,48,6..., dimensions={0}, use_global_device_ids=true | all-gather | bytes 417792 | tf_op jit(solution)/shard_map/all_gather | solution.py:33
  131.4 0.0 copy-done.6
  131.4 0.0 copy-done.7
  131.5 1.1 norm_rows.1
  132.6 3.6 %all-to-all-start.2 = ((bf16[8,16,640]{2,1,0:T(8,128)(2,1)}), bf16[8,16,640]{2,1,0:T(8,128)(2,1)S(1)}, u32[]{:S(2)}, u32[]{:S(2)}) async-start(bf16[8,16,640]{2,1,0:T(8,128)(2,1)} %get-tuple-element.24), calls=%async_computation.2 | async-start | bytes 327680 | tf_op jit(solution)/shard_map/all_to_all | solution.py:37
  136.2 26.8 %all-gather.2 = bf16[128,3968]{1,0:T(8,128)(2,1)S(1)} all-gather(bf16[16,3968]{1,0:T(8,128)(2,1)S(1)} %get-tuple-element.23), channel_id=4, replica_groups={{0,3,4,7,8,11,12,15},{1,2,5,6,9,10,13,14},{16,19,20,23,24,27,28,31},{17..., dimensions={0}, use_global_device_ids=true | all-gather | bytes 1142784 | tf_op jit(solution)/shard_map/all_gather | solution.py:33
  163.0 0.0 all-to-all-done.2
  163.0 0.1 pad_maximum_fusion.refs_0_
  163.1 2.3 %collective-permute-start = (bf16[128,4736]{1,0:T(8,128)(2,1)S(1)}, bf16[128,4736]{1,0:T(8,128)(2,1)S(1)}, u32[]{:S(2)}, u32[]{:S(2)}) collective-permute-start(bf16[128,4736]{1,0:T(8,128)(2,1)S(1)} %pad_maximum_fusion.refs_0_), channel_id=1, source_target_pairs={{0,1},{1,0},{2,3},{3,2},{4,5},{5,4},{6,7},{7,6},{8,9},{9,8},{10,11... | collective-permute-start | bytes 3637256 | tf_op jit(solution)/shard_map/ppermute | solution.py:324
  165.4 0.1 shift_left.49
  165.5 0.1 shift_left.50
  165.6 0.0 copy-done.4
  165.6 2.7 %fusion.4 = bf16[512,4608]{0,1:T(8,128)(2,1)S(1)} fusion(s32[4608]{0:T(1024)S(1)} %shift_left.50, s32[512,576]{0,1:T(8,128)} %param.16, bf16[512,36]{0,1:T(8,128)(2,1)S(1)} %copy-done.4), kind=kLoop, calls=%fused_computation.6 | loop fusion | flops 16515072 | bytes 5953536 | tf_op jit(solution)/shard_map/mul | solution.py:63
  168.3 0.0 collective-permute-done.refs_1_
  168.3 1.6 vocab_sums.1
  169.9 12.0 %all_to_all.26 = f32[16,4,128]{2,1,0:T(4,128)S(1)} all-to-all(f32[16,4,128]{2,1,0:T(4,128)S(1)} %get-tuple-element.26), channel_id=1, replica_groups=mesh['groups'=2,'fsdp'=16,'mp'=8,'sub'=2] {'mp','sub'}, dimensions={0} | all-to-all | bytes 65536 | tf_op jit(solution)/shard_map/all_to_all | solution.py:328
  181.9 20.3 %all_to_all.27.packed_ref = f32[16,4,128]{2,1,0:T(4,128)S(1)} all-to-all(f32[16,4,128]{2,1,0:T(4,128)S(1)} %broadcast_in_dim.8), channel_id=1, replica_groups=mesh['groups'=2,'fsdp'=16,'mp'=8,'sub'=2] {'fsdp'}, dimensions={0} | all-to-all | bytes 65536 | tf_op jit(solution)/shard_map/all_to_all | solution.py:22
  202.2 0.7 losses_of.1
  (7 shorter events, 0.1 us)
Async XLA Ops:
  0.6 0.9 copy-start
  2.2 84.5 %all-to-all-start = ((bf16[16,8,640]{2,1,0:T(8,128)(2,1)}), bf16[16,8,640]{2,1,0:T(8,128)(2,1)S(1)}, u32[]{:S(2)}, u32[]{:S(2)}) async-start(bf16[16,8,640]{2,1,0:T(8,128)(2,1)} %get-tuple-element.16), calls=%async_computation | async-start | bytes 327680 | tf_op jit(solution)/shard_map/all_to_all | solution.py:37
  47.0 1.9 copy-start.5
  50.7 53.1 %copy-start.1 = (bf16[8,4608]{1,0:T(8,128)(2,1)S(1)}, bf16[8,4608]{1,0:T(8,128)(2,1)}, u32[]{:S(2)}) copy-start(bf16[8,4608]{1,0:T(8,128)(2,1)} %residual_ref) | copy-start | bytes 221188
  50.7 53.0 %copy-start.2 = (s32[8]{0:T(128)S(1)}, s32[8]{0:T(128)}, u32[]{:S(2)}) copy-start(s32[8]{0:T(128)} %targets_ref) | copy-start | bytes 100
  50.8 53.0 %copy-start.3 = (s32[8]{0:T(128)S(1)}, s32[8]{0:T(128)}, u32[]{:S(2)}) copy-start(s32[8]{0:T(128)} %loss_mask_ref.1) | copy-start | bytes 100
  50.8 80.7 %copy-start.6 = (f32[4608]{0:T(1024)S(1)}, f32[4608]{0:T(1024)}, u32[]{:S(2)}) copy-start(f32[4608]{0:T(1024)} %param.14) | copy-start | bytes 55300
  50.8 80.7 %copy-start.7 = (f32[4608]{0:T(1024)S(1)}, f32[4608]{0:T(1024)}, u32[]{:S(2)}) copy-start(f32[4608]{0:T(1024)} %param.15) | copy-start | bytes 55300
  85.6 80.0 %copy-start.4 = (bf16[512,36]{0,1:T(8,128)(2,1)S(1)}, bf16[512,36]{0,1:T(8,128)(2,1)}, u32[]{:S(2)}) copy-start(bf16[512,36]{0,1:T(8,128)(2,1)} %param.17) | copy-start | bytes 110596
  132.6 30.4 %all-to-all-start.2 = ((bf16[8,16,640]{2,1,0:T(8,128)(2,1)}), bf16[8,16,640]{2,1,0:T(8,128)(2,1)S(1)}, u32[]{:S(2)}, u32[]{:S(2)}) async-start(bf16[8,16,640]{2,1,0:T(8,128)(2,1)} %get-tuple-element.24), calls=%async_computation.2 | async-start | bytes 327680 | tf_op jit(solution)/shard_map/all_to_all | solution.py:37
  163.1 5.2 %collective-permute-start = (bf16[128,4736]{1,0:T(8,128)(2,1)S(1)}, bf16[128,4736]{1,0:T(8,128)(2,1)S(1)}, u32[]{:S(2)}, u32[]{:S(2)}) collective-permute-start(bf16[128,4736]{1,0:T(8,128)(2,1)S(1)} %pad_maximum_fusion.refs_0_), channel_id=1, source_target_pairs={{0,1},{1,0},{2,3},{3,2},{4,5},{5,4},{6,7},{7,6},{8,9},{9,8},{10,11... | collective-permute-start | bytes 3637256 | tf_op jit(solution)/shard_map/ppermute | solution.py:324

commit v9 on v8

--- a/solution.py
+++ b/solution.py
@@ -93,9 +93,12 @@
     width = out_ref.shape[1]
     ffn = jnp.sum(parts_ref[...], axis=0)
     high = ffn.astype(jnp.bfloat16)
-    low = (ffn - high.astype(jnp.float32)).astype(jnp.bfloat16)
+    low = ffn - high.astype(jnp.float32)
+    spare, half = width - cols, per // 2
     out_ref[:per, :cols] = high
-    out_ref[:per, cols:] = low[:, : width - cols]
+    out_ref[:per, cols:] = low[:, :spare].astype(jnp.bfloat16)
+    low = jnp.concatenate([low[:half, spare:], low[half:, spare:]], axis=1)
+    out_ref[per : per + half] = low.astype(jnp.bfloat16)
     x = lax.axis_index("mp")
     res = residual_ref[...].astype(jnp.float32)
     token = lax.broadcasted_iota(jnp.int32, res.shape, 0)
@@ -109,18 +112,18 @@
         for v, value in enumerate(values):
             digit = jnp.where(lane == DIGITS * i + v, value, digit)
     rows.append(digit.astype(jnp.float32))
-    rows.append(jnp.zeros((out_ref.shape[0] - per - len(rows), width), jnp.float32))
-    out_ref[per:] = jnp.concatenate(rows, axis=0).astype(jnp.bfloat16)
+    rows.append(jnp.zeros((out_ref.shape[0] - per - half - len(rows), width), jnp.float32))
+    out_ref[per + half :] = jnp.concatenate(rows, axis=0).astype(jnp.bfloat16)
 
 
 def pack_rows(targets, loss_mask, parts, residual):
     per, cols = parts.shape[1:]
     width = cols + -cols % LANES
-    count = per + residual.shape[1] // width + 1
+    count = per + per // 2 + residual.shape[1] // width + 1
     return pl.pallas_call(
         pack_kernel,
         in_specs=[SMEM, SMEM, VMEM, VMEM],
-        out_shape=jax.ShapeDtypeStruct((count + -count % 16, width), jnp.bfloat16),
+        out_shape=jax.ShapeDtypeStruct((count + -count % 8, width), jnp.bfloat16),
         compiler_params=pltpu.CompilerParams(vmem_limit_bytes=4 << 20),
         name="pack_rows",
     )(targets, loss_mask, parts, residual)
@@ -133,16 +136,19 @@
     cols = dim // n_z
     rest, width = turn_ref.shape[1] // n_z, blocks_ref.shape[2]
     f32 = jnp.float32
+    lead = per + per // 2
     pieces = []
     for i in range(n_z):
         high = blocks_ref[i, :per, :cols].astype(f32)
         low = blocks_ref[i, :per, cols:].astype(f32)
-        pieces += [high[:, : width - cols] + low, high[:, width - cols :]]
+        rest_low = blocks_ref[i, per:lead].astype(f32)
+        rest_low = jnp.concatenate([rest_low[:, : width // 2], rest_low[:, width // 2 :]], axis=0)
+        pieces += [high[:, : width - cols] + low, high[:, width - cols :] + rest_low]
     ffn = jnp.concatenate(pieces, axis=1)
     for i in range(n_z):
         for c in range(width // LANES):
             turn_ref[c, i * rest : (i + 1) * rest] = blocks_ref[
-                i, per:, c * LANES : (c + 1) * LANES
+                i, lead:, c * LANES : (c + 1) * LANES
             ].astype(f32)
 
     def turned(r, c):
@@ -175,7 +181,7 @@
             jax.ShapeDtypeStruct((copies, per, dim - cut), blocks.dtype),
             jax.ShapeDtypeStruct((toks * n_z, LANES), blocks.dtype),
         ),
-        scratch_shapes=[pltpu.VMEM((width // LANES, n_z * (rows - per), LANES), jnp.float32)],
+        scratch_shapes=[pltpu.VMEM((width // LANES, n_z * (rows - per - per // 2), LANES), jnp.float32)],
         compiler_params=pltpu.CompilerParams(vmem_limit_bytes=8 << 20),
         name="norm_rows",
     )(blocks, post_gain[None], final_gain[None])

time: 204 us -> 205 us (level)
  no operation moved by 1% of the time
where the time goes in v9:
time: 205 us; the launch traced here: 204 us
  blocking collectives  138 us (67%)
  starting transfers between devices  50.6 us (25%)
  Pallas kernels  4.76 us (2%)
  other arithmetic  4.12 us (2%)
  local copies, waits for them, and re-layouts  3.79 us (2%)
    all_gather x3, blocking collectives, gather_ring(): return lax.all_gather(value, (axis, 'sub'), axis_index_groups=rings(axis))  89.2 us
    all_to_all x2, starting transfers between devices, exchange_ring(): lax.all_to_all(copies, (axis, 'sub'), 0, 0, tiled=True, axis_index_groups...  48.3 us
    all_to_all x1, blocking collectives, copy_for_each(): lax.all_to_all(jnp.broadcast_to(value[None], (peers, *value.shape)), axis...  20.6 us
    all_to_all x1, blocking collectives, on_device(): parts = lax.all_to_all(part, 'mp', 0, 0, tiled=True)  16.6 us
    all_to_all x1, blocking collectives, on_device(): lax.all_to_all(packed, ('mp', 'sub'), 0, 0, tiled=True)  11.8 us
  transfers between devices with their start and end apart: 3, of which 0 were waited for; matrix products, arithmetic and copies ran while one was open for 4% of the time, Pallas kernels for 0%

profile of v9, /device:TPU:65, one launch (start us, length us, event | category | flops | bytes accessed | tf_op | source)
XLA Modules:
  0.0 203.7 jit_solution(7266319570271031528)
XLA Ops:
  0.6 0.0 copy-start
  0.6 0.9 copy-done
  1.5 0.7 split_columns.1
  2.2 44.7 %all-to-all-start = ((bf16[16,8,640]{2,1,0:T(8,128)(2,1)}), bf16[16,8,640]{2,1,0:T(8,128)(2,1)S(1)}, u32[]{:S(2)}, u32[]{:S(2)}) async-start(bf16[16,8,640]{2,1,0:T(8,128)(2,1)} %get-tuple-element.16), calls=%async_computation | async-start | bytes 327680 | tf_op jit(solution)/shard_map/all_to_all | solution.py:37
  46.9 0.1 shift_left.44
  47.0 0.0 copy-start.5
  47.0 1.4 copy.19
  48.5 0.5 shift_left.41
  48.9 0.0 copy-done.5
  49.0 1.3 fusion.5
  50.2 0.5 slice.16
  50.7 0.0 copy-start.1
  50.7 0.0 copy-start.2
  50.8 0.0 copy-start.3
  50.8 0.0 copy-start.6
  50.8 0.0 copy-start.7
  50.8 0.1 slice.17
  50.9 34.7 %all-gather = bf16[128,3968]{1,0:T(8,128)(2,1)S(1)} all-gather(bf16[8,3968]{1,0:T(8,128)(2,1)S(1)} %get-tuple-element.15), channel_id=2, replica_groups={{0,17,32,49,64,81,96,113,128,145,160,177,192,209,224,241},{1,16,33,48,6..., dimensions={0}, use_global_device_ids=true | all-gather | bytes 1079296 | tf_op jit(solution)/shard_map/all_gather | solution.py:33
  85.6 1.1 fusion.8
  86.7 0.0 copy-start.4
  86.7 0.0 all-to-all-done
  86.7 0.3 fusion.6
  87.0 0.1 copy.21
  87.2 16.6 %all_to_all.25.parts_ref = f32[8,16,288]{2,1,0:T(8,128)S(1)} all-to-all(f32[8,16,288]{2,1,0:T(8,128)S(1)} %bitcast.41), channel_id=1, replica_groups=mesh['groups'=2,'fsdp'=16,'mp'=8,'sub'=2] {'mp'}, dimensions={0} | all-to-all | bytes 294912 | tf_op jit(solution)/shard_map/all_to_all | solution.py:317
  103.8 0.0 copy-done.1
  103.8 0.0 copy-done.2
  103.8 0.0 copy-done.3
  103.8 0.6 pack_rows.1
  104.4 27.5 %all-gather.1 = bf16[640,384]{1,0:T(8,128)(2,1)S(1)} all-gather(bf16[40,384]{1,0:T(8,128)(2,1)S(1)} %pack_rows.1), channel_id=3, replica_groups={{0,17,32,49,64,81,96,113,128,145,160,177,192,209,224,241},{1,16,33,48,6..., dimensions={0}, use_global_device_ids=true | all-gather | bytes 522240 | tf_op jit(solution)/shard_map/all_gather | solution.py:33
  132.0 0.0 copy-done.6
  132.0 0.0 copy-done.7
  132.0 1.2 norm_rows.1
  133.2 3.6 %all-to-all-start.2 = ((bf16[8,16,640]{2,1,0:T(8,128)(2,1)}), bf16[8,16,640]{2,1,0:T(8,128)(2,1)S(1)}, u32[]{:S(2)}, u32[]{:S(2)}) async-start(bf16[8,16,640]{2,1,0:T(8,128)(2,1)} %get-tuple-element.24), calls=%async_computation.2 | async-start | bytes 327680 | tf_op jit(solution)/shard_map/all_to_all | solution.py:37
  136.8 26.9 %all-gather.2 = bf16[128,3968]{1,0:T(8,128)(2,1)S(1)} all-gather(bf16[16,3968]{1,0:T(8,128)(2,1)S(1)} %get-tuple-element.23), channel_id=4, replica_groups={{0,3,4,7,8,11,12,15},{1,2,5,6,9,10,13,14},{16,19,20,23,24,27,28,31},{17..., dimensions={0}, use_global_device_ids=true | all-gather | bytes 1142784 | tf_op jit(solution)/shard_map/all_gather | solution.py:33
  163.8 0.0 all-to-all-done.2
  163.8 0.1 pad_maximum_fusion.refs_0_
  163.9 2.3 %collective-permute-start = (bf16[128,4736]{1,0:T(8,128)(2,1)S(1)}, bf16[128,4736]{1,0:T(8,128)(2,1)S(1)}, u32[]{:S(2)}, u32[]{:S(2)}) collective-permute-start(bf16[128,4736]{1,0:T(8,128)(2,1)S(1)} %pad_maximum_fusion.refs_0_), channel_id=1, source_target_pairs={{0,1},{1,0},{2,3},{3,2},{4,5},{5,4},{6,7},{7,6},{8,9},{9,8},{10,11... | collective-permute-start | bytes 3637256 | tf_op jit(solution)/shard_map/ppermute | solution.py:330
  166.2 0.1 shift_left.49
  166.3 0.1 shift_left.50
  166.3 0.0 copy-done.4
  166.3 2.7 %fusion.4 = bf16[512,4608]{0,1:T(8,128)(2,1)S(1)} fusion(s32[4608]{0:T(1024)S(1)} %shift_left.50, s32[512,576]{0,1:T(8,128)} %param.16, bf16[512,36]{0,1:T(8,128)(2,1)S(1)} %copy-done.4), kind=kLoop, calls=%fused_computation.6 | loop fusion | flops 16515072 | bytes 5953536 | tf_op jit(solution)/shard_map/mul | solution.py:63
  169.1 0.0 collective-permute-done.refs_1_
  169.1 1.6 vocab_sums.1
  170.7 11.8 %all_to_all.26 = f32[16,4,128]{2,1,0:T(4,128)S(1)} all-to-all(f32[16,4,128]{2,1,0:T(4,128)S(1)} %get-tuple-element.26), channel_id=1, replica_groups=mesh['groups'=2,'fsdp'=16,'mp'=8,'sub'=2] {'mp','sub'}, dimensions={0} | all-to-all | bytes 65536 | tf_op jit(solution)/shard_map/all_to_all | solution.py:334
  182.5 20.6 %all_to_all.27.packed_ref = f32[16,4,128]{2,1,0:T(4,128)S(1)} all-to-all(f32[16,4,128]{2,1,0:T(4,128)S(1)} %broadcast_in_dim.8), channel_id=1, replica_groups=mesh['groups'=2,'fsdp'=16,'mp'=8,'sub'=2] {'fsdp'}, dimensions={0} | all-to-all | bytes 65536 | tf_op jit(solution)/shard_map/all_to_all | solution.py:22
  203.0 0.7 losses_of.1
  (7 shorter events, 0.1 us)
Async XLA Ops:
  0.6 0.9 copy-start
  2.2 84.5 %all-to-all-start = ((bf16[16,8,640]{2,1,0:T(8,128)(2,1)}), bf16[16,8,640]{2,1,0:T(8,128)(2,1)S(1)}, u32[]{:S(2)}, u32[]{:S(2)}) async-start(bf16[16,8,640]{2,1,0:T(8,128)(2,1)} %get-tuple-element.16), calls=%async_computation | async-start | bytes 327680 | tf_op jit(solution)/shard_map/all_to_all | solution.py:37
  47.0 1.9 copy-start.5
  50.7 53.1 %copy-start.1 = (bf16[8,4608]{1,0:T(8,128)(2,1)S(1)}, bf16[8,4608]{1,0:T(8,128)(2,1)}, u32[]{:S(2)}) copy-start(bf16[8,4608]{1,0:T(8,128)(2,1)} %residual_ref) | copy-start | bytes 221188
  50.7 53.1 %copy-start.2 = (s32[8]{0:T(128)S(1)}, s32[8]{0:T(128)}, u32[]{:S(2)}) copy-start(s32[8]{0:T(128)} %targets_ref) | copy-start | bytes 100
  50.8 53.0 %copy-start.3 = (s32[8]{0:T(128)S(1)}, s32[8]{0:T(128)}, u32[]{:S(2)}) copy-start(s32[8]{0:T(128)} %loss_mask_ref.1) | copy-start | bytes 100
  50.8 81.2 %copy-start.6 = (f32[4608]{0:T(1024)S(1)}, f32[4608]{0:T(1024)}, u32[]{:S(2)}) copy-start(f32[4608]{0:T(1024)} %param.14) | copy-start | bytes 55300
  50.8 81.2 %copy-start.7 = (f32[4608]{0:T(1024)S(1)}, f32[4608]{0:T(1024)}, u32[]{:S(2)}) copy-start(f32[4608]{0:T(1024)} %param.15) | copy-start | bytes 55300
  86.7 79.7 %copy-start.4 = (bf16[512,36]{0,1:T(8,128)(2,1)S(1)}, bf16[512,36]{0,1:T(8,128)(2,1)}, u32[]{:S(2)}) copy-start(bf16[512,36]{0,1:T(8,128)(2,1)} %param.17) | copy-start | bytes 110596
  133.2 30.5 %all-to-all-start.2 = ((bf16[8,16,640]{2,1,0:T(8,128)(2,1)}), bf16[8,16,640]{2,1,0:T(8,128)(2,1)S(1)}, u32[]{:S(2)}, u32[]{:S(2)}) async-start(bf16[8,16,640]{2,1,0:T(8,128)(2,1)} %get-tuple-element.24), calls=%async_computation.2 | async-start | bytes 327680 | tf_op jit(solution)/shard_map/all_to_all | solution.py:37
  163.9 5.2 %collective-permute-start = (bf16[128,4736]{1,0:T(8,128)(2,1)S(1)}, bf16[128,4736]{1,0:T(8,128)(2,1)S(1)}, u32[]{:S(2)}, u32[]{:S(2)}) collective-permute-start(bf16[128,4736]{1,0:T(8,128)(2,1)S(1)} %pad_maximum_fusion.refs_0_), channel_id=1, source_target_pairs={{0,1},{1,0},{2,3},{3,2},{4,5},{5,4},{6,7},{7,6},{8,9},{9,8},{10,11... | collective-permute-start | bytes 3637256 | tf_op jit(solution)/shard_map/ppermute | solution.py:330

commit v10 on v9

--- a/solution.py
+++ b/solution.py
@@ -50,13 +50,6 @@
     return jnp.right_shift(lifted, 28)
 
 
-def dequant_down(words, scales):
-    cols = words.shape[1]
-    codes = signed_planes(words).astype(jnp.bfloat16)
-    grouped = codes.reshape(scales.shape[0], -1, cols) * scales[:, None, :]
-    return grouped.reshape(-1, cols)
-
-
 def dequant_embed(words, scales):
     rows = words.shape[0]
     codes = signed_planes(words).astype(jnp.bfloat16)
@@ -68,16 +61,31 @@
     return lax.dot_general(a, b, (dims, ((), ())), preferred_element_type=jnp.float32)
 
 
-def split_kernel(hidden_ref, head_ref, tail_ref):
+def split_kernel(span, hidden_ref, head_ref, tail_ref):
+    rows, width = hidden_ref.shape
     cut = head_ref.shape[1]
-    head_ref[...] = hidden_ref[:, :cut]
-    tail_ref[...] = jnp.broadcast_to(hidden_ref[:, cut:][None], tail_ref.shape)
-
-
-def split_columns(hidden, cut, copies):
+    place = lax.broadcasted_iota(jnp.int32, (span, span), 1)
+    unit = place % (span // 8) * 8 + place // (span // 8)
+    order = jnp.where(lax.broadcasted_iota(jnp.int32, (span, span), 0) == unit, 1.0, 0.0)
+    hidden = hidden_ref[...].astype(jnp.float32)
+    tiles = [hidden[:, c : c + span] for c in range(0, width, span)]
+    tiles = jnp.concatenate(tiles, axis=0).astype(jnp.bfloat16)
+    turned = dot_f32(tiles, order.astype(jnp.bfloat16), ((1,), (0,)))
+    for i, c in enumerate(range(0, width, span)):
+        tile = turned[i * rows : (i + 1) * rows].astype(jnp.bfloat16)
+        if c < cut:
+            head_ref[:, c : c + span] = tile
+        else:
+            c -= cut
+            tail_ref[:, :, c : c + span] = jnp.broadcast_to(
+                tile[None], (tail_ref.shape[0], rows, span)
+            )
+
+
+def split_columns(hidden, cut, copies, span):
     rows, width = hidden.shape
     return pl.pallas_call(
-        split_kernel,
+        functools.partial(split_kernel, span),
         in_specs=[VMEM],
         out_shape=(
             jax.ShapeDtypeStruct((rows, cut), hidden.dtype),
@@ -86,6 +94,38 @@
         compiler_params=pltpu.CompilerParams(vmem_limit_bytes=4 << 20),
         name="split_columns",
     )(hidden)
+
+
+def weight_kernel(words_ref, scale_ref, head_ref, tail_ref):
+    cut = head_ref.shape[0]
+    words = words_ref[...].T
+    scale = scale_ref[...].astype(jnp.float32)
+    groups = scale.shape[0]
+    per = words.shape[0] // groups
+    for g in range(groups):
+        block = words[g * per : (g + 1) * per]
+        for k in range(8):
+            code = ((block << (28 - 4 * k)) >> 28).astype(jnp.float32)
+            value = (code * scale[g : g + 1]).astype(jnp.bfloat16)
+            row = (g * 8 + k) * per
+            if row < cut:
+                head_ref[row : row + per] = value
+            else:
+                tail_ref[row - cut : row - cut + per] = value
+
+
+def down_weight(words, scale, cut):
+    cols, rows = words.shape
+    return pl.pallas_call(
+        weight_kernel,
+        in_specs=[VMEM] * 2,
+        out_shape=(
+            jax.ShapeDtypeStruct((cut, cols), scale.dtype),
+            jax.ShapeDtypeStruct((8 * rows - cut, cols), scale.dtype),
+        ),
+        compiler_params=pltpu.CompilerParams(vmem_limit_bytes=12 << 20),
+        name="down_weight",
+    )(words, scale)
 
 
 def pack_kernel(targets_ref, loss_mask_ref, parts_ref, residual_ref, out_ref):
@@ -305,12 +345,13 @@
     per_x = held // n_x
 
     cut = gather_cut(toks, width, n_z)
-    head, tail = split_columns(hidden, cut, n_z)
+    head, tail = split_columns(hidden, cut, n_z, width // down_scale.shape[0])
     tail = exchange_ring(tail, "fsdp")
+    head_weight, tail_weight = down_weight(down_packed.T, down_scale, cut)
+    head, head_weight, tail_weight = lax.optimization_barrier((head, head_weight, tail_weight))
     head = gather_ring(head, "fsdp")
-    weight = dequant_down(down_packed, down_scale)
-    part = dot_f32(head.reshape(held, cut), weight[:cut], ((1,), (0,))) + dot_f32(
-        tail.reshape(held, width - cut), weight[cut:], ((1,), (0,))
+    part = dot_f32(head.reshape(held, cut), head_weight, ((1,), (0,))) + dot_f32(
+        tail.reshape(held, width - cut), tail_weight, ((1,), (0,))
     )
 
     part = jnp.swapaxes(part.reshape(n_z, toks, cols), 0, 1).reshape(n_x, per_x, cols)

time: 205 us -> 205 us (level)
  transfers between devices with their start and end apart: 3 -> 3, of which waited for: 0 -> 0; matrix products, arithmetic and copies ran while one was open for 4% -> 2% of each run, Pallas kernels for 0% -> 1%
where the time goes in v10:
time: 205 us; the launch traced here: 204 us
  blocking collectives  139 us (68%)
  starting transfers between devices  50.6 us (25%)
  Pallas kernels  6.1 us (3%)
  local copies, waits for them, and re-layouts  3.12 us (2%)
  other arithmetic  2.84 us (1%)
    all_gather x3, blocking collectives, gather_ring(): return lax.all_gather(value, (axis, 'sub'), axis_index_groups=rings(axis))  90.2 us
    all_to_all x2, starting transfers between devices, exchange_ring(): lax.all_to_all(copies, (axis, 'sub'), 0, 0, tiled=True, axis_index_groups...  48.3 us
    all_to_all x1, blocking collectives, copy_for_each(): lax.all_to_all(jnp.broadcast_to(value[None], (peers, *value.shape)), axis...  19.7 us
    all_to_all x1, blocking collectives, on_device(): parts = lax.all_to_all(part, 'mp', 0, 0, tiled=True)  16.3 us
    all_to_all x1, blocking collectives, on_device(): lax.all_to_all(packed, ('mp', 'sub'), 0, 0, tiled=True)  12.8 us
  transfers between devices with their start and end apart: 3, of which 0 were waited for; matrix products, arithmetic and copies ran while one was open for 2% of the time, Pallas kernels for 1%

profile of v10, /device:TPU:65, one launch (start us, length us, event | category | flops | bytes accessed | tf_op | source)
XLA Modules:
  0.0 204.0 jit_solution(8805665455636759228)
XLA Ops:
  0.6 0.0 copy-start.1
  0.6 0.9 copy-done.1
  1.5 0.8 split_columns.1
  2.4 44.7 %all-to-all-start = ((bf16[16,8,640]{2,1,0:T(8,128)(2,1)}), bf16[16,8,640]{2,1,0:T(8,128)(2,1)S(1)}, u32[]{:S(2)}, u32[]{:S(2)}) async-start(bf16[16,8,640]{2,1,0:T(8,128)(2,1)} %get-tuple-element.26), calls=%async_computation | async-start | bytes 327680 | tf_op jit(solution)/shard_map/all_to_all | solution.py:37
  47.1 0.0 copy-start
  47.1 1.1 copy-done
  48.2 0.0 copy-start.3
  48.2 0.8 copy-done.3
  48.9 1.2 down_weight.1
  50.1 35.1 %all-gather = bf16[128,3968]{1,0:T(8,128)(2,1)S(1)} all-gather(bf16[8,3968]{1,0:T(8,128)(2,1)S(1)} %get-tuple-element.23), channel_id=2, replica_groups={{0,17,32,49,64,81,96,113,128,145,160,177,192,209,224,241},{1,16,33,48,6..., dimensions={0}, use_global_device_ids=true | all-gather | bytes 1079296 | tf_op jit(solution)/shard_map/all_gather | solution.py:33
  85.2 0.0 copy-start.2
  85.3 0.0 copy-start.4
  85.3 0.0 copy-start.5
  85.3 0.0 copy-start.7
  85.3 0.0 copy-start.8
  85.3 1.2 fusion.5
  86.5 0.0 all-to-all-done
  86.5 0.3 fusion.3
  86.8 0.1 copy.12
  86.9 0.0 copy-start.6
  87.0 16.3 %all_to_all.25.parts_ref = f32[8,16,288]{2,1,0:T(8,128)S(1)} all-to-all(f32[8,16,288]{2,1,0:T(8,128)S(1)} %bitcast.31), channel_id=1, replica_groups=mesh['groups'=2,'fsdp'=16,'mp'=8,'sub'=2] {'mp'}, dimensions={0} | all-to-all | bytes 294912 | tf_op jit(solution)/shard_map/all_to_all | solution.py:358
  103.3 0.0 copy-done.2
  103.3 0.0 copy-done.4
  103.3 0.0 copy-done.5
  103.3 0.6 pack_rows.1
  104.0 28.4 %all-gather.1 = bf16[640,384]{1,0:T(8,128)(2,1)S(1)} all-gather(bf16[40,384]{1,0:T(8,128)(2,1)S(1)} %pack_rows.1), channel_id=3, replica_groups={{0,17,32,49,64,81,96,113,128,145,160,177,192,209,224,241},{1,16,33,48,6..., dimensions={0}, use_global_device_ids=true | all-gather | bytes 522240 | tf_op jit(solution)/shard_map/all_gather | solution.py:33
  132.4 0.0 copy-done.7
  132.4 0.0 copy-done.8
  132.4 1.2 norm_rows.1
  133.6 3.6 %all-to-all-start.2 = ((bf16[8,16,640]{2,1,0:T(8,128)(2,1)}), bf16[8,16,640]{2,1,0:T(8,128)(2,1)S(1)}, u32[]{:S(2)}, u32[]{:S(2)}) async-start(bf16[8,16,640]{2,1,0:T(8,128)(2,1)} %get-tuple-element.34), calls=%async_computation.2 | async-start | bytes 327680 | tf_op jit(solution)/shard_map/all_to_all | solution.py:37
  137.2 26.7 %all-gather.2 = bf16[128,3968]{1,0:T(8,128)(2,1)S(1)} all-gather(bf16[16,3968]{1,0:T(8,128)(2,1)S(1)} %get-tuple-element.33), channel_id=4, replica_groups={{0,3,4,7,8,11,12,15},{1,2,5,6,9,10,13,14},{16,19,20,23,24,27,28,31},{17..., dimensions={0}, use_global_device_ids=true | all-gather | bytes 1142784 | tf_op jit(solution)/shard_map/all_gather | solution.py:33
  163.9 0.0 all-to-all-done.2
  163.9 0.1 pad_maximum_fusion.refs_0_
  164.0 2.3 %collective-permute-start = (bf16[128,4736]{1,0:T(8,128)(2,1)S(1)}, bf16[128,4736]{1,0:T(8,128)(2,1)S(1)}, u32[]{:S(2)}, u32[]{:S(2)}) collective-permute-start(bf16[128,4736]{1,0:T(8,128)(2,1)S(1)} %pad_maximum_fusion.refs_0_), channel_id=1, source_target_pairs={{0,1},{1,0},{2,3},{3,2},{4,5},{5,4},{6,7},{7,6},{8,9},{9,8},{10,11... | collective-permute-start | bytes 3637256 | tf_op jit(solution)/shard_map/ppermute | solution.py:371
  166.4 0.1 shift_left.23
  166.5 0.1 shift_left.24
  166.5 0.0 copy-done.6
  166.5 2.7 %fusion.2 = bf16[512,4608]{0,1:T(8,128)(2,1)S(1)} fusion(s32[4608]{0:T(1024)S(1)} %shift_left.24, s32[512,576]{0,1:T(8,128)} %param.16, bf16[512,36]{0,1:T(8,128)(2,1)S(1)} %copy-done.6), kind=kLoop, calls=%fused_computation.3 | loop fusion | flops 16515072 | bytes 5953536 | tf_op jit(solution)/shard_map/mul | solution.py:56
  169.3 0.0 collective-permute-done.refs_1_
  169.3 1.6 vocab_sums.1
  170.9 12.8 %all_to_all.26 = f32[16,4,128]{2,1,0:T(4,128)S(1)} all-to-all(f32[16,4,128]{2,1,0:T(4,128)S(1)} %get-tuple-element.36), channel_id=1, replica_groups=mesh['groups'=2,'fsdp'=16,'mp'=8,'sub'=2] {'mp','sub'}, dimensions={0} | all-to-all | bytes 65536 | tf_op jit(solution)/shard_map/all_to_all | solution.py:375
  183.7 19.7 %all_to_all.27.packed_ref = f32[16,4,128]{2,1,0:T(4,128)S(1)} all-to-all(f32[16,4,128]{2,1,0:T(4,128)S(1)} %broadcast_in_dim.8), channel_id=1, replica_groups=mesh['groups'=2,'fsdp'=16,'mp'=8,'sub'=2] {'fsdp'}, dimensions={0} | all-to-all | bytes 65536 | tf_op jit(solution)/shard_map/all_to_all | solution.py:22
  203.3 0.7 losses_of.1
  (6 shorter events, 0.1 us)
Async XLA Ops:
  0.6 0.9 copy-start.1
  2.4 84.1 %all-to-all-start = ((bf16[16,8,640]{2,1,0:T(8,128)(2,1)}), bf16[16,8,640]{2,1,0:T(8,128)(2,1)S(1)}, u32[]{:S(2)}, u32[]{:S(2)}) async-start(bf16[16,8,640]{2,1,0:T(8,128)(2,1)} %get-tuple-element.26), calls=%async_computation | async-start | bytes 327680 | tf_op jit(solution)/shard_map/all_to_all | solution.py:37
  47.1 1.1 copy-start
  48.2 0.8 copy-start.3
  85.2 18.1 %copy-start.2 = (bf16[8,4608]{1,0:T(8,128)(2,1)S(1)}, bf16[8,4608]{1,0:T(8,128)(2,1)}, u32[]{:S(2)}) copy-start(bf16[8,4608]{1,0:T(8,128)(2,1)} %residual_ref) | copy-start | bytes 221188
  85.3 18.1 %copy-start.4 = (s32[8]{0:T(128)S(1)}, s32[8]{0:T(128)}, u32[]{:S(2)}) copy-start(s32[8]{0:T(128)} %targets_ref) | copy-start | bytes 100
  85.3 18.1 %copy-start.5 = (s32[8]{0:T(128)S(1)}, s32[8]{0:T(128)}, u32[]{:S(2)}) copy-start(s32[8]{0:T(128)} %loss_mask_ref.1) | copy-start | bytes 100
  85.3 47.1 %copy-start.7 = (f32[4608]{0:T(1024)S(1)}, f32[4608]{0:T(1024)}, u32[]{:S(2)}) copy-start(f32[4608]{0:T(1024)} %param.14) | copy-start | bytes 55300
  85.3 47.1 %copy-start.8 = (f32[4608]{0:T(1024)S(1)}, f32[4608]{0:T(1024)}, u32[]{:S(2)}) copy-start(f32[4608]{0:T(1024)} %param.15) | copy-start | bytes 55300
  86.9 79.6 %copy-start.6 = (bf16[512,36]{0,1:T(8,128)(2,1)S(1)}, bf16[512,36]{0,1:T(8,128)(2,1)}, u32[]{:S(2)}) copy-start(bf16[512,36]{0,1:T(8,128)(2,1)} %param.17) | copy-start | bytes 110596
  133.6 30.3 %all-to-all-start.2 = ((bf16[8,16,640]{2,1,0:T(8,128)(2,1)}), bf16[8,16,640]{2,1,0:T(8,128)(2,1)S(1)}, u32[]{:S(2)}, u32[]{:S(2)}) async-start(bf16[8,16,640]{2,1,0:T(8,128)(2,1)} %get-tuple-element.34), calls=%async_computation.2 | async-start | bytes 327680 | tf_op jit(solution)/shard_map/all_to_all | solution.py:37
  164.0 5.2 %collective-permute-start = (bf16[128,4736]{1,0:T(8,128)(2,1)S(1)}, bf16[128,4736]{1,0:T(8,128)(2,1)S(1)}, u32[]{:S(2)}, u32[]{:S(2)}) collective-permute-start(bf16[128,4736]{1,0:T(8,128)(2,1)S(1)} %pad_maximum_fusion.refs_0_), channel_id=1, source_target_pairs={{0,1},{1,0},{2,3},{3,2},{4,5},{5,4},{6,7},{7,6},{8,9},{9,8},{10,11... | collective-permute-start | bytes 3637256 | tf_op jit(solution)/shard_map/ppermute | solution.py:371
